TPU v7x, 512 devices: a whole 4x8x8 slice. The times are simulated.
512 devices in a mesh: lat: 8 (over y), lon: 32 (over x, z_hi, core), lev: 2 (over z_lo).
Axes of the slice: x: 4, y: 8, z: 8 (z_hi: 4, z_lo: 2; z = z_hi * 2 + z_lo), core: 2. Of those that a mesh axis runs over, the one named last changes fastest.
Arguments:
- tokens: bfloat16 [4, 48, 384, 192], P('lev', 'lat', 'lon'), may hold values from -6 to 6
- norm1_gain: float32 [192], replicated, may hold values from 0.8 to 10
- qkv_weight: bfloat16 [192, 576], replicated, may hold values from -0.4375 to 0.4375
- proj_weight: bfloat16 [192, 192], replicated, may hold values from -0.4375 to 0.4375
- earth_bias: bfloat16 [2, 8, 6, 3312], P(None, 'lat'), may hold values from -4 to 4
- norm2_gain: float32 [192], replicated, may hold values from 0.5 to 1.5
- fc1_weight: bfloat16 [192, 768], replicated, may hold values from -0.4375 to 0.4375
- fc2_weight: bfloat16 [768, 192], replicated, may hold values from -0.21875 to 0.21875
Outputs:
- blended: bfloat16 [4, 48, 384, 192], P('lev', 'lat', 'lon')
All inputs are finite; a program needn't handle non-finite values.
Results may differ from a plain program's by a relative error of at most 0.008.
The roundings to bfloat16 on the way count: a program that leaves them out, or rounds other values in their place, can miss the bound.
Values may be sent and summed in bfloat16 or wider, within the bound.
No kernel may reach another device: no remote copies, remote signals or barrier semaphores. Data moves between devices by JAX's collectives and lax.ppermute only.
A program may use at most 64 MiB of HBM per device.

v0:
```python
import jax
import jax.numpy as jnp
from jax import lax
from jax.sharding import PartitionSpec as P

HEADS = 6
WLV = 2
WLA = 6
WLO = 12


norm_eps = 1e-05


def padded(x, sides, width):
    for axis, dim in sides:
        size, length = (lax.axis_size(axis), x.shape[dim])
        up = [(i, (i + 1) % size) for i in range(size - 1)]
        down = [(j, i) for i, j in up]
        last = lax.slice_in_dim(x, length - width, length, axis=dim)
        first = lax.slice_in_dim(x, 0, width, axis=dim)
        before = lax.ppermute(last, axis, up)
        after = lax.ppermute(first, axis, down)
        x = jnp.concatenate([before, x, after], axis=dim)
    return x


def from_behind(block, axis, distance):
    devices = range(lax.axis_size(axis))
    route = [((i - distance) % len(devices), i) for i in devices]
    return lax.ppermute(block, axis, route)


def layer_norm(values, scale_gain):
    average = jnp.mean(values, axis=-1, keepdims=True)
    centered = values - average
    variance = jnp.mean(centered * centered, axis=-1, keepdims=True)
    return centered * lax.rsqrt(variance + norm_eps) * scale_gain


def window_coords():
    places = jnp.arange(WLV * WLA * WLO, dtype=jnp.int32)
    return (places // (WLA * WLO), places // WLO % WLA, places % WLO)


def bias_index():
    lev_place, lat_place, lon_place = window_coords()
    paired = (lev_place[:, None] * WLV + lev_place[None, :]) * WLA + lat_place[:, None]
    paired = paired * WLA + lat_place[None, :]
    return paired * (2 * WLO - 1) + lon_place[:, None] - lon_place[None, :] + WLO - 1


def region_of(places, extent, window):
    return jnp.where(
        places < extent - window, 0, jnp.where(places < extent - window // 2, 1, 2)
    ).astype(jnp.int32)


def attend_windows(windows, qkv_weight, bias_terms, allowed):
    lat_windows, lon_windows, window_size, feature_width = windows.shape
    head_dim = feature_width // HEADS
    projected = jnp.dot(
        windows.reshape(-1, feature_width), qkv_weight, preferred_element_type=jnp.float32
    )
    projected = projected.astype(jnp.bfloat16).reshape(
        lat_windows, lon_windows, window_size, 3, HEADS, head_dim
    )
    queries = projected[:, :, :, 0]
    key_rows = projected[:, :, :, 1]
    value_rows = projected[:, :, :, 2]
    scores = jnp.einsum("abqhd,abkhd->abhqk", queries, key_rows, preferred_element_type=jnp.float32)
    scores = scores * head_dim ** (-0.5) + bias_terms[:, None].astype(jnp.float32)
    scores = jnp.where(allowed[:, None, None], scores, -1e30)
    row_max = jnp.max(scores, axis=-1, keepdims=True)
    weights = jnp.exp(scores - row_max)
    probs = (weights / jnp.sum(weights, axis=-1, keepdims=True)).astype(jnp.bfloat16)
    context = jnp.einsum(
        "abhqk,abkhd->abqhd", probs, value_rows, preferred_element_type=jnp.float32
    )
    return context.astype(jnp.bfloat16).reshape(
        lat_windows, lon_windows, window_size, feature_width
    )


def rim_levlat(blocks):
    lev_cells, lat_cells, lon_cells, feature_width = blocks.shape
    grouped = blocks.reshape(lev_cells, lat_cells // (WLA // 2), WLA // 2, lon_cells, feature_width)
    widened = padded(grouped, (("lev", 0), ("lat", 1)), 1)
    return widened.reshape(lev_cells + WLV, lat_cells + WLA, lon_cells, feature_width)


def along_lon(blocks):
    ahead = from_behind(blocks[:, :, : WLO // 2], "lon", -1)
    widened = jnp.concatenate([blocks[:, :, WLO // 2 :], ahead], axis=2)
    return widened


def per_device(
    tokens, norm1_gain, qkv_weight, proj_weight, earth_bias, norm2_gain, fc1_weight, fc2_weight
):
    lev_cells, lat_cells, lon_cells, feature_width = tokens.shape
    half_lev, half_lat, half_lon = (WLV // 2, WLA // 2, WLO // 2)
    total_lev = lev_cells * lax.axis_size("lev")
    total_lat = lat_cells * lax.axis_size("lat")
    lev_start = lax.axis_index("lev") * lev_cells
    lat_start = lax.axis_index("lat") * lat_cells
    lev_types = total_lev // WLV
    window_size = WLV * WLA * WLO
    normed = layer_norm(tokens.astype(jnp.float32), norm1_gain).astype(jnp.bfloat16)
    extended = along_lon(rim_levlat(normed))
    edge_tables = from_behind(earth_bias, "lat", 1)
    all_tables = jnp.concatenate([edge_tables, earth_bias], axis=1)
    table_index = bias_index()
    lev_place, lat_place, lon_place = window_coords()
    lat_windows = (lat_cells + WLA) // WLA
    ext_columns = extended.shape[2]
    lon_windows = ext_columns // WLO
    lat_rolled = jnp.mod(
        lat_start
        - WLA
        + jnp.arange(lat_windows, dtype=jnp.int32)[:, None] * WLA
        + lat_place[None, :],
        total_lat,
    )
    lat_region = region_of(lat_rolled, total_lat, WLA)
    lat_allowed = lat_region[:, :, None] == lat_region[:, None, :]
    pieces = []
    for lev_window in range(lev_cells // WLV + 1):
        slab = extended[lev_window * WLV : (lev_window + 1) * WLV]
        windows = slab.reshape(WLV, lat_windows, WLA, lon_windows, WLO, feature_width).transpose(
            1, 3, 0, 2, 4, 5
        )
        windows = windows.reshape(lat_windows, lon_windows, window_size, feature_width)
        lev_type = jnp.mod(lev_start // WLV - 1 + lev_window, lev_types)
        lev_tables = jnp.take(all_tables, lev_type, axis=0)
        bias_terms = jnp.take(lev_tables, table_index, axis=2)
        lev_rolled = jnp.mod(lev_start - WLV + lev_window * WLV + lev_place, total_lev)
        lev_region = region_of(lev_rolled, total_lev, WLV)
        allowed = lat_allowed & (lev_region[:, None] == lev_region[None, :])[None]
        context = attend_windows(windows, qkv_weight, bias_terms, allowed)
        context = context.reshape(lat_windows, lon_windows, WLV, WLA, WLO, feature_width).transpose(
            2, 0, 3, 1, 4, 5
        )
        pieces.append(context.reshape(WLV, lat_windows * WLA, ext_columns, feature_width))
    inner = jnp.concatenate(pieces, axis=0)[
        half_lev : half_lev + lev_cells, half_lat : half_lat + lat_cells
    ]
    behind = from_behind(inner[:, :, -half_lon:], "lon", 1)
    context_own = jnp.concatenate([behind, inner[:, :, :-half_lon]], axis=2)
    first = tokens.reshape(-1, feature_width).astype(jnp.float32) + jnp.dot(
        context_own.reshape(-1, feature_width), proj_weight, preferred_element_type=jnp.float32
    )
    normed_two = layer_norm(first, norm2_gain).astype(jnp.bfloat16)
    hidden = jax.nn.gelu(
        jnp.dot(normed_two, fc1_weight, preferred_element_type=jnp.float32), approximate=False
    ).astype(jnp.bfloat16)
    result = first + jnp.dot(hidden, fc2_weight, preferred_element_type=jnp.float32)
    return result.astype(jnp.bfloat16).reshape(tokens.shape)


def solution(mesh):
    placed = (
        P("lev", "lat", "lon", None),
        P(),
        P(),
        P(),
        P(None, "lat", None, None),
        P(),
        P(),
        P(),
    )
    return jax.shard_map(
        per_device,
        mesh=mesh,
        in_specs=placed,
        out_specs=P("lev", "lat", "lon", None),
        check_vma=False,
    )
```

profile of v0, /device:TPU:24, one launch (start us, length us, event | category | flops | bytes accessed | tf_op | source)
XLA Modules:
  0.0 229.5 jit_solution(8898718136321923199)
XLA Ops:
  0.0 4.8 %collective-permute-start.5 = (bf16[2,1,6,3312]{3,0,2,1:T(2,128)(2,1)}, bf16[2,1,6,3312]{3,0,2,1:T(2,128)(2,1)S(1)}, u32[]{:S(2)}, u32[]{:S(2)}) collective-permute-start(bf16[2,1,6,3312]{3,0,2,1:T(2,128)(2,1)} %param.16), channel_id=1, source_target_pairs={{448,0},{0,64},{64,128},{128,192},{192,256},{256,320},{320,384},{3... | collective-permute-start | bytes 238472 | tf_op jit(solution)/shard_map/ppermute | solution.py:31
  4.8 1.0 convert_reduce_fusion
  5.8 1.1 multiply_reduce_fusion
  6.9 1.0 multiply_convert_fusion
  8.0 4.3 %collective-permute-start = (bf16[1,2,3,12,192]{4,3,2,1,0:T(8,128)(2,1)S(1)}, bf16[1,2,3,12,192]{4,3,2,1,0:T(8,128)(2,1)S(1)}, u32[]{:S(2)}, u32[]{:S(2)}) collective-permute-start(bf16[1,2,3,12,192]{4,3,2,1,0:T(8,128)(2,1)S(1)} %bitcast.122), channel_id=1, source_target_pairs={{0,1},{2,3},{4,5},{6,7},{8,9},{10,11},{12,13},{14,15},{16,17},{18,... | collective-permute-start | bytes 82952 | tf_op jit(solution)/shard_map/ppermute | solution.py:22
  12.2 1.3 collective-permute-start.1
  13.6 0.1 compare_select_fusion
  14.2 0.8 compare_and_fusion.1
  15.0 0.2 compare_and_fusion.2
  15.4 2.9 %collective-permute-done.1 = bf16[1,2,3,12,192]{4,3,2,1,0:T(8,128)(2,1)S(1)} collective-permute-done((bf16[1,2,3,12,192]{4,3,2,1,0:T(8,128)(2,1)S(1)}, bf16[1,2,3,12,192]{4,3,2,1,0:T(8,128)(2,1)S(1)}, u32[]{:S(2)}, u32[]{:S(2)}) %collective-permute-start.1) | collective-permute-done | bytes 27680 | tf_op jit(solution)/shard_map/ppermute | solution.py:23
  18.3 2.6 %collective-permute-start.2 = (bf16[4,1,3,12,192]{4,3,2,1,0:T(8,128)(2,1)S(1)}, bf16[4,1,3,12,192]{4,3,2,1,0:T(8,128)(2,1)S(1)}, u32[]{:S(2)}, u32[]{:S(2)}) collective-permute-start(bf16[4,1,3,12,192]{4,3,2,1,0:T(8,128)(2,1)S(1)} %get-tuple-element.28), channel_id=1, source_target_pairs={{0,64},{64,128},{128,192},{192,256},{256,320},{320,384},{384,448},... | collective-permute-start | bytes 165896 | tf_op jit(solution)/shard_map/ppermute | solution.py:22
  20.9 3.3 %collective-permute-start.3 = (bf16[4,1,3,12,192]{4,3,2,1,0:T(8,128)(2,1)S(1)}, bf16[4,1,3,12,192]{4,3,2,1,0:T(8,128)(2,1)S(1)}, u32[]{:S(2)}, u32[]{:S(2)}) collective-permute-start(bf16[4,1,3,12,192]{4,3,2,1,0:T(8,128)(2,1)S(1)} %get-tuple-element.29), channel_id=1, source_target_pairs={{64,0},{128,64},{192,128},{256,192},{320,256},{384,320},{448,384},... | collective-permute-start | bytes 165896 | tf_op jit(solution)/shard_map/ppermute | solution.py:23
  24.3 0.5 collective-permute-done.2
  24.8 3.8 %collective-permute-done.3 = bf16[4,1,3,12,192]{4,3,2,1,0:T(8,128)(2,1)S(1)} collective-permute-done((bf16[4,1,3,12,192]{4,3,2,1,0:T(8,128)(2,1)S(1)}, bf16[4,1,3,12,192]{4,3,2,1,0:T(8,128)(2,1)S(1)}, u32[]{:S(2)}, u32[]{:S(2)}) %collective-permute-start.3) | collective-permute-done | bytes 55328 | tf_op jit(solution)/shard_map/ppermute | solution.py:23
  28.7 0.2 copy.49
  29.0 0.8 fusion.101
  29.8 8.5 %collective-permute-start.4 = (bf16[4,12,6,192]{3,0,2,1:T(4,128)(2,1)}, bf16[4,12,6,192]{3,0,2,1:T(4,128)(2,1)}, u32[]{:S(2)}, u32[]{:S(2)}) collective-permute-start(bf16[4,12,6,192]{3,0,2,1:T(4,128)(2,1)} %get-tuple-element.27), channel_id=1, source_target_pairs={{2,0},{4,2},{6,4},{8,6},{10,8},{12,10},{14,12},{16,14},{18,16},{20... | collective-permute-start | bytes 331784 | tf_op jit(solution)/shard_map/ppermute | solution.py:31
  38.3 0.4 broadcast_select_fusion.1
  38.7 2.4 %copy.80 = bf16[1,2,6,3312]{2,1,3,0:T(2,128)(2,1)S(1)} copy(bf16[1,2,6,3312]{3,0,2,1:T(2,128)(2,1)S(1)} %get-tuple-element.30) | data formatting | bytes 158976 | tf_op jit(solution)/shard_map/jit(_take)/select_n | solution.py:135
  41.1 51.3 %gather_fusion = bf16[20736,2,6]{2,1,0:T(2,128)(2,1)} fusion(bf16[2,6,3312]{1,0,2:T(2,128)(2,1)S(1)} %bitcast.109, s32[21504]{0:T(1024)S(1)} %pad_clamp_fusion), kind=kCustom, calls=%fused_computation.clone | custom fusion | bytes 1078272 | tf_op jit(solution)/shard_map/jit(_take)/gather | solution.py:136
  92.4 27.8 %copy.59 = bf16[144,144,2,6]{0,1,3,2:T(8,128)(2,1)S(1)} copy(bf16[144,144,2,6]{3,2,1,0:T(2,128)(2,1)} %bitcast.107) | data formatting | bytes 995328 | tf_op jit(solution)/shard_map/jit(_take)/gather | solution.py:136
  120.2 2.4 %copy.83 = bf16[1,2,6,3312]{2,1,3,0:T(2,128)(2,1)S(1)} copy(bf16[1,2,6,3312]{3,0,2,1:T(2,128)(2,1)S(1)} %get-tuple-element.31) | data formatting | bytes 158976 | tf_op jit(solution)/shard_map/jit(_take)/select_n | solution.py:135
  122.5 51.3 %gather_fusion.1 = bf16[20736,2,6]{2,1,0:T(2,128)(2,1)} fusion(bf16[2,6,3312]{1,0,2:T(2,128)(2,1)S(1)} %bitcast.108, s32[21504]{0:T(1024)S(1)} %pad_clamp_fusion), kind=kCustom, calls=%fused_computation.1.clone | custom fusion | bytes 1078272 | tf_op jit(solution)/shard_map/jit(_take)/gather | solution.py:136
  173.8 27.8 %copy.72 = bf16[144,144,2,6]{0,1,3,2:T(8,128)(2,1)S(1)} copy(bf16[144,144,2,6]{3,2,1,0:T(2,128)(2,1)} %bitcast.106) | data formatting | bytes 995328 | tf_op jit(solution)/shard_map/jit(_take)/gather | solution.py:136
  201.6 2.0 fusion.46
  203.7 0.3 convolution_convert_fusion.1
  204.0 0.2 copy.51
  204.2 0.2 reshape.426
  204.5 0.5 fusion.99
  205.0 3.1 %fusion.105 = (f32[2,6,144]{2,1,0:T(8,128)S(1)}, f32[2,6,144,144]{2,3,1,0:T(8,128)}) fusion(bf16[144,144,2,6]{0,1,3,2:T(8,128)(2,1)S(1)} %copy.59, pred[144,144]{0,1:T(8,128)(4,1)S(1)} %copy.55, pred[2,144,144]{1,2,0:T(8,128)(4,1)} %get-tuple-element.34, bf16[2,1,144,1,6,32]{2,0,5,4,3,1:T(2,128)(2,1)S(1)} %get-tuple-element.20, ...), kind=kOutput, calls=%fused_computation.182 | convolution fusion | flops 17667216 | bytes 1783296 | tf_op jit(solution)/shard_map/sub | solution.py:75
  208.1 1.7 fusion.2
  209.8 0.5 copy.61
  210.3 0.4 reshape_reshape.13
  210.9 0.3 convolution_convert_fusion
  211.2 0.2 copy.64
  211.4 0.2 reshape.432
  211.7 0.5 fusion.100
  212.2 2.2 fusion.104
  214.4 1.7 fusion.3
  216.1 0.5 copy.74
  216.6 0.4 reshape_reshape.15
  217.2 1.9 collective-permute-start.6
  219.2 7.5 %collective-permute-done.6 = bf16[2,6,6,192]{3,0,2,1:T(2,128)(2,1)S(1)} collective-permute-done((bf16[2,6,6,192]{3,0,2,1:T(2,128)(2,1)S(1)}, bf16[2,6,6,192]{3,0,2,1:T(2,128)(2,1)S(1)}, u32[]{:S(2)}, u32[]{:S(2)}) %collective-permute-start.6) | collective-permute-done | bytes 27680 | tf_op jit(solution)/shard_map/ppermute | solution.py:31
  226.7 0.1 fusion.48
  227.0 0.3 fusion.106
  227.2 0.2 multiply_reduce_fusion.1
  227.5 1.3 fusion.4
  228.8 0.7 copy.77
  (55 shorter events, 1.6 us)
Async XLA Ops:
  0.0 227.5 %copy-start = (bf16[768,192]{0,1:T(8,128)(2,1)S(1)}, bf16[768,192]{0,1:T(8,128)(2,1)}, u32[]{:S(2)}) copy-start(bf16[768,192]{0,1:T(8,128)(2,1)} %param.19) | copy-start | bytes 884740
  0.0 24.2 %copy-start.6 = (bf16[2,1,6,3312]{3,0,2,1:T(2,128)(2,1)S(1)}, bf16[2,1,6,3312]{3,0,2,1:T(2,128)(2,1)}, u32[]{:S(2)}) copy-start(bf16[2,1,6,3312]{3,0,2,1:T(2,128)(2,1)} %param.16) | copy-start | bytes 238468
  0.0 24.2 %collective-permute-start.5 = (bf16[2,1,6,3312]{3,0,2,1:T(2,128)(2,1)}, bf16[2,1,6,3312]{3,0,2,1:T(2,128)(2,1)S(1)}, u32[]{:S(2)}, u32[]{:S(2)}) collective-permute-start(bf16[2,1,6,3312]{3,0,2,1:T(2,128)(2,1)} %param.16), channel_id=1, source_target_pairs={{448,0},{0,64},{64,128},{128,192},{192,256},{256,320},{320,384},{3... | collective-permute-start | bytes 238472 | tf_op jit(solution)/shard_map/ppermute | solution.py:31
  8.0 7.4 %collective-permute-start = (bf16[1,2,3,12,192]{4,3,2,1,0:T(8,128)(2,1)S(1)}, bf16[1,2,3,12,192]{4,3,2,1,0:T(8,128)(2,1)S(1)}, u32[]{:S(2)}, u32[]{:S(2)}) collective-permute-start(bf16[1,2,3,12,192]{4,3,2,1,0:T(8,128)(2,1)S(1)} %bitcast.122), channel_id=1, source_target_pairs={{0,1},{2,3},{4,5},{6,7},{8,9},{10,11},{12,13},{14,15},{16,17},{18,... | collective-permute-start | bytes 82952 | tf_op jit(solution)/shard_map/ppermute | solution.py:22
  12.2 6.0 %collective-permute-start.1 = (bf16[1,2,3,12,192]{4,3,2,1,0:T(8,128)(2,1)S(1)}, bf16[1,2,3,12,192]{4,3,2,1,0:T(8,128)(2,1)S(1)}, u32[]{:S(2)}, u32[]{:S(2)}) collective-permute-start(bf16[1,2,3,12,192]{4,3,2,1,0:T(8,128)(2,1)S(1)} %bitcast.121), channel_id=1, source_target_pairs={{1,0},{3,2},{5,4},{7,6},{9,8},{11,10},{13,12},{15,14},{17,16},{19,... | collective-permute-start | bytes 82952 | tf_op jit(solution)/shard_map/ppermute | solution.py:23
  18.3 6.5 %collective-permute-start.2 = (bf16[4,1,3,12,192]{4,3,2,1,0:T(8,128)(2,1)S(1)}, bf16[4,1,3,12,192]{4,3,2,1,0:T(8,128)(2,1)S(1)}, u32[]{:S(2)}, u32[]{:S(2)}) collective-permute-start(bf16[4,1,3,12,192]{4,3,2,1,0:T(8,128)(2,1)S(1)} %get-tuple-element.28), channel_id=1, source_target_pairs={{0,64},{64,128},{128,192},{192,256},{256,320},{320,384},{384,448},... | collective-permute-start | bytes 165896 | tf_op jit(solution)/shard_map/ppermute | solution.py:22
  20.9 7.7 %collective-permute-start.3 = (bf16[4,1,3,12,192]{4,3,2,1,0:T(8,128)(2,1)S(1)}, bf16[4,1,3,12,192]{4,3,2,1,0:T(8,128)(2,1)S(1)}, u32[]{:S(2)}, u32[]{:S(2)}) collective-permute-start(bf16[4,1,3,12,192]{4,3,2,1,0:T(8,128)(2,1)S(1)} %get-tuple-element.29), channel_id=1, source_target_pairs={{64,0},{128,64},{192,128},{256,192},{320,256},{384,320},{448,384},... | collective-permute-start | bytes 165896 | tf_op jit(solution)/shard_map/ppermute | solution.py:23
  29.8 171.9 %collective-permute-start.4 = (bf16[4,12,6,192]{3,0,2,1:T(4,128)(2,1)}, bf16[4,12,6,192]{3,0,2,1:T(4,128)(2,1)}, u32[]{:S(2)}, u32[]{:S(2)}) collective-permute-start(bf16[4,12,6,192]{3,0,2,1:T(4,128)(2,1)} %get-tuple-element.27), channel_id=1, source_target_pairs={{2,0},{4,2},{6,4},{8,6},{10,8},{12,10},{14,12},{16,14},{18,16},{20... | collective-permute-start | bytes 331784 | tf_op jit(solution)/shard_map/ppermute | solution.py:31
  173.8 27.9 %copy-start.4 = (bf16[4,12,6,192]{3,0,2,1:T(4,128)(2,1)S(1)}, bf16[4,12,6,192]{3,0,2,1:T(4,128)(2,1)}, u32[]{:S(2)}) copy-start(bf16[4,12,6,192]{3,0,2,1:T(4,128)(2,1)} %get-tuple-element.26) | copy-start | bytes 331780
  173.8 29.9 %copy-start.2 = (bf16[192,576]{1,0:T(8,128)(2,1)S(1)}, bf16[192,576]{1,0:T(8,128)(2,1)}, u32[]{:S(2)}) copy-start(bf16[192,576]{1,0:T(8,128)(2,1)} %param.14) | copy-start | bytes 663556
  209.8 1.0 copy-start.3
  210.9 1.3 copy-start.7
  216.1 3.1 %copy-start.1 = (bf16[2,6,12,192]{3,0,2,1:T(2,128)(2,1)S(1)}, bf16[2,6,12,192]{3,0,2,1:T(2,128)(2,1)}, u32[]{:S(2)}) copy-start(bf16[2,6,12,192]{3,0,2,1:T(2,128)(2,1)} %param.12) | copy-start | bytes 165892
  216.1 10.9 %copy-start.5 = (bf16[192,192]{1,0:T(8,128)(2,1)S(1)}, bf16[192,192]{1,0:T(8,128)(2,1)}, u32[]{:S(2)}) copy-start(bf16[192,192]{1,0:T(8,128)(2,1)} %param.15) | copy-start | bytes 221188
  216.6 10.9 %copy-start.8 = (bf16[192,768]{1,0:T(8,128)(2,1)S(1)}, bf16[192,768]{1,0:T(8,128)(2,1)}, u32[]{:S(2)}) copy-start(bf16[192,768]{1,0:T(8,128)(2,1)} %param.18) | copy-start | bytes 884740
  216.6 10.9 %copy-start.9 = (f32[192]{0:T(256)S(1)}, f32[192]{0:T(256)}, u32[]{:S(2)}) copy-start(f32[192]{0:T(256)} %param.17) | copy-start | bytes 2308
  217.2 9.5 %collective-permute-start.6 = (bf16[2,6,6,192]{3,0,2,1:T(2,128)(2,1)S(1)}, bf16[2,6,6,192]{3,0,2,1:T(2,128)(2,1)S(1)}, u32[]{:S(2)}, u32[]{:S(2)}) collective-permute-start(bf16[2,6,6,192]{3,0,2,1:T(2,128)(2,1)S(1)} %pad_maximum_fusion.4), channel_id=1, source_target_pairs={{62,0},{0,2},{2,4},{4,6},{6,8},{8,10},{10,12},{12,14},{14,16},{16,... | collective-permute-start | bytes 82952 | tf_op jit(solution)/shard_map/ppermute | solution.py:31
where the time goes:
time: 231 us; the launch traced here: 230 us
  local copies, waits for them, and re-layouts  169 us (73%)
  starting transfers between devices  26.7 us (12%)
  waiting for transfers between devices  14.7 us (6%)
  matrix products  10.8 us (5%)
  other arithmetic  7.49 us (3%)
    gather x4, local copies, waits for them, and re-layouts, per_device(): bias_terms = jnp.take(lev_tables, table_index, axis=2)  158 us
    ppermute x3, starting transfers between devices, from_behind(): return lax.ppermute(block, axis, route)  15.3 us
    ppermute x3, waiting for transfers between devices, from_behind(): return lax.ppermute(block, axis, route)  7.51 us
    ppermute x2, starting transfers between devices, padded(): before = lax.ppermute(last, axis, up)  6.86 us
    ppermute x2, waiting for transfers between devices, padded(): after = lax.ppermute(first, axis, down)  6.67 us
    sub x2, matrix products, attend_windows(): weights = jnp.exp(scores - row_max)  5.24 us
    select_n x2, local copies, waits for them, and re-layouts, per_device(): lev_tables = jnp.take(all_tables, lev_type, axis=0)  4.7 us
  transfers between devices with their start and end apart: 7, of which 4 were waited for; matrix products, arithmetic and copies ran while one was open for 73% of the time, Pallas kernels for 0%

commit v1 on v0

v1 whole, which is shorter than its diff:
```python
import numpy as np
import jax
import jax.numpy as jnp
from jax import lax
from jax.experimental import pallas as pl
from jax.experimental.pallas import tpu as pltpu
from jax.sharding import PartitionSpec as P

D = 192
HEADS = 6
HEAD_DIM = 32
WLA = 6
WLO = 12
HLA = 3
HLO = 6
SPAN = 2 * WLO - 1
ROWS = 288
HALF = 144
QROWS = 288
GROUP = 24
FAR = -1e30

norm_eps = 1e-05


def constants():
    column = np.arange(24)
    place = np.arange(WLA)
    spread = np.zeros((WLO, WLA * SPAN, HALF), np.float32)
    for o in range(WLO):
        for k in column:
            d = o - k + 17
            if (o < HLO) == (k < WLO):
                spread[o, place * SPAN + d, place * 24 + k] = 1
    pick = np.zeros((2, QROWS, HALF), np.float32)
    back = np.zeros((72, 2 * QROWS), np.float32)
    owned = np.zeros((QROWS, D), np.float32)
    for o in range(WLO):
        for h in range(HEADS):
            for a in range(4):
                row = o * GROUP + h * 4 + a
                owned[row, h * HEAD_DIM : (h + 1) * HEAD_DIM] = 1
                if a < HLA:
                    pick[0, row, (HLA + a) * 24 + HLO + o] = 1
                    pick[1, row, a * 24 + HLO + o] = 1
                    back[a * WLO + o, row] = 1
                    back[(HLA + a) * WLO + o, QROWS + row] = 1
    side = (np.arange(HALF) % 24 >= WLO).astype(np.float32).reshape(1, HALF)
    return spread, pick, back, owned, side


def normalized(values, gain):
    average = jnp.mean(values, axis=-1, keepdims=True)
    centered = values - average
    variance = jnp.mean(centered * centered, axis=-1, keepdims=True)
    return centered * lax.rsqrt(variance + norm_eps) * gain


def dot(a, b):
    return jnp.dot(a, b, preferred_element_type=jnp.float32)


def dot_t(a, b):
    return lax.dot_general(a, b, (((1,), (1,)), ((), ())), preferred_element_type=jnp.float32)


def block_kernel(
    where_ref,
    wide_ref,
    other_ref,
    own_ref,
    table_ref,
    gain1_ref,
    qkv_ref,
    proj_ref,
    gain2_ref,
    fc1_ref,
    fc2_ref,
    spread_ref,
    pick_ref,
    back_ref,
    owned_ref,
    side_ref,
    out_ref,
):
    lev = where_ref[0]
    lat = where_ref[1]
    lat_last = where_ref[2]
    gain1 = gain1_ref[...]
    w_q = qkv_ref[:, :D]
    w_k = qkv_ref[:, D : 2 * D]
    w_v = qkv_ref[:, 2 * D :]

    def normed(rows):
        return normalized(rows.astype(jnp.float32), gain1).astype(jnp.bfloat16)

    n_alone = normed(wide_ref[lev])
    n_pair = normed(wide_ref[1 - lev])
    n_other = normed(other_ref[...])

    table = table_ref[...]
    spreads = [dot(table, spread_ref[o]) for o in range(WLO)]
    row_half = lax.broadcasted_iota(jnp.int32, (QROWS, HALF), 0) >= QROWS // 2
    lane = lax.broadcasted_iota(jnp.int32, (QROWS, HALF), 1)
    side = jnp.broadcast_to(side_ref[...], (QROWS, HALF)) > 0.5
    same_side = row_half == side

    def bias_of(lat_window, entry, allowed):
        at = (lat_window * 3 + entry) * GROUP
        terms = jnp.concatenate([s[at : at + GROUP] for s in spreads], axis=0)
        return jnp.where(allowed, terms, FAR)

    owned = owned_ref[...]
    scale = HEAD_DIM**-0.5

    def level(n_self, n_extra, entries):
        queries = dot(n_self, w_q).astype(jnp.bfloat16)
        sources = [n_self] if n_extra is None else [n_self, n_extra]
        keys = [dot(n, w_k).astype(jnp.bfloat16) for n in sources]
        values = [dot(n, w_v).astype(jnp.bfloat16) for n in sources]
        parts = []
        for lat_window in range(2):
            rows = slice(lat_window * HALF, (lat_window + 1) * HALF)
            if lat_window == 0:
                near = (lane >= 72) | (lat > 0)
            else:
                near = (lane < 72) | (lat < lat_last)
            allowed = same_side & near
            spread_q = dot(pick_ref[lat_window], queries[rows]).astype(jnp.bfloat16) * owned
            scores = [
                dot_t(spread_q, k[rows]) * scale + bias_of(lat_window, e, allowed)
                for k, e in zip(keys, entries)
            ]
            top = jnp.max(scores[0], axis=-1, keepdims=True)
            for s in scores[1:]:
                top = jnp.maximum(top, jnp.max(s, axis=-1, keepdims=True))
            weights = [jnp.exp(s - top) for s in scores]
            total = jnp.sum(weights[0], axis=-1, keepdims=True)
            for w in weights[1:]:
                total = total + jnp.sum(w, axis=-1, keepdims=True)
            inverse = 1.0 / total
            context = 0.0
            for w, v in zip(weights, values):
                context = context + dot((w * inverse).astype(jnp.bfloat16), v[rows])
            parts.append(context.astype(jnp.bfloat16) * owned)
        return dot(back_ref[...], jnp.concatenate(parts, axis=0)).astype(jnp.bfloat16)

    context = jnp.concatenate(
        [level(n_alone, None, (0,)), level(n_pair, n_other, (1, 2))], axis=0
    )
    own = jnp.concatenate([own_ref[lev], own_ref[1 - lev]], axis=0).astype(jnp.float32)
    first = own + dot(context, proj_ref[...])
    normed_two = normalized(first, gain2_ref[...]).astype(jnp.bfloat16)
    mixed = dot(normed_two, fc1_ref[...])
    hidden = (mixed * (1.0 + lax.erf(mixed * (0.5**0.5))) * 0.5).astype(jnp.bfloat16)
    result = (first + dot(hidden, fc2_ref[...])).astype(jnp.bfloat16)
    out_ref[lev] = result[:72]
    out_ref[1 - lev] = result[72:]


def swapped(block, axis, crossed):
    size = lax.axis_size(axis)
    route = []
    for i in range(size):
        mate = i ^ 1 if not crossed else (i + 1 if i % 2 else i - 1) % size
        route.append((mate, i))
    return lax.ppermute(block, axis, route)


def per_device(
    tokens, norm1_gain, qkv_weight, proj_weight, earth_bias, norm2_gain, fc1_weight, fc2_weight
):
    lev = lax.axis_index("lev")
    lat = lax.axis_index("lat")
    lat_size = lax.axis_size("lat")
    lon_even = lax.axis_index("lon") % 2 == 0
    lat_even = lat % 2 == 0

    to_near = jnp.where(lon_even, tokens[:, :, HLO:], tokens[:, :, :HLO])
    to_far = jnp.where(lon_even, tokens[:, :, :HLO], tokens[:, :, HLO:])
    from_far = swapped(to_far, "lon", True)
    from_near = swapped(to_near, "lon", False)
    left = jnp.where(lon_even, from_far, from_near)
    right = jnp.where(lon_even, from_near, from_far)
    wide = jnp.concatenate([left, tokens, right], axis=2)

    tables = earth_bias[:, 0].reshape(2, HEADS, 4, WLA, WLA * SPAN)
    chosen = jnp.stack(
        [
            lax.dynamic_index_in_dim(tables[1], 3 - 3 * lev, 1, False),
            lax.dynamic_index_in_dim(tables[0], 3 * lev, 1, False),
            lax.dynamic_index_in_dim(tables[0], lev + 1, 1, False),
        ]
    )
    chosen = jnp.pad(chosen, ((0, 0), (0, 0), (0, 0), (0, D - WLA * SPAN)))
    lower = chosen[:, :, :HLA].reshape(3 * HEADS * HLA, D)
    upper = chosen[:, :, HLA:].reshape(3 * HEADS * HLA, D)

    head = wide[:, :HLA].reshape(-1, D)
    tail = wide[:, HLA:].reshape(-1, D)
    to_next = jnp.concatenate([tail, upper], axis=0)
    to_prev = jnp.pad(head, ((0, upper.shape[0]), (0, 0)))
    lat_far = swapped(jnp.where(lat_even, to_prev, to_next), "lat", True)
    lat_near = swapped(jnp.where(lat_even, to_next, to_prev), "lat", False)
    before = jnp.where(lat_even, lat_far, lat_near)
    after = jnp.where(lat_even, lat_near, lat_far)
    cells = head.shape[0]
    edges = (2, HLA * 24, D)
    extended = jnp.concatenate(
        [
            before[:cells].reshape(edges),
            wide.reshape(2, -1, D),
            after[:cells].reshape(edges),
        ],
        axis=1,
    )
    other = swapped(lax.dynamic_index_in_dim(extended, 1 - lev, 0, False), "lev", False)

    table = jnp.stack([before[cells:], lower])[:, :, : WLA * SPAN]
    table = table.reshape(2 * 3 * HEADS, HLA, WLA * SPAN)
    table = jnp.pad(table, ((0, 0), (0, 1), (0, 0))).reshape(2 * 3 * GROUP, WLA * SPAN)

    spread, pick, back, owned, side = constants()
    half = lambda a: jnp.asarray(a, jnp.bfloat16)
    whole = pl.BlockSpec(memory_space=pltpu.VMEM)
    result = pl.pallas_call(
        block_kernel,
        out_shape=jax.ShapeDtypeStruct((2, 72, D), jnp.bfloat16),
        in_specs=[pl.BlockSpec(memory_space=pltpu.SMEM)] + [whole] * 15,
        out_specs=whole,
        name="block",
    )(
        jnp.stack([lev, lat, jnp.int32(lat_size - 1)]).astype(jnp.int32),
        extended,
        other,
        tokens.reshape(2, 72, D),
        table,
        norm1_gain.reshape(1, D),
        qkv_weight,
        proj_weight,
        norm2_gain.reshape(1, D),
        fc1_weight,
        fc2_weight,
        half(spread),
        half(pick),
        half(back),
        half(owned),
        jnp.asarray(side),
    )
    return result.reshape(tokens.shape)


def solution(mesh):
    placed = (
        P("lev", "lat", "lon", None),
        P(),
        P(),
        P(),
        P(None, "lat", None, None),
        P(),
        P(),
        P(),
    )
    return jax.shard_map(
        per_device,
        mesh=mesh,
        in_specs=placed,
        out_specs=P("lev", "lat", "lon", None),
        check_vma=False,
    )
```

time: 231 us -> 47 us (0.20)
  the two profiles are of different devices: /device:TPU:24 before, /device:TPU:1 now
where the time goes in v1:
time: 47 us; the launch traced here: 46.6 us
  starting transfers between devices  27.1 us (58%)
  local copies, waits for them, and re-layouts  7.21 us (15%)
  Pallas kernels  6.22 us (13%)
  waiting for transfers between devices  4.88 us (10%)
  other arithmetic  0.87 us (2%)
    ppermute x5, starting transfers between devices, swapped(): return lax.ppermute(block, axis, route)  27.1 us
    pallas_call x1, Pallas kernels, per_device(): pl.pallas_call(block_kernel, out_shape=jax.ShapeDtypeStruct((2, 72, D), j...  6.22 us
    ppermute x5, waiting for transfers between devices, swapped(): return lax.ppermute(block, axis, route)  4.88 us
    unnamed x12, local copies, waits for them, and re-layouts  3.31 us
    pallas_call x1, local copies, waits for them, and re-layouts, per_device(): pl.pallas_call(block_kernel, out_shape=jax.ShapeDtypeStruct((2, 72, D), j...  1.57 us
  transfers between devices with their start and end apart: 5, of which 2 were waited for; matrix products, arithmetic and copies ran while one was open for 8% of the time, Pallas kernels for 0%

profile of v1, /device:TPU:1, one launch (start us, length us, event | category | flops | bytes accessed | tf_op | source)
XLA Modules:
  0.0 46.6 jit_solution(2453955314142421141)
XLA Ops:
  0.0 0.9 %copy.18 = bf16[2,6,12,192]{3,2,1,0:T(8,128)(2,1)S(1)} copy(bf16[2,6,12,192]{3,0,2,1:T(2,128)(2,1)} %param.13) | data formatting | bytes 110592 | tf_op args[0]
  0.9 0.0 copy-start.1
  0.9 7.2 %collective-permute-start = (bf16[2,6,6,192]{3,2,1,0:T(8,128)(2,1)S(1)}, bf16[2,6,6,192]{3,2,1,0:T(8,128)(2,1)S(1)}, u32[]{:S(2)}, u32[]{:S(2)}) collective-permute-start(bf16[2,6,6,192]{3,2,1,0:T(8,128)(2,1)S(1)} %get-tuple-element.15), channel_id=1, source_target_pairs={{62,0},{4,2},{2,4},{8,6},{6,8},{12,10},{10,12},{16,14},{14,16},{20... | collective-permute-start | bytes 82952 | tf_op jit(solution)/shard_map/ppermute | solution.py:167
  8.1 8.8 %collective-permute-start.1 = (bf16[2,6,6,192]{3,2,1,0:T(8,128)(2,1)S(1)}, bf16[2,6,6,192]{3,2,1,0:T(8,128)(2,1)S(1)}, u32[]{:S(2)}, u32[]{:S(2)}) collective-permute-start(bf16[2,6,6,192]{3,2,1,0:T(8,128)(2,1)S(1)} %get-tuple-element.16), channel_id=1, source_target_pairs={{2,0},{0,2},{6,4},{4,6},{10,8},{8,10},{14,12},{12,14},{18,16},{16,... | collective-permute-start | bytes 82952 | tf_op jit(solution)/shard_map/ppermute | solution.py:167
  16.9 0.0 copy-done.1
  16.9 0.3 slice_reduce_fusion.1
  17.3 0.2 squeeze.15
  17.5 0.2 squeeze.16
  17.8 0.0 copy-start.2
  17.8 0.0 copy-start.3
  17.9 0.8 %copy-done.2 = bf16[2,6,12,192]{3,0,2,1:T(2,128)(2,1)S(1)} copy-done((bf16[2,6,12,192]{3,0,2,1:T(2,128)(2,1)S(1)}, bf16[2,6,12,192]{3,0,2,1:T(2,128)(2,1)}, u32[]{:S(2)}) %copy-start.2) | copy-done | bytes 55320
  18.7 0.6 %copy.21.own_ref = bf16[2,72,192]{2,1,0:T(8,128)(2,1)} copy(bf16[2,72,192]{2,0,1:T(2,128)(2,1)S(1)} %bitcast.24) | data formatting | bytes 110592 | tf_op jit(solution)/shard_map/reshape | solution.py:236
  19.4 0.0 copy-done.3
  19.4 0.9 %copy.22.fc2_ref = bf16[768,192]{1,0:T(8,128)(2,1)} copy(bf16[768,192]{0,1:T(8,128)(2,1)S(1)} %copy-done.3) | data formatting | bytes 589824 | tf_op args[7]
  20.3 0.0 collective-permute-done
  20.3 0.0 collective-permute-done.1
  20.4 0.1 pad_maximum_fusion.1
  20.5 3.2 %collective-permute-start.3 = (bf16[198,192]{1,0:T(8,128)(2,1)S(1)}, bf16[198,192]{1,0:T(8,128)(2,1)S(1)}, u32[]{:S(2)}, u32[]{:S(2)}) collective-permute-start(bf16[198,192]{1,0:T(8,128)(2,1)S(1)} %get-tuple-element.7), channel_id=1, source_target_pairs={{64,0},{0,64},{192,128},{128,192},{320,256},{256,320},{448,384},{3... | collective-permute-start | bytes 228104 | tf_op jit(solution)/shard_map/ppermute | solution.py:167
  23.7 4.9 %collective-permute-start.2 = (bf16[198,192]{1,0:T(8,128)(2,1)S(1)}, bf16[198,192]{1,0:T(8,128)(2,1)S(1)}, u32[]{:S(2)}, u32[]{:S(2)}) collective-permute-start(bf16[198,192]{1,0:T(8,128)(2,1)S(1)} %get-tuple-element.8), channel_id=1, source_target_pairs={{448,0},{128,64},{64,128},{256,192},{192,256},{384,320},{320,384},... | collective-permute-start | bytes 228104 | tf_op jit(solution)/shard_map/ppermute | solution.py:167
  28.6 0.6 %pad_add_fusion.where_ref = s32[3]{0:T(128)} fusion(s32[1]{0:T(128)} %constant.57.clone.1, s32[1]{0:T(128)} %bitcast.1, s32[1]{0:T(128)} %bitcast), kind=kLoop, calls=%fused_computation.25 | loop fusion | flops 6 | bytes 24 | tf_op jit(solution)/shard_map/stack | solution.py:233
  29.2 0.0 collective-permute-done.3
  29.2 2.3 %collective-permute-done.2 = bf16[198,192]{1,0:T(8,128)(2,1)S(1)} collective-permute-done((bf16[198,192]{1,0:T(8,128)(2,1)S(1)}, bf16[198,192]{1,0:T(8,128)(2,1)S(1)}, u32[]{:S(2)}, u32[]{:S(2)}) %collective-permute-start.2) | collective-permute-done | bytes 76064 | tf_op jit(solution)/shard_map/ppermute | solution.py:167
  31.7 0.0 copy-start
  31.7 3.1 %collective-permute-start.4 = (bf16[288,192]{1,0:T(8,128)(2,1)S(1)}, bf16[288,192]{1,0:T(8,128)(2,1)S(1)}, u32[]{:S(2)}, u32[]{:S(2)}) collective-permute-start(bf16[288,192]{1,0:T(8,128)(2,1)S(1)} %dynamic-slice_bitcast_fusion), channel_id=1, source_target_pairs={{1,0},{0,1},{3,2},{2,3},{5,4},{4,5},{7,6},{6,7},{9,8},{8,9},{11,10... | collective-permute-start | bytes 331784 | tf_op jit(solution)/shard_map/ppermute | solution.py:167
  34.9 0.0 copy-done
  34.9 0.7 %reshape.51.table_ref = bf16[144,138]{1,0:T(8,128)(2,1)} reshape(bf16[36,4,138]{2,1,0:T(4,128)(2,1)S(1)} %pad.14) | data formatting | bytes 79488 | tf_op jit(solution)/shard_map/reshape | solution.py:221
  35.6 2.5 %collective-permute-done.4.other_ref = bf16[288,192]{1,0:T(8,128)(2,1)S(1)} collective-permute-done((bf16[288,192]{1,0:T(8,128)(2,1)S(1)}, bf16[288,192]{1,0:T(8,128)(2,1)S(1)}, u32[]{:S(2)}, u32[]{:S(2)}) %collective-permute-start.4) | collective-permute-done | bytes 110624 | tf_op jit(solution)/shard_map/ppermute | solution.py:167
  38.1 0.0 copy-start.4
  38.1 0.7 %copy-done.4 = bf16[288,192]{1,0:T(8,128)(2,1)} copy-done((bf16[288,192]{1,0:T(8,128)(2,1)}, bf16[288,192]{1,0:T(8,128)(2,1)S(1)}, u32[]{:S(2)}) %copy-start.4) | copy-done | bytes 110616
  38.8 6.2 %block.1 = bf16[2,72,192]{2,1,0:T(8,128)(2,1)} custom-call(s32[3]{0:T(128)} %pad_add_fusion.where_ref, bf16[2,288,192]{2,1,0:T(8,128)(2,1)} %copy-done, bf16[288,192]{1,0:T(8,128)(2,1)} %copy-done.4, bf16[2,72,192]{2,1,0:T(8,128)(2,1)} %copy.21.own_ref, bf16[144,138]{1,0:T(8,128)(2,1)} %reshape.51.table_ref, f32[1,192]{1,0:T(1,128)} %bitcast.27, ...), custom_call_target="tpu_custom_call" | custom-call | tf_op jit(solution)/shard_map/block/pallas_call | solution.py:226
  45.0 1.6 %copy.23 = bf16[2,72,192]{2,0,1:T(2,128)(2,1)} copy(bf16[2,72,192]{2,1,0:T(8,128)(2,1)} %block.1) | data formatting | bytes 110592 | tf_op jit(solution)/shard_map/block/pallas_call | solution.py:226
  (18 shorter events, 0.4 us)
Async XLA Ops:
  0.9 16.0 %copy-start.1 = (bf16[2,1,6,3312]{3,0,2,1:T(2,128)(2,1)S(1)}, bf16[2,1,6,3312]{3,0,2,1:T(2,128)(2,1)}, u32[]{:S(2)}) copy-start(bf16[2,1,6,3312]{3,0,2,1:T(2,128)(2,1)} %param.17) | copy-start | bytes 238468
  0.9 19.4 %collective-permute-start = (bf16[2,6,6,192]{3,2,1,0:T(8,128)(2,1)S(1)}, bf16[2,6,6,192]{3,2,1,0:T(8,128)(2,1)S(1)}, u32[]{:S(2)}, u32[]{:S(2)}) collective-permute-start(bf16[2,6,6,192]{3,2,1,0:T(8,128)(2,1)S(1)} %get-tuple-element.15), channel_id=1, source_target_pairs={{62,0},{4,2},{2,4},{8,6},{6,8},{12,10},{10,12},{16,14},{14,16},{20... | collective-permute-start | bytes 82952 | tf_op jit(solution)/shard_map/ppermute | solution.py:167
  8.1 12.2 %collective-permute-start.1 = (bf16[2,6,6,192]{3,2,1,0:T(8,128)(2,1)S(1)}, bf16[2,6,6,192]{3,2,1,0:T(8,128)(2,1)S(1)}, u32[]{:S(2)}, u32[]{:S(2)}) collective-permute-start(bf16[2,6,6,192]{3,2,1,0:T(8,128)(2,1)S(1)} %get-tuple-element.16), channel_id=1, source_target_pairs={{2,0},{0,2},{6,4},{4,6},{10,8},{8,10},{14,12},{12,14},{18,16},{16,... | collective-permute-start | bytes 82952 | tf_op jit(solution)/shard_map/ppermute | solution.py:167
  17.8 0.9 %copy-start.2 = (bf16[2,6,12,192]{3,0,2,1:T(2,128)(2,1)S(1)}, bf16[2,6,12,192]{3,0,2,1:T(2,128)(2,1)}, u32[]{:S(2)}) copy-start(bf16[2,6,12,192]{3,0,2,1:T(2,128)(2,1)} %param.13) | copy-start | bytes 165892
  17.8 1.6 %copy-start.3 = (bf16[768,192]{0,1:T(8,128)(2,1)S(1)}, bf16[768,192]{0,1:T(8,128)(2,1)}, u32[]{:S(2)}) copy-start(bf16[768,192]{0,1:T(8,128)(2,1)} %param.20) | copy-start | bytes 884740
  20.5 8.7 %collective-permute-start.3 = (bf16[198,192]{1,0:T(8,128)(2,1)S(1)}, bf16[198,192]{1,0:T(8,128)(2,1)S(1)}, u32[]{:S(2)}, u32[]{:S(2)}) collective-permute-start(bf16[198,192]{1,0:T(8,128)(2,1)S(1)} %get-tuple-element.7), channel_id=1, source_target_pairs={{64,0},{0,64},{192,128},{128,192},{320,256},{256,320},{448,384},{3... | collective-permute-start | bytes 228104 | tf_op jit(solution)/shard_map/ppermute | solution.py:167
  23.7 7.8 %collective-permute-start.2 = (bf16[198,192]{1,0:T(8,128)(2,1)S(1)}, bf16[198,192]{1,0:T(8,128)(2,1)S(1)}, u32[]{:S(2)}, u32[]{:S(2)}) collective-permute-start(bf16[198,192]{1,0:T(8,128)(2,1)S(1)} %get-tuple-element.8), channel_id=1, source_target_pairs={{448,0},{128,64},{64,128},{256,192},{192,256},{384,320},{320,384},... | collective-permute-start | bytes 228104 | tf_op jit(solution)/shard_map/ppermute | solution.py:167
  31.7 3.3 %copy-start = (bf16[2,288,192]{2,1,0:T(8,128)(2,1)}, bf16[2,288,192]{2,1,0:T(8,128)(2,1)S(1)}, u32[]{:S(2)}) copy-start(bf16[2,288,192]{2,1,0:T(8,128)(2,1)S(1)} %pad_maximum_fusion.wide_ref) | copy-start | bytes 663556
  31.7 6.4 %collective-permute-start.4 = (bf16[288,192]{1,0:T(8,128)(2,1)S(1)}, bf16[288,192]{1,0:T(8,128)(2,1)S(1)}, u32[]{:S(2)}, u32[]{:S(2)}) collective-permute-start(bf16[288,192]{1,0:T(8,128)(2,1)S(1)} %dynamic-slice_bitcast_fusion), channel_id=1, source_target_pairs={{1,0},{0,1},{3,2},{2,3},{5,4},{4,5},{7,6},{6,7},{9,8},{8,9},{11,10... | collective-permute-start | bytes 331784 | tf_op jit(solution)/shard_map/ppermute | solution.py:167
  38.1 0.7 %copy-start.4 = (bf16[288,192]{1,0:T(8,128)(2,1)}, bf16[288,192]{1,0:T(8,128)(2,1)S(1)}, u32[]{:S(2)}) copy-start(bf16[288,192]{1,0:T(8,128)(2,1)S(1)} %collective-permute-done.4.other_ref) | copy-start | bytes 331780

commit v2 on v1

v2 whole, which is shorter than its diff:
```python
import numpy as np
import jax
import jax.numpy as jnp
from jax import lax
from jax.experimental import pallas as pl
from jax.experimental.pallas import tpu as pltpu
from jax.sharding import PartitionSpec as P

D = 192
HEADS = 6
HEAD_DIM = 32
WLA = 6
WLO = 12
HLA = 3
HLO = 6
SPAN = 2 * WLO - 1
ROWS = 288
HALF = 144
QROWS = 288
GROUP = 24
FAR = -1e30
LANES = 256
VMEM_LIMIT = 16 * 1024 * 1024

norm_eps = 1e-05


def constants():
    column = np.arange(24)
    place = np.arange(WLA)
    spread = np.zeros((WLO, D, HALF), np.float32)
    for o in range(WLO):
        for k in column:
            d = o - k + 17
            if (o < HLO) == (k < WLO):
                spread[o, place * SPAN + d, place * 24 + k] = 1
    pick = np.zeros((2, QROWS, HALF), np.float32)
    back = np.zeros((72, 2 * QROWS), np.float32)
    owned = np.zeros((QROWS, D), np.float32)
    mine = np.zeros((72, ROWS), np.float32)
    for o in range(WLO):
        for a in range(WLA):
            mine[a * WLO + o, (HLA + a) * 24 + HLO + o] = 1
        for h in range(HEADS):
            for a in range(4):
                row = o * GROUP + h * 4 + a
                owned[row, h * HEAD_DIM : (h + 1) * HEAD_DIM] = 1
                if a < HLA:
                    pick[0, row, (HLA + a) * 24 + HLO + o] = 1
                    pick[1, row, a * 24 + HLO + o] = 1
                    back[a * WLO + o, row] = 1
                    back[(HLA + a) * WLO + o, QROWS + row] = 1
    gaps = np.zeros((3 * GROUP, 3 * HEADS * HLA), np.float32)
    for e in range(3 * HEADS):
        for a in range(HLA):
            gaps[e * 4 + a, e * HLA + a] = 1
    woven = np.zeros((2, 144, 72), np.float32)
    cell = np.arange(72)
    for at in range(2):
        woven[at, 2 * cell + at, cell] = 1
    side = (np.arange(HALF) % 24 >= WLO).astype(np.float32).reshape(1, HALF)
    return spread, pick, back, owned, mine, gaps, woven, side


def normalized(values, gain):
    average = jnp.mean(values, axis=-1, keepdims=True)
    centered = values - average
    variance = jnp.mean(centered * centered, axis=-1, keepdims=True)
    return centered * lax.rsqrt(variance + norm_eps) * gain


def dot(a, b):
    return jnp.dot(a, b, preferred_element_type=jnp.float32)


def dot_t(a, b):
    return lax.dot_general(a, b, (((1,), (1,)), ((), ())), preferred_element_type=jnp.float32)


def halved(x):
    return x.astype(jnp.bfloat16)


def softmax_context(scores, values, owned):
    top = jnp.max(scores[0], axis=-1, keepdims=True)
    for s in scores[1:]:
        top = jnp.maximum(top, jnp.max(s, axis=-1, keepdims=True))
    weights = [jnp.exp(s - top) for s in scores]
    total = jnp.sum(weights[0], axis=-1, keepdims=True)
    for w in weights[1:]:
        total = total + jnp.sum(w, axis=-1, keepdims=True)
    inverse = 1.0 / total
    context = 0.0
    for w, v in zip(weights, values):
        context = context + dot(halved(w * inverse), v)
    return halved(context) * owned


def finish(own, parts, back, proj, gain, fc1, fc2_t):
    context = halved(dot(back, jnp.concatenate(parts, axis=0)))
    first = own + dot(context, proj)
    mixed = dot(halved(normalized(first, gain)), fc1)
    hidden = halved(mixed * (1.0 + lax.erf(mixed * (0.5**0.5))) * 0.5)
    return halved(first + dot_t(hidden, fc2_t))


def early_kernel(
    wide_ref,
    before_ref,
    lower_ref,
    gain1_ref,
    qkv_ref,
    proj_ref,
    gain2_ref,
    fc1_ref,
    fc2_ref,
    spread_ref,
    pick_ref,
    back_ref,
    owned_ref,
    mine_ref,
    gaps_ref,
    side_ref,
    alone_ref,
    own_ref,
    asked_ref,
    value_ref,
    score_ref,
    bias_ref,
):
    lev = lax.axis_index("lev")
    lat = lax.axis_index("lat")
    lat_last = lax.axis_size("lat") - 1
    gain1 = gain1_ref[...]
    w_q = qkv_ref[:, :D]
    w_k = qkv_ref[:, D : 2 * D]
    w_v = qkv_ref[:, 2 * D :]
    owned = owned_ref[...]

    gaps = gaps_ref[...]
    cells = 2 * HLA * 24
    table = halved(
        jnp.concatenate(
            [
                dot(gaps, before_ref[cells : cells + 3 * HEADS * HLA, :D]),
                dot(gaps, lower_ref[:, :D]),
            ],
            axis=0,
        )
    )
    spreads = [dot(table, spread_ref[o]) for o in range(WLO)]
    row_half = lax.broadcasted_iota(jnp.int32, (QROWS, HALF), 0) >= QROWS // 2
    lane = lax.broadcasted_iota(jnp.int32, (QROWS, HALF), 1)
    side = jnp.broadcast_to(side_ref[...], (QROWS, HALF)) > 0.5
    same_side = row_half == side
    allowed = [
        same_side & ((lane >= 72) | (lat > 0)),
        same_side & ((lane < 72) | (lat < lat_last)),
    ]

    def bias_of(lat_window, entry):
        at = (lat_window * 3 + entry) * GROUP
        terms = jnp.concatenate([s[at : at + GROUP] for s in spreads], axis=0)
        return jnp.where(allowed[lat_window], terms, FAR)

    def asked_of(cells):
        n = halved(normalized(cells.astype(jnp.float32), gain1))
        queries = halved(dot(n, w_q))
        keys = halved(dot(n, w_k))
        values = halved(dot(n, w_v))
        out = []
        for lat_window in range(2):
            rows = slice(lat_window * HALF, (lat_window + 1) * HALF)
            asked = halved(dot(pick_ref[lat_window], queries[rows])) * owned
            out.append((asked, dot_t(asked, keys[rows]) * HEAD_DIM**-0.5, values[rows]))
        return out

    pair_cells = wide_ref[1 - lev]
    for lat_window, (asked, scores, values) in enumerate(asked_of(pair_cells)):
        asked_ref[lat_window] = asked
        value_ref[lat_window] = values
        score_ref[lat_window] = scores + bias_of(lat_window, 1)
        bias_ref[lat_window] = bias_of(lat_window, 2)
    own_ref[...] = dot(mine_ref[...], pair_cells)

    alone_cells = wide_ref[lev]
    parts = []
    for lat_window, (asked, scores, values) in enumerate(asked_of(alone_cells)):
        parts.append(softmax_context([scores + bias_of(lat_window, 0)], [values], owned))
    alone_ref[...] = finish(
        dot(mine_ref[...], alone_cells),
        parts,
        back_ref[...],
        proj_ref[...],
        gain2_ref[...],
        fc1_ref[...],
        fc2_ref[...],
    )


def late_kernel(
    other_ref,
    alone_ref,
    own_ref,
    asked_ref,
    value_ref,
    score_ref,
    bias_ref,
    gain1_ref,
    qkv_ref,
    proj_ref,
    gain2_ref,
    fc1_ref,
    fc2_ref,
    back_ref,
    owned_ref,
    woven_ref,
    out_ref,
):
    lev = lax.axis_index("lev")
    owned = owned_ref[...]
    n = halved(normalized(other_ref[...].astype(jnp.float32), gain1_ref[...]))
    keys = halved(dot(n, qkv_ref[:, D : 2 * D]))
    values = halved(dot(n, qkv_ref[:, 2 * D :]))
    parts = []
    for lat_window in range(2):
        rows = slice(lat_window * HALF, (lat_window + 1) * HALF)
        scores = dot_t(asked_ref[lat_window], keys[rows]) * HEAD_DIM**-0.5 + bias_ref[lat_window]
        parts.append(
            softmax_context(
                [score_ref[lat_window], scores], [value_ref[lat_window], values[rows]], owned
            )
        )
    pair = finish(
        own_ref[...],
        parts,
        back_ref[...],
        proj_ref[...],
        gain2_ref[...],
        fc1_ref[...],
        fc2_ref[...],
    )
    alone = alone_ref[...]
    lower = jnp.where(lev == 0, alone, pair)
    upper = jnp.where(lev == 0, pair, alone)
    result = halved(dot(woven_ref[0], lower) + dot(woven_ref[1], upper))
    out_ref[...] = result.reshape(72, 2, D)


def pairs_of(size, crossed):
    shift = 1 if crossed else 0
    return [[(2 * i + shift) % size, (2 * i + 1 + shift) % size] for i in range(size // 2)]


def swapped(block, axis, crossed):
    route = []
    for a, b in pairs_of(lax.axis_size(axis), crossed):
        route += [(a, b), (b, a)]
    return lax.ppermute(block, axis, route)


def per_device(
    tokens, norm1_gain, qkv_weight, proj_weight, earth_bias, norm2_gain, fc1_weight, fc2_weight
):
    lev = lax.axis_index("lev")
    lat = lax.axis_index("lat")
    lon_size = lax.axis_size("lon")
    lat_size = lax.axis_size("lat")
    lon_even = lax.axis_index("lon") % 2 == 0
    lat_even = lat % 2 == 0

    far = swapped(jnp.where(lon_even, tokens[:, :, :HLO], tokens[:, :, HLO:]), "lon", True)
    joint = lax.all_gather(
        tokens, "lon", axis_index_groups=pairs_of(lon_size, False), axis=2, tiled=True
    )
    wide = jnp.where(
        lon_even,
        jnp.concatenate([far, joint[:, :, : WLO + HLO]], axis=2),
        jnp.concatenate([joint[:, :, HLO:], far], axis=2),
    )

    tables = earth_bias[:, 0].reshape(2, HEADS, 4, WLA, WLA * SPAN)
    chosen = jnp.stack(
        [
            lax.dynamic_index_in_dim(tables[1], 3 - 3 * lev, 1, False),
            lax.dynamic_index_in_dim(tables[0], 3 * lev, 1, False),
            lax.dynamic_index_in_dim(tables[0], lev + 1, 1, False),
        ]
    )
    chosen = jnp.pad(chosen, ((0, 0), (0, 0), (0, 0), (0, LANES - WLA * SPAN)))
    lower = chosen[:, :, :HLA].reshape(3 * HEADS * HLA, LANES)
    upper = chosen[:, :, HLA:].reshape(3 * HEADS * HLA, LANES)

    head = wide[:, :HLA].reshape(-1, D)
    tail = wide[:, HLA:].reshape(-1, D)
    cells = head.shape[0]
    to_next = jnp.concatenate([jnp.pad(tail, ((0, 0), (0, LANES - D))), upper], axis=0)
    to_prev = jnp.pad(head, ((0, upper.shape[0]), (0, LANES - D)))
    lat_far = swapped(jnp.where(lat_even, to_prev, to_next), "lat", True)
    lat_both = lax.all_gather(
        jnp.where(lat_even, to_next, to_prev), "lat", axis_index_groups=pairs_of(lat_size, False)
    )
    lat_near = jnp.where(lat_even, lat_both[1], lat_both[0])
    before = jnp.where(lat_even, lat_far, lat_near)
    after = jnp.where(lat_even, lat_near, lat_far)
    edges = (2, HLA * 24, D)
    extended = jnp.concatenate(
        [
            before[:cells, :D].reshape(edges),
            wide.reshape(2, -1, D),
            after[:cells, :D].reshape(edges),
        ],
        axis=1,
    )
    other = swapped(lax.dynamic_index_in_dim(extended, 1 - lev, 0, False), "lev", False)

    spread, pick, back, owned, mine, gaps, woven = [
        jnp.asarray(a, jnp.bfloat16) for a in constants()[:-1]
    ]
    side = jnp.asarray(constants()[-1])
    whole = pl.BlockSpec(memory_space=pltpu.VMEM)
    held = lambda x: pltpu.with_memory_space_constraint(x, pltpu.VMEM)
    shared = [
        held(a)
        for a in (
            norm1_gain.reshape(1, D),
            qkv_weight,
            proj_weight,
            norm2_gain.reshape(1, D),
            fc1_weight,
            fc2_weight.T,
        )
    ]
    back = held(back)
    owned = held(owned)
    passed = [
        pltpu.VMEM((72, D), jnp.bfloat16),
        pltpu.VMEM((72, D), jnp.float32),
        pltpu.VMEM((2, QROWS, D), jnp.bfloat16),
        pltpu.VMEM((2, HALF, D), jnp.bfloat16),
        pltpu.VMEM((2, QROWS, HALF), jnp.float32),
        pltpu.VMEM((2, QROWS, HALF), jnp.float32),
    ]
    early = pl.pallas_call(
        early_kernel,
        out_shape=passed,
        in_specs=[whole] * 16,
        out_specs=[whole] * 6,
        cost_estimate=pl.CostEstimate(flops=4_000_000_000, transcendentals=0, bytes_accessed=0),
        compiler_params=pltpu.CompilerParams(vmem_limit_bytes=VMEM_LIMIT),
        name="early",
    )(
        held(extended),
        held(before),
        held(lower),
        *shared,
        held(spread),
        held(pick),
        back,
        owned,
        held(mine),
        held(gaps),
        held(side),
    )
    result = pl.pallas_call(
        late_kernel,
        out_shape=jax.ShapeDtypeStruct((72, 2, D), jnp.bfloat16),
        in_specs=[whole] * 16,
        out_specs=whole,
        compiler_params=pltpu.CompilerParams(vmem_limit_bytes=VMEM_LIMIT),
        name="late",
    )(held(other), *[held(x) for x in early], *shared, back, owned, held(woven))
    return result.reshape(WLA, WLO, 2, D).transpose(2, 0, 1, 3)


def solution(mesh):
    placed = (
        P("lev", "lat", "lon", None),
        P(),
        P(),
        P(),
        P(None, "lat", None, None),
        P(),
        P(),
        P(),
    )
    return jax.shard_map(
        per_device,
        mesh=mesh,
        in_specs=placed,
        out_specs=P("lev", "lat", "lon", None),
        check_vma=False,
    )
```

time: 47 us -> 39 us (0.83)
  the two profiles are of different devices: /device:TPU:1 before, /device:TPU:24 now
where the time goes in v2:
time: 39 us; the launch traced here: 38.7 us
  starting transfers between devices  20.8 us (53%)
  blocking collectives  7.58 us (19%)
  Pallas kernels  5.32 us (14%)
  local copies, waits for them, and re-layouts  2.29 us (6%)
  other arithmetic  1.32 us (3%)
  waiting for transfers between devices  1 us (3%)
  between operations  0.41 us (1%)
    ppermute x3, starting transfers between devices, swapped(): return lax.ppermute(block, axis, route)  20.8 us
    all_gather x1, blocking collectives, per_device(): lax.all_gather(jnp.where(lat_even, to_next, to_prev), 'lat', axis_index_g...  5.46 us
    pallas_call x1, Pallas kernels, per_device(): pl.pallas_call(late_kernel, out_shape=jax.ShapeDtypeStruct((72, 2, D), jn...  2.82 us
    pallas_call x1, Pallas kernels, per_device(): pl.pallas_call(early_kernel, out_shape=passed, in_specs=[whole] * 16, out...  2.5 us
    all_gather x1, blocking collectives, per_device(): lax.all_gather(tokens, 'lon', axis_index_groups=pairs_of(lon_size, False)...  2.12 us
    slice x1, local copies, waits for them, and re-layouts, per_device(): tables[1]  1.32 us
    ppermute x3, waiting for transfers between devices, swapped(): return lax.ppermute(block, axis, route)  1 us
    select_n x1, other arithmetic, per_device(): jnp.where(lon_even, tokens[:, :, :HLO], tokens[:, :, HLO:])  0.83 us
  transfers between devices with their start and end apart: 3, of which 1 were waited for; matrix products, arithmetic and copies ran while one was open for 5% of the time, Pallas kernels for 6%

profile of v2, /device:TPU:24, one launch (start us, length us, event | category | flops | bytes accessed | tf_op | source)
XLA Modules:
  0.0 38.7 jit_solution(9582877796476753080)
XLA Ops:
  0.0 0.8 %broadcast_select_fusion.2 = bf16[2,6,6,192]{3,0,2,1:T(2,128)(2,1)S(1)} fusion(pred[]{:T(512)S(6)} %eq.10, bf16[2,6,12,192]{3,0,2,1:T(2,128)(2,1)} %param.16), kind=kLoop, calls=%fused_computation.21 | loop fusion | flops 13824 | bytes 82945 | tf_op jit(solution)/shard_map/jit(_where)/select_n | solution.py:272
  0.8 12.6 %collective-permute-start = (bf16[2,6,6,192]{3,0,2,1:T(2,128)(2,1)S(1)}, bf16[2,6,6,192]{3,0,2,1:T(2,128)(2,1)S(1)}, u32[]{:S(2)}, u32[]{:S(2)}) collective-permute-start(bf16[2,6,6,192]{3,0,2,1:T(2,128)(2,1)S(1)} %broadcast_select_fusion.2), channel_id=1, source_target_pairs={{2,4},{4,2},{6,8},{8,6},{10,12},{12,10},{14,16},{16,14},{18,20},{2... | collective-permute-start | bytes 82952 | tf_op jit(solution)/shard_map/ppermute | solution.py:259
  13.4 2.1 %all_gather.9 = bf16[2,6,24,192]{3,0,2,1:T(2,128)(2,1)S(1)} all-gather(bf16[2,6,12,192]{3,0,2,1:T(2,128)(2,1)} %param.16), channel_id=1, replica_groups={{0,2},{4,6},{8,10},{12,14},{16,18},{20,22},{24,26},{28,30},{32,34},{36,..., dimensions={2}, use_global_device_ids=true | all-gather | bytes 165888 | tf_op jit(solution)/shard_map/all_gather | solution.py:273
  15.5 1.3 %slice_reduce_fusion.1 = (bf16[6,3312]{1,0:T(8,128)(2,1)S(1)}, bf16[6,3312]{1,0:T(8,128)(2,1)S(1)}) fusion(bf16[2,1,6,3312]{3,0,2,1:T(2,128)(2,1)} %param.20), kind=kLoop, calls=%fused_computation.17 | loop fusion | bytes 158976 | tf_op jit(solution)/shard_map/slice | solution.py:285
  16.9 0.2 squeeze.17
  17.1 0.2 squeeze.18
  17.3 0.1 fusion.11
  17.6 0.0 collective-permute-done
  17.6 0.3 broadcast_select_fusion
  18.0 0.1 fusion.10
  18.1 0.0 copy-start.10
  18.2 4.8 %collective-permute-start.1 = (bf16[198,256]{1,0:T(8,128)(2,1)S(1)}, bf16[198,256]{1,0:T(8,128)(2,1)S(1)}, u32[]{:S(2)}, u32[]{:S(2)}) collective-permute-start(bf16[198,256]{1,0:T(8,128)(2,1)S(1)} %get-tuple-element.22), channel_id=1, source_target_pairs={{64,128},{128,64},{192,256},{256,192},{320,384},{384,320},{448,0},... | collective-permute-start | bytes 304136 | tf_op jit(solution)/shard_map/ppermute | solution.py:259
  23.0 0.0 copy-start.11
  23.1 0.0 copy-start
  23.1 0.0 copy-start.1
  23.1 0.0 copy-start.2
  23.1 0.0 copy-start.3
  23.1 0.0 copy-start.4
  23.1 0.0 copy-start.5
  23.1 0.0 copy-start.7
  23.2 0.0 copy-start.8
  23.2 0.0 copy-start.9
  23.2 0.0 copy-start.12
  23.2 0.0 copy-start.13
  23.2 5.5 %all-gather.1 = bf16[2,198,256]{2,1,0:T(8,128)(2,1)S(1)} all-gather(bf16[1,198,256]{2,1,0:T(8,128)(2,1)S(1)} %get-tuple-element.21), channel_id=2, replica_groups={{0,64},{128,192},{256,320},{384,448},{1,65},{129,193},{257,321},{385,44..., dimensions={0}, use_global_device_ids=true | all-gather | bytes 304128 | tf_op jit(solution)/shard_map/all_gather | solution.py:300
  28.7 0.0 collective-permute-done.1
  28.8 3.4 %collective-permute-start.2 = (bf16[288,192]{1,0:T(8,128)(2,1)S(1)}, bf16[288,192]{1,0:T(8,128)(2,1)S(1)}, u32[]{:S(2)}, u32[]{:S(2)}) collective-permute-start(bf16[288,192]{1,0:T(8,128)(2,1)S(1)} %dynamic-slice_bitcast_fusion), channel_id=1, source_target_pairs={{0,1},{1,0},{2,3},{3,2},{4,5},{5,4},{6,7},{7,6},{8,9},{9,8},{10,11... | collective-permute-start | bytes 331784 | tf_op jit(solution)/shard_map/ppermute | solution.py:259
  32.2 0.0 copy-done.10
  32.2 0.0 copy-done.11
  32.3 0.0 copy-done
  32.3 0.0 copy-done.1
  32.3 0.0 copy-done.2
  32.3 0.0 copy-done.3
  32.3 0.0 copy-done.4
  32.3 0.0 copy-done.5
  32.3 0.0 copy-done.7
  32.3 0.0 copy-done.8
  32.3 0.0 copy-done.9
  32.3 0.0 copy-done.12
  32.4 0.0 copy-done.13
  32.4 0.0 copy-start.6
  32.4 2.5 %early.1 = (bf16[72,192]{1,0:T(8,128)(2,1)S(1)}, f32[72,192]{1,0:T(8,128)S(1)}, bf16[2,288,192]{2,1,0:T(8,128)(2,1)S(1)}, bf16[2,144,192]{2,1,0:T(8,128)(2,1)S(1...) custom-call(bf16[2,288,192]{2,1,0:T(8,128)(2,1)S(1)} %pad_maximum_fusion.wide_ref, ...), custom_call_target="tpu_custom_call" | custom-call | flops 4000000000 | tf_op jit(solution)/shard_map/early/pallas_call | solution.py:344
  34.9 1.0 %collective-permute-done.2.other_ref = bf16[288,192]{1,0:T(8,128)(2,1)S(1)} collective-permute-done((bf16[288,192]{1,0:T(8,128)(2,1)S(1)}, bf16[288,192]{1,0:T(8,128)(2,1)S(1)}, u32[]{:S(2)}, u32[]{:S(2)}) %collective-permute-start.2) | collective-permute-done | bytes 110624 | tf_op jit(solution)/shard_map/ppermute | solution.py:259
  35.9 0.0 copy-done.6
  35.9 2.8 %late.1 = bf16[72,2,192]{2,1,0:T(2,128)(2,1)} custom-call(bf16[288,192]{1,0:T(8,128)(2,1)S(1)} %collective-permute-done.2.other_ref, bf16[72,192]{1,0:T(8,128)(2,1)S(1)} %get-tuple-element.11.alone_ref, f32[72,192]{1,0:T(8,128)S(1)} %get-tuple-element.12.own_ref, bf16[2,288,192]{2,1,0:T(8,128)(2,1)S(1)} %get-tuple-element.13.asked_ref, ...), custom_call_target="tpu_custom_call" | custom-call | tf_op jit(solution)/shard_map/late/pallas_call | solution.py:365
  (14 shorter events, 0.3 us)
Async XLA Ops:
  0.8 16.8 %collective-permute-start = (bf16[2,6,6,192]{3,0,2,1:T(2,128)(2,1)S(1)}, bf16[2,6,6,192]{3,0,2,1:T(2,128)(2,1)S(1)}, u32[]{:S(2)}, u32[]{:S(2)}) collective-permute-start(bf16[2,6,6,192]{3,0,2,1:T(2,128)(2,1)S(1)} %broadcast_select_fusion.2), channel_id=1, source_target_pairs={{2,4},{4,2},{6,8},{8,6},{10,12},{12,10},{14,16},{16,14},{18,20},{2... | collective-permute-start | bytes 82952 | tf_op jit(solution)/shard_map/ppermute | solution.py:259
  18.1 14.1 %copy-start.10 = (bf16[2,288,144]{2,1,0:T(8,128)(2,1)S(1)}, bf16[2,288,144]{2,1,0:T(8,128)(2,1)}, u32[]{:S(2)}) copy-start(bf16[2,288,144]{2,1,0:T(8,128)(2,1)} %constant.72.clone.pick_ref) | copy-start | bytes 497668
  18.2 10.5 %collective-permute-start.1 = (bf16[198,256]{1,0:T(8,128)(2,1)S(1)}, bf16[198,256]{1,0:T(8,128)(2,1)S(1)}, u32[]{:S(2)}, u32[]{:S(2)}) collective-permute-start(bf16[198,256]{1,0:T(8,128)(2,1)S(1)} %get-tuple-element.22), channel_id=1, source_target_pairs={{64,128},{128,64},{192,256},{256,192},{320,384},{384,320},{448,0},... | collective-permute-start | bytes 304136 | tf_op jit(solution)/shard_map/ppermute | solution.py:259
  23.0 9.2 %copy-start.11 = (bf16[72,288]{1,0:T(8,128)(2,1)S(1)}, bf16[72,288]{1,0:T(8,128)(2,1)}, u32[]{:S(2)}) copy-start(bf16[72,288]{1,0:T(8,128)(2,1)} %constant.75.clone.mine_ref) | copy-start | bytes 124420
  23.1 9.2 %copy-start = (bf16[192,768]{1,0:T(8,128)(2,1)S(1)}, bf16[192,768]{1,0:T(8,128)(2,1)}, u32[]{:S(2)}) copy-start(bf16[192,768]{1,0:T(8,128)(2,1)} %fc1_ref.3) | copy-start | bytes 884740
  23.1 9.2 %copy-start.1 = (bf16[768,192]{0,1:T(8,128)(2,1)S(1)}, bf16[768,192]{0,1:T(8,128)(2,1)}, u32[]{:S(2)}) copy-start(bf16[768,192]{0,1:T(8,128)(2,1)} %param.23) | copy-start | bytes 884740
  23.1 9.2 %copy-start.2 = (bf16[192,576]{1,0:T(8,128)(2,1)S(1)}, bf16[192,576]{1,0:T(8,128)(2,1)}, u32[]{:S(2)}) copy-start(bf16[192,576]{1,0:T(8,128)(2,1)} %qkv_ref.3) | copy-start | bytes 663556
  23.1 9.2 %copy-start.3 = (bf16[288,192]{1,0:T(8,128)(2,1)S(1)}, bf16[288,192]{1,0:T(8,128)(2,1)}, u32[]{:S(2)}) copy-start(bf16[288,192]{1,0:T(8,128)(2,1)} %constant.74.clone.owned_ref) | copy-start | bytes 331780
  23.1 9.2 %copy-start.4 = (bf16[192,192]{1,0:T(8,128)(2,1)S(1)}, bf16[192,192]{1,0:T(8,128)(2,1)}, u32[]{:S(2)}) copy-start(bf16[192,192]{1,0:T(8,128)(2,1)} %proj_ref.3) | copy-start | bytes 221188
  23.1 9.2 %copy-start.5 = (bf16[72,576]{1,0:T(8,128)(2,1)S(1)}, bf16[72,576]{1,0:T(8,128)(2,1)}, u32[]{:S(2)}) copy-start(bf16[72,576]{1,0:T(8,128)(2,1)} %constant.73.clone.back_ref) | copy-start | bytes 248836
  23.1 9.2 %copy-start.7 = (f32[192]{0:T(256)S(1)}, f32[192]{0:T(256)}, u32[]{:S(2)}) copy-start(f32[192]{0:T(256)} %param.17) | copy-start | bytes 2308
  23.2 9.2 %copy-start.8 = (f32[192]{0:T(256)S(1)}, f32[192]{0:T(256)}, u32[]{:S(2)}) copy-start(f32[192]{0:T(256)} %param.21) | copy-start | bytes 2308
  23.2 9.2 %copy-start.9 = (bf16[12,192,144]{2,1,0:T(8,128)(2,1)S(1)}, bf16[12,192,144]{2,1,0:T(8,128)(2,1)}, u32[]{:S(2)}) copy-start(bf16[12,192,144]{2,1,0:T(8,128)(2,1)} %constant.71.clone.spread_ref) | copy-start | bytes 1990660
  23.2 9.2 %copy-start.12 = (bf16[72,54]{1,0:T(8,128)(2,1)S(1)}, bf16[72,54]{1,0:T(8,128)(2,1)}, u32[]{:S(2)}) copy-start(bf16[72,54]{1,0:T(8,128)(2,1)} %constant.76.clone.gaps_ref) | copy-start | bytes 23332
  23.2 9.2 %copy-start.13 = (f32[1,144]{1,0:T(1,128)S(1)}, f32[1,144]{1,0:T(1,128)}, u32[]{:S(2)}) copy-start(f32[1,144]{1,0:T(1,128)} %constant.78.clone.side_ref) | copy-start | bytes 1732
  28.8 7.0 %collective-permute-start.2 = (bf16[288,192]{1,0:T(8,128)(2,1)S(1)}, bf16[288,192]{1,0:T(8,128)(2,1)S(1)}, u32[]{:S(2)}, u32[]{:S(2)}) collective-permute-start(bf16[288,192]{1,0:T(8,128)(2,1)S(1)} %dynamic-slice_bitcast_fusion), channel_id=1, source_target_pairs={{0,1},{1,0},{2,3},{3,2},{4,5},{5,4},{6,7},{7,6},{8,9},{9,8},{10,11... | collective-permute-start | bytes 331784 | tf_op jit(solution)/shard_map/ppermute | solution.py:259
  32.4 3.5 %copy-start.6 = (bf16[2,144,72]{2,1,0:T(8,128)(2,1)S(1)}, bf16[2,144,72]{2,1,0:T(8,128)(2,1)}, u32[]{:S(2)}) copy-start(bf16[2,144,72]{2,1,0:T(8,128)(2,1)} %constant.77.clone.woven_ref) | copy-start | bytes 124420

commit v3 on v2

--- a/solution.py
+++ b/solution.py
@@ -20,20 +20,15 @@
 GROUP = 24
 FAR = -1e30
 LANES = 256
+TABLE = 54
+CELLS = 144
+FAR_COLUMNS = 6
 VMEM_LIMIT = 16 * 1024 * 1024
 
 norm_eps = 1e-05
 
 
 def constants():
-    column = np.arange(24)
-    place = np.arange(WLA)
-    spread = np.zeros((WLO, D, HALF), np.float32)
-    for o in range(WLO):
-        for k in column:
-            d = o - k + 17
-            if (o < HLO) == (k < WLO):
-                spread[o, place * SPAN + d, place * 24 + k] = 1
     pick = np.zeros((2, QROWS, HALF), np.float32)
     back = np.zeros((72, 2 * QROWS), np.float32)
     owned = np.zeros((QROWS, D), np.float32)
@@ -50,16 +45,39 @@
                     pick[1, row, a * 24 + HLO + o] = 1
                     back[a * WLO + o, row] = 1
                     back[(HLA + a) * WLO + o, QROWS + row] = 1
-    gaps = np.zeros((3 * GROUP, 3 * HEADS * HLA), np.float32)
-    for e in range(3 * HEADS):
-        for a in range(HLA):
-            gaps[e * 4 + a, e * HLA + a] = 1
+    gaps = np.zeros((3 * GROUP, TABLE), np.float32)
+    for e in range(3):
+        for h in range(HEADS):
+            for a in range(HLA):
+                gaps[e * GROUP + h * 4 + a, (e * HLA + a) * HEADS + h] = 1
     woven = np.zeros((2, 144, 72), np.float32)
     cell = np.arange(72)
     for at in range(2):
         woven[at, 2 * cell + at, cell] = 1
-    side = (np.arange(HALF) % 24 >= WLO).astype(np.float32).reshape(1, HALF)
-    return spread, pick, back, owned, mine, gaps, woven, side
+    bank = np.zeros((688, 768), np.float32)
+    bank[:ROWS, :HALF] = pick[0]
+    bank[:ROWS, 256 : 256 + HALF] = pick[1]
+    bank[:ROWS, 512 : 512 + D] = owned
+    bank[288:360, : 2 * QROWS] = back
+    bank[368:440, :ROWS] = mine
+    bank[368:440, 384 : 384 + TABLE] = gaps
+    bank[448:592, :72] = woven[0]
+    bank[448:592, 128:200] = woven[1]
+    return bank
+
+
+def counted(shape, dim):
+    return lax.broadcasted_iota(jnp.int32, shape, dim)
+
+
+def by_24(n):
+    quotient = (n * 2731) >> 16
+    return quotient, n - 24 * quotient
+
+
+def one_hot(target, width):
+    shape = (target.shape[0], width)
+    return halved(jnp.where(counted(shape, 1) == target, 1.0, 0.0))
 
 
 def normalized(values, gain):
@@ -104,6 +122,70 @@
     return halved(first + dot_t(hidden, fc2_t))
 
 
+def fetch_kernel(cells_ref, tables_ref, half_ref, own_ref, held_ref, sems):
+    odd = lax.axis_index("lon") % 2
+    copies = [
+        pltpu.make_async_copy(cells_ref.at[:, pl.ds(HLO * odd, HLO)], half_ref, sems.at[0]),
+        pltpu.make_async_copy(cells_ref, own_ref, sems.at[1]),
+        pltpu.make_async_copy(tables_ref, held_ref, sems.at[2]),
+    ]
+    for copy in copies:
+        copy.start()
+    for copy in copies:
+        copy.wait()
+
+
+def pack_kernel(
+    far_ref, joint_ref, tables_ref,
+    wide_ref, lower_ref, sent_far_ref, sent_near_ref,
+):
+    lev = lax.axis_index("lev")
+    lat_even = lax.axis_index("lat") % 2 == 0
+    odd = lax.axis_index("lon") % 2
+    joint = joint_ref[...].reshape(ROWS, D)
+    far = far_ref[...].reshape(2 * WLA * FAR_COLUMNS, D)
+    row = counted((ROWS, 1), 0)
+    level = (row >= HALF).astype(jnp.int32)
+    cell = row - HALF * level
+    lat_row, column = by_24(cell)
+    from_far = odd * (column - WLO - HLO) + (1 - odd) * (HLO - 1 - column) >= 0
+    near_cell = cell + HLO * (2 * odd - 1)
+    far_cell = lat_row * FAR_COLUMNS + column
+    far_cell = far_cell + (1 - odd) * (FAR_COLUMNS - HLO) - odd * (WLO + HLO)
+    near_pick = one_hot(jnp.where(from_far, -1, 2 * near_cell + level), ROWS)
+    far_pick = one_hot(jnp.where(from_far, 2 * far_cell + level, -1), 2 * WLA * FAR_COLUMNS)
+    wide = dot(near_pick, joint) + dot(far_pick, far)
+    wide_ref[...] = halved(wide)
+    head = jnp.concatenate([wide[:72], wide[HALF : HALF + 72]], axis=0)
+    tail = jnp.concatenate([wide[72:HALF], wide[HALF + 72 :]], axis=0)
+
+    tables = tables_ref[...].reshape(2 * HEADS, 4 * WLA * WLA * SPAN)
+    kinds = [dot(one_hot(2 * counted((8, 1), 0) + i, 2 * HEADS), tables) for i in range(2)]
+    width = WLA * WLA * SPAN
+    part = lambda i, at: kinds[i][:HEADS, at * width : (at + 1) * width]
+    entries = [
+        jnp.where(lev == 0, part(1, 3), part(1, 0)),
+        jnp.where(lev == 0, part(0, 0), part(0, 3)),
+        jnp.where(lev == 0, part(0, 1), part(0, 2)),
+    ]
+    span = WLA * SPAN
+    rows = [
+        jnp.concatenate(
+            [e[:, (at + a) * span : (at + a + 1) * span] for e in entries for a in range(HLA)],
+            axis=0,
+        )
+        for at in (0, HLA)
+    ]
+    lower_ref[...] = halved(rows[0])
+    blank = jnp.zeros((CELLS + TABLE, LANES), jnp.bfloat16)
+    sent_far_ref[...] = blank
+    sent_near_ref[...] = blank
+    sent_far_ref[:CELLS, :D] = halved(jnp.where(lat_even, head, tail))
+    sent_near_ref[:CELLS, :D] = halved(jnp.where(lat_even, tail, head))
+    sent_far_ref[CELLS:, :span] = halved(rows[1])
+    sent_near_ref[CELLS:, :span] = halved(rows[1])
+
+
 def early_kernel(
     wide_ref,
     before_ref,
@@ -114,13 +196,7 @@
     gain2_ref,
     fc1_ref,
     fc2_ref,
-    spread_ref,
-    pick_ref,
-    back_ref,
-    owned_ref,
-    mine_ref,
-    gaps_ref,
-    side_ref,
+    bank_ref,
     alone_ref,
     own_ref,
     asked_ref,
@@ -135,24 +211,31 @@
     w_q = qkv_ref[:, :D]
     w_k = qkv_ref[:, D : 2 * D]
     w_v = qkv_ref[:, 2 * D :]
-    owned = owned_ref[...]
-
-    gaps = gaps_ref[...]
-    cells = 2 * HLA * 24
+    owned = bank_ref[:ROWS, 512 : 512 + D]
+    picks = [bank_ref[:ROWS, :HALF], bank_ref[:ROWS, 256 : 256 + HALF]]
+    back = bank_ref[288:360, : 2 * QROWS]
+    mine = bank_ref[368:440, :ROWS]
+    gaps = bank_ref[368:440, 384 : 384 + TABLE]
+    span = WLA * SPAN
     table = halved(
         jnp.concatenate(
             [
-                dot(gaps, before_ref[cells : cells + 3 * HEADS * HLA, :D]),
-                dot(gaps, lower_ref[:, :D]),
+                dot(gaps, before_ref[CELLS:, :span]),
+                dot(gaps, lower_ref[...]),
             ],
             axis=0,
         )
     )
-    spreads = [dot(table, spread_ref[o]) for o in range(WLO)]
-    row_half = lax.broadcasted_iota(jnp.int32, (QROWS, HALF), 0) >= QROWS // 2
-    lane = lax.broadcasted_iota(jnp.int32, (QROWS, HALF), 1)
-    side = jnp.broadcast_to(side_ref[...], (QROWS, HALF)) > 0.5
-    same_side = row_half == side
+    lat_place, column = by_24(counted((span, HALF), 1))
+    offset = counted((span, HALF), 0) - (lat_place * SPAN + 17 - column)
+    sides = [jnp.where(column < WLO, offset, -1), jnp.where(column < WLO, -1, offset)]
+    spreads = []
+    for o in range(WLO):
+        chosen = jnp.where(sides[o >= HLO] == o, 1.0, 0.0)
+        spreads.append(dot(table, halved(chosen)))
+    row_half = counted((QROWS, HALF), 0) >= QROWS // 2
+    lane = counted((QROWS, HALF), 1)
+    same_side = row_half == (by_24(lane)[1] >= WLO)
     allowed = [
         same_side & ((lane >= 72) | (lat > 0)),
         same_side & ((lane < 72) | (lat < lat_last)),
@@ -171,7 +254,7 @@
         out = []
         for lat_window in range(2):
             rows = slice(lat_window * HALF, (lat_window + 1) * HALF)
-            asked = halved(dot(pick_ref[lat_window], queries[rows])) * owned
+            asked = halved(dot(picks[lat_window], queries[rows])) * owned
             out.append((asked, dot_t(asked, keys[rows]) * HEAD_DIM**-0.5, values[rows]))
         return out
 
@@ -181,16 +264,16 @@
         value_ref[lat_window] = values
         score_ref[lat_window] = scores + bias_of(lat_window, 1)
         bias_ref[lat_window] = bias_of(lat_window, 2)
-    own_ref[...] = dot(mine_ref[...], pair_cells)
+    own_ref[...] = dot(mine, pair_cells)
 
     alone_cells = wide_ref[lev]
     parts = []
     for lat_window, (asked, scores, values) in enumerate(asked_of(alone_cells)):
         parts.append(softmax_context([scores + bias_of(lat_window, 0)], [values], owned))
     alone_ref[...] = finish(
-        dot(mine_ref[...], alone_cells),
+        dot(mine, alone_cells),
         parts,
-        back_ref[...],
+        back,
         proj_ref[...],
         gain2_ref[...],
         fc1_ref[...],
@@ -212,13 +295,11 @@
     gain2_ref,
     fc1_ref,
     fc2_ref,
-    back_ref,
-    owned_ref,
-    woven_ref,
+    bank_ref,
     out_ref,
 ):
     lev = lax.axis_index("lev")
-    owned = owned_ref[...]
+    owned = bank_ref[:ROWS, 512 : 512 + D]
     n = halved(normalized(other_ref[...].astype(jnp.float32), gain1_ref[...]))
     keys = halved(dot(n, qkv_ref[:, D : 2 * D]))
     values = halved(dot(n, qkv_ref[:, 2 * D :]))
@@ -234,7 +315,7 @@
     pair = finish(
         own_ref[...],
         parts,
-        back_ref[...],
+        bank_ref[288:360, : 2 * QROWS],
         proj_ref[...],
         gain2_ref[...],
         fc1_ref[...],
@@ -243,7 +324,7 @@
     alone = alone_ref[...]
     lower = jnp.where(lev == 0, alone, pair)
     upper = jnp.where(lev == 0, pair, alone)
-    result = halved(dot(woven_ref[0], lower) + dot(woven_ref[1], upper))
+    result = halved(dot(bank_ref[448:592, :72], lower) + dot(bank_ref[448:592, 128:200], upper))
     out_ref[...] = result.reshape(72, 2, D)
 
 
@@ -269,37 +350,51 @@
     lon_even = lax.axis_index("lon") % 2 == 0
     lat_even = lat % 2 == 0
 
-    far = swapped(jnp.where(lon_even, tokens[:, :, :HLO], tokens[:, :, HLO:]), "lon", True)
+    cells_t = tokens.transpose(1, 2, 0, 3)
+    tables_t = earth_bias[:, 0].transpose(1, 0, 2)
+    params = pltpu.CompilerParams(vmem_limit_bytes=VMEM_LIMIT)
+    anywhere = pl.BlockSpec(memory_space=pltpu.HBM)
+    half_t, own_t, tables_t = pl.pallas_call(
+        fetch_kernel,
+        out_shape=[
+            pltpu.VMEM((WLA, HLO, 2, D), jnp.bfloat16),
+            pltpu.VMEM(cells_t.shape, jnp.bfloat16),
+            pltpu.VMEM(tables_t.shape, jnp.bfloat16),
+        ],
+        in_specs=[anywhere] * 2,
+        out_specs=[pl.BlockSpec(memory_space=pltpu.VMEM)] * 3,
+        scratch_shapes=[pltpu.SemaphoreType.DMA((3,))],
+        compiler_params=params,
+        name="fetch",
+    )(*[pltpu.with_memory_space_constraint(x, pltpu.HBM) for x in (cells_t, tables_t)])
+    far = swapped(half_t, "lon", True)
     joint = lax.all_gather(
-        tokens, "lon", axis_index_groups=pairs_of(lon_size, False), axis=2, tiled=True
-    )
-    wide = jnp.where(
-        lon_even,
-        jnp.concatenate([far, joint[:, :, : WLO + HLO]], axis=2),
-        jnp.concatenate([joint[:, :, HLO:], far], axis=2),
-    )
-
-    tables = earth_bias[:, 0].reshape(2, HEADS, 4, WLA, WLA * SPAN)
-    chosen = jnp.stack(
-        [
-            lax.dynamic_index_in_dim(tables[1], 3 - 3 * lev, 1, False),
-            lax.dynamic_index_in_dim(tables[0], 3 * lev, 1, False),
-            lax.dynamic_index_in_dim(tables[0], lev + 1, 1, False),
-        ]
-    )
-    chosen = jnp.pad(chosen, ((0, 0), (0, 0), (0, 0), (0, LANES - WLA * SPAN)))
-    lower = chosen[:, :, :HLA].reshape(3 * HEADS * HLA, LANES)
-    upper = chosen[:, :, HLA:].reshape(3 * HEADS * HLA, LANES)
-
-    head = wide[:, :HLA].reshape(-1, D)
-    tail = wide[:, HLA:].reshape(-1, D)
-    cells = head.shape[0]
-    to_next = jnp.concatenate([jnp.pad(tail, ((0, 0), (0, LANES - D))), upper], axis=0)
-    to_prev = jnp.pad(head, ((0, upper.shape[0]), (0, LANES - D)))
-    lat_far = swapped(jnp.where(lat_even, to_prev, to_next), "lat", True)
-    lat_both = lax.all_gather(
-        jnp.where(lat_even, to_next, to_prev), "lat", axis_index_groups=pairs_of(lat_size, False)
-    )
+        own_t, "lon", axis_index_groups=pairs_of(lon_size, False), axis=1, tiled=True
+    )
+    bank = jnp.asarray(constants(), jnp.bfloat16)
+    whole = pl.BlockSpec(memory_space=pltpu.VMEM)
+    held = lambda x: pltpu.with_memory_space_constraint(x, pltpu.VMEM)
+    sent = pltpu.VMEM((CELLS + TABLE, LANES), jnp.bfloat16)
+    wide, lower, sent_far, sent_near = pl.pallas_call(
+        pack_kernel,
+        out_shape=[
+            pltpu.VMEM((ROWS, D), jnp.bfloat16),
+            pltpu.VMEM((TABLE, WLA * SPAN), jnp.bfloat16),
+            sent,
+            sent,
+        ],
+        in_specs=[whole] * 3,
+        out_specs=[whole] * 4,
+        compiler_params=params,
+        name="pack",
+    )(
+        held(far),
+        held(joint),
+        held(tables_t),
+    )
+    cells = CELLS
+    lat_far = swapped(sent_far, "lat", True)
+    lat_both = lax.all_gather(sent_near, "lat", axis_index_groups=pairs_of(lat_size, False))
     lat_near = jnp.where(lat_even, lat_both[1], lat_both[0])
     before = jnp.where(lat_even, lat_far, lat_near)
     after = jnp.where(lat_even, lat_near, lat_far)
@@ -307,19 +402,13 @@
     extended = jnp.concatenate(
         [
             before[:cells, :D].reshape(edges),
-            wide.reshape(2, -1, D),
+            wide.reshape(2, HALF, D),
             after[:cells, :D].reshape(edges),
         ],
         axis=1,
     )
     other = swapped(lax.dynamic_index_in_dim(extended, 1 - lev, 0, False), "lev", False)
 
-    spread, pick, back, owned, mine, gaps, woven = [
-        jnp.asarray(a, jnp.bfloat16) for a in constants()[:-1]
-    ]
-    side = jnp.asarray(constants()[-1])
-    whole = pl.BlockSpec(memory_space=pltpu.VMEM)
-    held = lambda x: pltpu.with_memory_space_constraint(x, pltpu.VMEM)
     shared = [
         held(a)
         for a in (
@@ -331,8 +420,7 @@
             fc2_weight.T,
         )
     ]
-    back = held(back)
-    owned = held(owned)
+    bank = held(bank)
     passed = [
         pltpu.VMEM((72, D), jnp.bfloat16),
         pltpu.VMEM((72, D), jnp.float32),
@@ -344,32 +432,26 @@
     early = pl.pallas_call(
         early_kernel,
         out_shape=passed,
-        in_specs=[whole] * 16,
+        in_specs=[whole] * 10,
         out_specs=[whole] * 6,
         cost_estimate=pl.CostEstimate(flops=4_000_000_000, transcendentals=0, bytes_accessed=0),
-        compiler_params=pltpu.CompilerParams(vmem_limit_bytes=VMEM_LIMIT),
+        compiler_params=params,
         name="early",
     )(
         held(extended),
         held(before),
         held(lower),
         *shared,
-        held(spread),
-        held(pick),
-        back,
-        owned,
-        held(mine),
-        held(gaps),
-        held(side),
+        bank,
     )
     result = pl.pallas_call(
         late_kernel,
         out_shape=jax.ShapeDtypeStruct((72, 2, D), jnp.bfloat16),
-        in_specs=[whole] * 16,
+        in_specs=[whole] * 14,
         out_specs=whole,
-        compiler_params=pltpu.CompilerParams(vmem_limit_bytes=VMEM_LIMIT),
+        compiler_params=params,
         name="late",
-    )(held(other), *[held(x) for x in early], *shared, back, owned, held(woven))
+    )(held(other), *[held(x) for x in early], *shared, bank)
     return result.reshape(WLA, WLO, 2, D).transpose(2, 0, 1, 3)
 
 

time: 39 us -> 36.6 us (0.938)
  local copies, waits for them, and re-layouts: 2.29 us -> 0.07 us
  Pallas kernels: 5.32 us -> 6.93 us
  other arithmetic: 1.32 us -> 0.07 us
    slice x6 -> x0, local copies, waits for them, and re-layouts: 1.61 us -> none  [the longest x1 1.32 us: per_device(): tables[1]]
    pallas_call x1 -> x3, Pallas kernels: 2.5 us -> 4.08 us  [the longest x1 2.48 us: per_device(): pl.pallas_call(early_kernel, out_shape=passed, in_specs=[whole] * 10, out...]
    select_n x2 -> x0, other arithmetic: 1.16 us -> none  [the longest x1 0.83 us: per_device(): jnp.where(lon_even, tokens[:, :, :HLO], tokens[:, :, HLO:])]
    squeeze x2 -> x0, local copies, waits for them, and re-layouts: 0.45 us -> none  [the longest x1 0.23 us: per_device(): tables[0]]
  transfers between devices with their start and end apart: 3 -> 3, of which waited for: 1 -> 1; matrix products, arithmetic and copies ran while one was open for 5% -> 0% of each run, Pallas kernels for 6% -> 7%
where the time goes in v3:
time: 36.6 us; the launch traced here: 36.4 us
  starting transfers between devices  20.7 us (57%)
  blocking collectives  7.37 us (20%)
  Pallas kernels  6.93 us (19%)
  waiting for transfers between devices  1 us (3%)
    ppermute x3, starting transfers between devices, swapped(): return lax.ppermute(block, axis, route)  20.7 us
    all_gather x1, blocking collectives, per_device(): lax.all_gather(sent_near, 'lat', axis_index_groups=pairs_of(lat_size, Fal...  5.46 us
    pallas_call x1, Pallas kernels, per_device(): pl.pallas_call(late_kernel, out_shape=jax.ShapeDtypeStruct((72, 2, D), jn...  2.84 us
    pallas_call x1, Pallas kernels, per_device(): pl.pallas_call(early_kernel, out_shape=passed, in_specs=[whole] * 10, out...  2.48 us
    all_gather x1, blocking collectives, per_device(): lax.all_gather(own_t, 'lon', axis_index_groups=pairs_of(lon_size, False),...  1.91 us
    ppermute x3, waiting for transfers between devices, swapped(): return lax.ppermute(block, axis, route)  1 us
    pallas_call x1, Pallas kernels, per_device(): pl.pallas_call(fetch_kernel, out_shape=[pltpu.VMEM((WLA, HLO, 2, D), jnp....  0.99 us
  transfers between devices with their start and end apart: 3, of which 1 were waited for; matrix products, arithmetic and copies ran while one was open for 0% of the time, Pallas kernels for 7%

profile of v3, /device:TPU:24, one launch (start us, length us, event | category | flops | bytes accessed | tf_op | source)
XLA Modules:
  0.0 36.4 jit_solution(15572568814911784477)
XLA Ops:
  0.0 1.0 %fetch.1 = (bf16[6,6,2,192]{3,2,1,0:T(2,128)(2,1)S(1)}, bf16[6,12,2,192]{3,2,1,0:T(2,128)(2,1)S(1)}, bf16[6,2,3312]{2,1,0:T(2,128)(2,1)S(1)}) custom-call(bf16[6,12,2,192]{3,2,1,0:T(2,128)(2,1)} %bitcast.30, bf16[6,2,3312]{2,1,0:T(2,128)(2,1)} %bitcast.29), custom_call_target="tpu_custom_call" | custom-call | tf_op jit(solution)/shard_map/fetch/pallas_call | solution.py:357
  1.0 12.6 %collective-permute-start = (bf16[6,6,2,192]{3,2,1,0:T(2,128)(2,1)S(1)}, bf16[6,6,2,192]{3,2,1,0:T(2,128)(2,1)S(1)}, u32[]{:S(2)}, u32[]{:S(2)}) collective-permute-start(bf16[6,6,2,192]{3,2,1,0:T(2,128)(2,1)S(1)} %get-tuple-element.18), channel_id=1, source_target_pairs={{2,4},{4,2},{6,8},{8,6},{10,12},{12,10},{14,16},{16,14},{18,20},{2... | collective-permute-start | bytes 82952 | tf_op jit(solution)/shard_map/ppermute | solution.py:340
  13.6 1.9 %all_gather.9.joint_ref = bf16[6,24,2,192]{3,2,1,0:T(2,128)(2,1)S(1)} all-gather(bf16[6,12,2,192]{3,2,1,0:T(2,128)(2,1)S(1)} %get-tuple-element.19), channel_id=1, replica_groups={{0,2},{4,6},{8,10},{12,14},{16,18},{20,22},{24,26},{28,30},{32,34},{36,..., dimensions={1}, use_global_device_ids=true | all-gather | bytes 165888 | tf_op jit(solution)/shard_map/all_gather | solution.py:371
  15.5 0.0 collective-permute-done.far_ref
  15.5 0.6 %pack.1 = (bf16[288,192]{1,0:T(8,128)(2,1)S(1)}, bf16[54,138]{1,0:T(8,128)(2,1)S(1)}, bf16[198,256]{1,0:T(8,128)(2,1)S(1)}, bf16[198,256]{1,0:T(8,128)(2,1)S(1)}) custom-call(bf16[6,6,2,192]{3,2,1,0:T(2,128)(2,1)S(1)} %collective-permute-done.far_ref, bf16[6,24,2,192]{3,2,1,0:T(2,128)(2,1)S(1)} %all_gather.9.joint_ref, ...), custom_call_target="tpu_custom_call" | custom-call | tf_op jit(solution)/shard_map/pack/pallas_call | solution.py:378
  16.1 4.7 %collective-permute-start.1 = (bf16[198,256]{1,0:T(8,128)(2,1)S(1)}, bf16[198,256]{1,0:T(8,128)(2,1)S(1)}, u32[]{:S(2)}, u32[]{:S(2)}) collective-permute-start(bf16[198,256]{1,0:T(8,128)(2,1)S(1)} %get-tuple-element.21), channel_id=1, source_target_pairs={{64,128},{128,64},{192,256},{256,192},{320,384},{384,320},{448,0},... | collective-permute-start | bytes 304136 | tf_op jit(solution)/shard_map/ppermute | solution.py:340
  20.8 0.0 copy-start
  20.8 0.0 copy-start.1
  20.8 0.0 copy-start.2
  20.9 0.0 copy-start.3
  20.9 0.0 copy-start.4
  20.9 0.0 copy-start.5
  20.9 0.0 copy-start.6
  20.9 5.5 %all-gather.1 = bf16[2,198,256]{2,1,0:T(8,128)(2,1)S(1)} all-gather(bf16[1,198,256]{2,1,0:T(8,128)(2,1)S(1)} %bitcast.22), channel_id=2, replica_groups={{0,64},{128,192},{256,320},{384,448},{1,65},{129,193},{257,321},{385,44..., dimensions={0}, use_global_device_ids=true | all-gather | bytes 304128 | tf_op jit(solution)/shard_map/all_gather | solution.py:397
  26.4 0.0 collective-permute-done.1
  26.5 3.5 %collective-permute-start.2 = (bf16[288,192]{1,0:T(8,128)(2,1)S(1)}, bf16[288,192]{1,0:T(8,128)(2,1)S(1)}, u32[]{:S(2)}, u32[]{:S(2)}) collective-permute-start(bf16[288,192]{1,0:T(8,128)(2,1)S(1)} %dynamic-slice_bitcast_fusion), channel_id=1, source_target_pairs={{0,1},{1,0},{2,3},{3,2},{4,5},{5,4},{6,7},{7,6},{8,9},{9,8},{10,11... | collective-permute-start | bytes 331784 | tf_op jit(solution)/shard_map/ppermute | solution.py:340
  30.0 0.0 copy-done
  30.0 0.0 copy-done.1
  30.0 0.0 copy-done.2
  30.0 0.0 copy-done.3
  30.0 0.0 copy-done.4
  30.0 0.0 copy-done.5
  30.1 0.0 copy-done.6
  30.1 2.5 %early.1 = (bf16[72,192]{1,0:T(8,128)(2,1)S(1)}, f32[72,192]{1,0:T(8,128)S(1)}, bf16[2,288,192]{2,1,0:T(8,128)(2,1)S(1)}, bf16[2,144,192]{2,1,0:T(8,128)(2,1)S(1...) custom-call(bf16[2,288,192]{2,1,0:T(8,128)(2,1)S(1)} %pad_maximum_fusion.wide_ref, ...), custom_call_target="tpu_custom_call" | custom-call | flops 4000000000 | tf_op jit(solution)/shard_map/early/pallas_call | solution.py:432
  32.6 1.0 %collective-permute-done.2.other_ref = bf16[288,192]{1,0:T(8,128)(2,1)S(1)} collective-permute-done((bf16[288,192]{1,0:T(8,128)(2,1)S(1)}, bf16[288,192]{1,0:T(8,128)(2,1)S(1)}, u32[]{:S(2)}, u32[]{:S(2)}) %collective-permute-start.2) | collective-permute-done | bytes 110624 | tf_op jit(solution)/shard_map/ppermute | solution.py:340
  33.6 2.8 %late.1 = bf16[72,2,192]{2,1,0:T(2,128)(2,1)} custom-call(bf16[288,192]{1,0:T(8,128)(2,1)S(1)} %collective-permute-done.2.other_ref, bf16[72,192]{1,0:T(8,128)(2,1)S(1)} %get-tuple-element.25.alone_ref, f32[72,192]{1,0:T(8,128)S(1)} %get-tuple-element.26.own_ref, bf16[2,288,192]{2,1,0:T(8,128)(2,1)S(1)} %get-tuple-element.27.asked_ref, ...), custom_call_target="tpu_custom_call" | custom-call | tf_op jit(solution)/shard_map/late/pallas_call | solution.py:447
  (5 shorter events, 0.1 us)
Async XLA Ops:
  1.0 14.5 %collective-permute-start = (bf16[6,6,2,192]{3,2,1,0:T(2,128)(2,1)S(1)}, bf16[6,6,2,192]{3,2,1,0:T(2,128)(2,1)S(1)}, u32[]{:S(2)}, u32[]{:S(2)}) collective-permute-start(bf16[6,6,2,192]{3,2,1,0:T(2,128)(2,1)S(1)} %get-tuple-element.18), channel_id=1, source_target_pairs={{2,4},{4,2},{6,8},{8,6},{10,12},{12,10},{14,16},{16,14},{18,20},{2... | collective-permute-start | bytes 82952 | tf_op jit(solution)/shard_map/ppermute | solution.py:340
  16.1 10.3 %collective-permute-start.1 = (bf16[198,256]{1,0:T(8,128)(2,1)S(1)}, bf16[198,256]{1,0:T(8,128)(2,1)S(1)}, u32[]{:S(2)}, u32[]{:S(2)}) collective-permute-start(bf16[198,256]{1,0:T(8,128)(2,1)S(1)} %get-tuple-element.21), channel_id=1, source_target_pairs={{64,128},{128,64},{192,256},{256,192},{320,384},{384,320},{448,0},... | collective-permute-start | bytes 304136 | tf_op jit(solution)/shard_map/ppermute | solution.py:340
  20.8 9.2 %copy-start = (bf16[688,768]{1,0:T(8,128)(2,1)S(1)}, bf16[688,768]{1,0:T(8,128)(2,1)}, u32[]{:S(2)}) copy-start(bf16[688,768]{1,0:T(8,128)(2,1)} %constant.33.clone.bank_ref) | copy-start | bytes 3170308
  20.8 9.2 %copy-start.1 = (bf16[192,768]{1,0:T(8,128)(2,1)S(1)}, bf16[192,768]{1,0:T(8,128)(2,1)}, u32[]{:S(2)}) copy-start(bf16[192,768]{1,0:T(8,128)(2,1)} %fc1_ref.3) | copy-start | bytes 884740
  20.8 9.2 %copy-start.2 = (bf16[768,192]{0,1:T(8,128)(2,1)S(1)}, bf16[768,192]{0,1:T(8,128)(2,1)}, u32[]{:S(2)}) copy-start(bf16[768,192]{0,1:T(8,128)(2,1)} %param.16) | copy-start | bytes 884740
  20.9 9.2 %copy-start.3 = (bf16[192,576]{1,0:T(8,128)(2,1)S(1)}, bf16[192,576]{1,0:T(8,128)(2,1)}, u32[]{:S(2)}) copy-start(bf16[192,576]{1,0:T(8,128)(2,1)} %qkv_ref.3) | copy-start | bytes 663556
  20.9 9.2 %copy-start.4 = (bf16[192,192]{1,0:T(8,128)(2,1)S(1)}, bf16[192,192]{1,0:T(8,128)(2,1)}, u32[]{:S(2)}) copy-start(bf16[192,192]{1,0:T(8,128)(2,1)} %proj_ref.3) | copy-start | bytes 221188
  20.9 9.2 %copy-start.5 = (f32[192]{0:T(256)S(1)}, f32[192]{0:T(256)}, u32[]{:S(2)}) copy-start(f32[192]{0:T(256)} %param.10) | copy-start | bytes 2308
  20.9 9.2 %copy-start.6 = (f32[192]{0:T(256)S(1)}, f32[192]{0:T(256)}, u32[]{:S(2)}) copy-start(f32[192]{0:T(256)} %param.14) | copy-start | bytes 2308
  26.5 7.0 %collective-permute-start.2 = (bf16[288,192]{1,0:T(8,128)(2,1)S(1)}, bf16[288,192]{1,0:T(8,128)(2,1)S(1)}, u32[]{:S(2)}, u32[]{:S(2)}) collective-permute-start(bf16[288,192]{1,0:T(8,128)(2,1)S(1)} %dynamic-slice_bitcast_fusion), channel_id=1, source_target_pairs={{0,1},{1,0},{2,3},{3,2},{4,5},{5,4},{6,7},{7,6},{8,9},{9,8},{10,11... | collective-permute-start | bytes 331784 | tf_op jit(solution)/shard_map/ppermute | solution.py:340

commit v4 on v3

v4 whole, which is shorter than its diff:
```python
import jax
import jax.numpy as jnp
from jax import lax
from jax.experimental import pallas as pl
from jax.experimental.pallas import tpu as pltpu
from jax.sharding import PartitionSpec as P

D = 192
HEADS = 6
HEAD_DIM = 32
WLA = 6
WLO = 12
HLA = 3
HLO = 6
SPAN = 2 * WLO - 1
ROWS = 288
HALF = 144
QROWS = 216
GROUP = 18
FAR = -1e30
LANES = 256
TABLE = 54
CELLS = 144
FAR_COLUMNS = 6
VMEM_LIMIT = 16 * 1024 * 1024

norm_eps = 1e-05


def counted(shape, dim):
    return lax.broadcasted_iota(jnp.int32, shape, dim)


def by_24(n):
    quotient = (n * 2731) >> 16
    return quotient, n - 24 * quotient


def by_18(n):
    quotient = (n * 3641) >> 16
    return quotient, n - 18 * quotient


def by_3(n):
    quotient = (n * 21846) >> 16
    return quotient, n - 3 * quotient


def one_hot(target, width):
    shape = (target.shape[0], width)
    return halved(jnp.where(counted(shape, 1) == target, 1.0, 0.0))


def normalized(values, gain):
    average = jnp.mean(values, axis=-1, keepdims=True)
    centered = values - average
    variance = jnp.mean(centered * centered, axis=-1, keepdims=True)
    return centered * lax.rsqrt(variance + norm_eps) * gain


def dot(a, b):
    return jnp.dot(a, b, preferred_element_type=jnp.float32)


def dot_t(a, b):
    return lax.dot_general(a, b, (((1,), (1,)), ((), ())), preferred_element_type=jnp.float32)


def halved(x):
    return x.astype(jnp.bfloat16)


def softmax_context(scores, values, owned):
    top = jnp.max(scores[0], axis=-1, keepdims=True)
    for s in scores[1:]:
        top = jnp.maximum(top, jnp.max(s, axis=-1, keepdims=True))
    weights = [jnp.exp(s - top) for s in scores]
    total = jnp.sum(weights[0], axis=-1, keepdims=True)
    for w in weights[1:]:
        total = total + jnp.sum(w, axis=-1, keepdims=True)
    inverse = 1.0 / total
    context = 0.0
    for w, v in zip(weights, values):
        context = context + dot(halved(w * inverse), v)
    return halved(context) * owned


def finish(own, parts, back, proj, gain, fc1, fc2_t):
    context = halved(dot(back[0], parts[0]) + dot(back[1], parts[1]))
    first = own + dot(context, proj)
    mixed = dot(halved(normalized(first, gain)), fc1)
    hidden = halved(mixed * (1.0 + lax.erf(mixed * (0.5**0.5))) * 0.5)
    return halved(first + dot_t(hidden, fc2_t))


def fetch_kernel(
    cells_ref, tables_ref, gain1_ref, gain2_ref,
    half_ref, own_ref, rows_ref, held_ref, gain2_held, raw_ref, gain1_held, sems,
):
    odd = lax.axis_index("lon") % 2
    copies = [
        pltpu.make_async_copy(gain1_ref, gain1_held, sems.at[0]),
        pltpu.make_async_copy(cells_ref, raw_ref, sems.at[1]),
        pltpu.make_async_copy(tables_ref, held_ref, sems.at[2]),
        pltpu.make_async_copy(gain2_ref, gain2_held, sems.at[3]),
    ]
    for copy in copies:
        copy.start()
    copies[0].wait()
    copies[1].wait()
    rows = raw_ref[...].reshape(CELLS, D)
    rows_ref[...] = rows
    cells = rows.astype(jnp.float32)
    own_ref[...] = halved(normalized(cells, gain1_held[...])).reshape(raw_ref.shape)
    half_ref[...] = own_ref[:, pl.ds(HLO * odd, HLO)]
    copies[2].wait()
    copies[3].wait()


def pack_kernel(
    far_ref, joint_ref, tables_ref,
    wide_ref, lower_ref, sent_far_ref, sent_near_ref,
):
    lev = lax.axis_index("lev")
    lat_even = lax.axis_index("lat") % 2 == 0
    odd = lax.axis_index("lon") % 2
    joint = joint_ref[...].reshape(ROWS, D)
    far = far_ref[...].reshape(2 * WLA * FAR_COLUMNS, D)
    row = counted((ROWS, 1), 0)
    level = (row >= HALF).astype(jnp.int32)
    cell = row - HALF * level
    lat_row, column = by_24(cell)
    from_far = odd * (column - WLO - HLO) + (1 - odd) * (HLO - 1 - column) >= 0
    near_cell = cell + HLO * (2 * odd - 1)
    far_cell = lat_row * FAR_COLUMNS + column
    far_cell = far_cell + (1 - odd) * (FAR_COLUMNS - HLO) - odd * (WLO + HLO)
    near_pick = one_hot(jnp.where(from_far, -1, 2 * near_cell + level), ROWS)
    far_pick = one_hot(jnp.where(from_far, 2 * far_cell + level, -1), 2 * WLA * FAR_COLUMNS)
    wide = dot(near_pick, joint) + dot(far_pick, far)
    wide_ref[...] = halved(wide)
    head = jnp.concatenate([wide[:72], wide[HALF : HALF + 72]], axis=0)
    tail = jnp.concatenate([wide[72:HALF], wide[HALF + 72 :]], axis=0)

    tables = tables_ref[...].reshape(2 * HEADS, 4 * WLA * WLA * SPAN)
    kinds = [dot(one_hot(2 * counted((8, 1), 0) + i, 2 * HEADS), tables) for i in range(2)]
    width = WLA * WLA * SPAN
    part = lambda i, at: kinds[i][:HEADS, at * width : (at + 1) * width]
    entries = [
        jnp.where(lev == 0, part(1, 3), part(1, 0)),
        jnp.where(lev == 0, part(0, 0), part(0, 3)),
        jnp.where(lev == 0, part(0, 1), part(0, 2)),
    ]
    span = WLA * SPAN
    rows = [
        jnp.concatenate(
            [e[:, (at + a) * span : (at + a + 1) * span] for e in entries for a in range(HLA)],
            axis=0,
        )
        for at in (0, HLA)
    ]
    lower_ref[...] = halved(rows[0])
    blank = jnp.zeros((CELLS + TABLE, LANES), jnp.bfloat16)
    sent_far_ref[...] = blank
    sent_near_ref[...] = blank
    sent_far_ref[:CELLS, :D] = halved(jnp.where(lat_even, head, tail))
    sent_near_ref[:CELLS, :D] = halved(jnp.where(lat_even, tail, head))
    sent_far_ref[CELLS:, :span] = halved(rows[1])
    sent_near_ref[CELLS:, :span] = halved(rows[1])


def assemble_kernel(
    far_ref, both_ref, wide_ref, alone_ref, pair_ref, table_ref, sent_ref
):
    lev = lax.axis_index("lev")
    lat_odd = lax.axis_index("lat") % 2
    near = both_ref[1 - lat_odd].astype(jnp.float32)
    far = far_ref[...].astype(jnp.float32)
    wide = wide_ref[...].astype(jnp.float32)
    before = jnp.where(lat_odd == 0, far, near)
    after = jnp.where(lat_odd == 0, near, far)
    levels = [
        jnp.concatenate(
            [
                before[l * 72 : (l + 1) * 72, :D],
                wide[l * HALF : (l + 1) * HALF],
                after[l * 72 : (l + 1) * 72, :D],
            ],
            axis=0,
        )
        for l in range(2)
    ]
    pair = jnp.where(lev == 0, levels[1], levels[0])
    pair_ref[...] = halved(pair)
    first = pair[:HALF]
    second = pair[HALF:]
    sent_ref[:HALF] = halved(jnp.concatenate([first, second[:, : LANES - D]], axis=1))
    rest = second[:, LANES - D :]
    sent_ref[HALF:] = halved(jnp.concatenate([rest[:72], rest[72:]], axis=1))
    alone_ref[...] = halved(jnp.where(lev == 0, levels[0], levels[1]))
    table_ref[...] = halved(before[CELLS:, : WLA * SPAN])


def packed_dots(packed, weight):
    spare = jnp.zeros((LANES - D, weight.shape[1]), weight.dtype)
    first = dot(packed[:HALF], jnp.concatenate([weight, spare], axis=0))
    low = jnp.concatenate([spare, weight[: LANES - D]], axis=0)
    second = dot(packed[:HALF, LANES // 2 :], low)
    high = weight[LANES - D :]
    rest = [dot(packed[HALF:, : LANES // 2], high), dot(packed[HALF:, LANES // 2 :], high)]
    return halved(first), halved(second + jnp.concatenate(rest, axis=0))


def early_kernel(
    alone_cells_ref,
    pair_cells_ref,
    raw_ref,
    upper_ref,
    lower_ref,
    qkv_ref,
    proj_ref,
    fc1_ref,
    fc2_ref,
    gain2_ref,
    alone_ref,
    own_ref,
    asked_ref,
    value_ref,
    score_ref,
    bias_ref,
    owned_ref,
    back_ref,
    woven_ref,
):
    lev = lax.axis_index("lev")
    lat = lax.axis_index("lat")
    lat_last = lax.axis_size("lat") - 1
    column, spot = by_18(counted((QROWS, 1), 0))
    head, place = by_3(spot)
    picks = [one_hot((at + place) * 24 + HLO + column, HALF) for at in (HLA, 0)]
    owned = halved(jnp.where(counted((QROWS, D), 1) >> 5 == head, 1.0, 0.0))
    owned_ref[...] = owned
    column, spot = by_18(counted((1, QROWS), 1))
    source = by_3(spot)[1] * WLO + column
    cell = counted((72, QROWS), 0)
    back = [halved(jnp.where(cell == source + at * WLO, 1.0, 0.0)) for at in (0, HLA)]
    for at in range(2):
        back_ref[at] = back[at]
    raw = raw_ref[...]
    cell = 2 * counted((72, 1), 0)
    own_ref[...] = dot(one_hot(cell + 1 - lev, CELLS), raw)
    alone_own = dot(one_hot(cell + lev, CELLS), raw)
    woven_row = counted((CELLS, 72), 0) - 2 * counted((CELLS, 72), 1)
    woven_ref[...] = halved(jnp.where(woven_row == 1 - lev, 1.0, 0.0))
    entry, spot = by_18(counted((3 * GROUP, 1), 0))
    head, place = by_3(spot)
    gaps = one_hot((entry * HLA + place) * HEADS + head, TABLE)
    span = WLA * SPAN
    tables = [halved(dot(gaps, ref[...])) for ref in (upper_ref, lower_ref)]
    lat_place, column = by_24(counted((span, HALF), 1))
    offset = counted((span, HALF), 0) - (lat_place * SPAN + 17 - column)
    sides = [jnp.where(column < WLO, offset, -1), jnp.where(column < WLO, -1, offset)]
    spreads = []
    for o in range(WLO):
        chosen = jnp.where(sides[o >= HLO] == o, 1.0, 0.0)
        spreads.append([dot(table, halved(chosen)) for table in tables])
    row_half = counted((QROWS, HALF), 0) >= QROWS // 2
    lane = counted((QROWS, HALF), 1)
    same_side = row_half == (by_24(lane)[1] >= WLO)
    allowed = [
        same_side & ((lane >= 72) | (lat > 0)),
        same_side & ((lane < 72) | (lat < lat_last)),
    ]

    def bias_of(lat_window, entry):
        at = entry * GROUP
        terms = jnp.concatenate([s[lat_window][at : at + GROUP] for s in spreads], axis=0)
        return jnp.where(allowed[lat_window], terms, FAR)

    w_q = qkv_ref[:, :D]
    w_k = qkv_ref[:, D : 2 * D]
    w_v = qkv_ref[:, 2 * D :]

    def asked_of(n):
        queries = halved(dot(n, w_q))
        keys = halved(dot(n, w_k))
        values = halved(dot(n, w_v))
        out = []
        for lat_window in range(2):
            rows = slice(lat_window * HALF, (lat_window + 1) * HALF)
            asked = halved(dot(picks[lat_window], queries[rows])) * owned
            out.append((asked, dot_t(asked, keys[rows]) * HEAD_DIM**-0.5, values[rows]))
        return out

    for lat_window, (asked, scores, values) in enumerate(asked_of(pair_cells_ref[...])):
        asked_ref[lat_window] = asked
        value_ref[lat_window] = values
        score_ref[lat_window] = scores + bias_of(lat_window, 1)
        bias_ref[lat_window] = bias_of(lat_window, 2)

    parts = []
    for lat_window, (asked, scores, values) in enumerate(asked_of(alone_cells_ref[...])):
        parts.append(softmax_context([scores + bias_of(lat_window, 0)], [values], owned))
    alone = finish(
        alone_own,
        parts,
        back,
        proj_ref[...],
        gain2_ref[...],
        fc1_ref[...],
        fc2_ref[...],
    )
    alone_ref[...] = dot(halved(jnp.where(woven_row == lev, 1.0, 0.0)), alone)


def late_kernel(
    other_ref,
    alone_ref,
    own_ref,
    asked_ref,
    value_ref,
    score_ref,
    bias_ref,
    owned_ref,
    back_ref,
    woven_ref,
    qkv_ref,
    proj_ref,
    fc1_ref,
    fc2_ref,
    gain2_ref,
    out_ref,
):
    owned = owned_ref[...]
    packed = other_ref[...]
    keys = packed_dots(packed, qkv_ref[:, D : 2 * D])
    values = packed_dots(packed, qkv_ref[:, 2 * D :])
    parts = []
    for lat_window in range(2):
        scores = dot_t(asked_ref[lat_window], keys[lat_window]) * HEAD_DIM**-0.5 + bias_ref[lat_window]
        parts.append(
            softmax_context(
                [score_ref[lat_window], scores], [value_ref[lat_window], values[lat_window]], owned
            )
        )
    pair = finish(
        own_ref[...],
        parts,
        (back_ref[0], back_ref[1]),
        proj_ref[...],
        gain2_ref[...],
        fc1_ref[...],
        fc2_ref[...],
    )
    result = halved(alone_ref[...] + dot(woven_ref[...], pair))
    out_ref[...] = result.reshape(72, 2, D)


def pairs_of(size, crossed):
    shift = 1 if crossed else 0
    return [[(2 * i + shift) % size, (2 * i + 1 + shift) % size] for i in range(size // 2)]


def swapped(block, axis, crossed):
    route = []
    for a, b in pairs_of(lax.axis_size(axis), crossed):
        route += [(a, b), (b, a)]
    return lax.ppermute(block, axis, route)


def per_device(
    tokens, norm1_gain, qkv_weight, proj_weight, earth_bias, norm2_gain, fc1_weight, fc2_weight
):
    lon_size = lax.axis_size("lon")
    lat_size = lax.axis_size("lat")

    cells_t = tokens.transpose(1, 2, 0, 3)
    tables_t = earth_bias[:, 0].transpose(1, 0, 2)
    params = pltpu.CompilerParams(vmem_limit_bytes=VMEM_LIMIT)
    anywhere = pl.BlockSpec(memory_space=pltpu.HBM)
    half_t, own_t, raw_t, tables_t, gain2 = pl.pallas_call(
        fetch_kernel,
        out_shape=[
            pltpu.VMEM((WLA, HLO, 2, D), jnp.bfloat16),
            pltpu.VMEM(cells_t.shape, jnp.bfloat16),
            pltpu.VMEM((CELLS, D), jnp.bfloat16),
            pltpu.VMEM(tables_t.shape, jnp.bfloat16),
            pltpu.VMEM((1, D), jnp.float32),
        ],
        in_specs=[anywhere] * 4,
        out_specs=[pl.BlockSpec(memory_space=pltpu.VMEM)] * 5,
        scratch_shapes=[
            pltpu.VMEM(cells_t.shape, jnp.bfloat16),
            pltpu.VMEM((1, D), jnp.float32),
            pltpu.SemaphoreType.DMA((4,)),
        ],
        compiler_params=params,
        name="fetch",
    )(
        *[
            pltpu.with_memory_space_constraint(x, pltpu.HBM)
            for x in (
                cells_t,
                tables_t,
                norm1_gain.reshape(1, D),
                norm2_gain.reshape(1, D),
            )
        ]
    )
    far = swapped(half_t, "lon", True)
    joint = lax.all_gather(
        own_t, "lon", axis_index_groups=pairs_of(lon_size, False), axis=1, tiled=True
    )
    whole = pl.BlockSpec(memory_space=pltpu.VMEM)
    placed = pltpu.with_memory_space_constraint
    held = lambda x: placed(x, pltpu.VMEM)
    sent = pltpu.VMEM((CELLS + TABLE, LANES), jnp.bfloat16)
    wide, lower, sent_far, sent_near = pl.pallas_call(
        pack_kernel,
        out_shape=[
            pltpu.VMEM((ROWS, D), jnp.bfloat16),
            pltpu.VMEM((TABLE, WLA * SPAN), jnp.bfloat16),
            sent,
            sent,
        ],
        in_specs=[whole] * 3,
        out_specs=[whole] * 4,
        compiler_params=params,
        name="pack",
    )(
        held(far),
        held(joint),
        held(tables_t),
    )
    lat_far = swapped(sent_far, "lat", True)
    lat_both = lax.all_gather(sent_near, "lat", axis_index_groups=pairs_of(lat_size, False))
    level = pltpu.VMEM((ROWS, D), jnp.bfloat16)
    alone_cells, pair_cells, upper, sent = pl.pallas_call(
        assemble_kernel,
        out_shape=[
            level,
            level,
            pltpu.VMEM((TABLE, WLA * SPAN), jnp.bfloat16),
            pltpu.VMEM((HALF + 72, LANES), jnp.bfloat16),
        ],
        in_specs=[whole] * 3,
        out_specs=[whole] * 4,
        compiler_params=params,
        name="assemble",
    )(held(lat_far), held(lat_both), wide)
    other = swapped(sent, "lev", False)

    shared = (
        qkv_weight,
        proj_weight,
        fc1_weight,
        fc2_weight.T,
        gain2,
    )
    passed = [
        pltpu.VMEM((CELLS, D), jnp.float32),
        pltpu.VMEM((72, D), jnp.float32),
        pltpu.VMEM((2, QROWS, D), jnp.bfloat16),
        pltpu.VMEM((2, HALF, D), jnp.bfloat16),
        pltpu.VMEM((2, QROWS, HALF), jnp.float32),
        pltpu.VMEM((2, QROWS, HALF), jnp.float32),
        pltpu.VMEM((QROWS, D), jnp.bfloat16),
        pltpu.VMEM((2, 72, QROWS), jnp.bfloat16),
        pltpu.VMEM((CELLS, 72), jnp.bfloat16),
    ]
    shared = [held(x) for x in shared]
    early = pl.pallas_call(
        early_kernel,
        out_shape=passed,
        in_specs=[whole] * (5 + len(shared)),
        out_specs=[whole] * len(passed),
        cost_estimate=pl.CostEstimate(flops=4_000_000_000, transcendentals=0, bytes_accessed=0),
        compiler_params=params,
        name="early",
    )(alone_cells, pair_cells, raw_t, upper, lower, *shared)
    result = pl.pallas_call(
        late_kernel,
        out_shape=jax.ShapeDtypeStruct((72, 2, D), jnp.bfloat16),
        in_specs=[whole] * 15,
        out_specs=whole,
        compiler_params=params,
        name="late",
    )(held(other), *early, *shared)
    return result.reshape(WLA, WLO, 2, D).transpose(2, 0, 1, 3)


def solution(mesh):
    placed = (
        P("lev", "lat", "lon", None),
        P(),
        P(),
        P(),
        P(None, "lat", None, None),
        P(),
        P(),
        P(),
    )
    return jax.shard_map(
        per_device,
        mesh=mesh,
        in_specs=placed,
        out_specs=P("lev", "lat", "lon", None),
        check_vma=False,
    )
```

time: 36.6 us -> 36.4 us (level)
  waiting for transfers between devices: 1 us -> 0.5 us
  Pallas kernels: 6.93 us -> 7.38 us
    ppermute x3, waiting for transfers between devices: 1 us -> 0.5 us  [swapped(): return lax.ppermute(block, axis, route)]
    pallas_call x1 -> x2, Pallas kernels: 2.48 us -> 2.74 us  [the longest x1 2.61 us: per_device(): pl.pallas_call(early_kernel, out_shape=passed, in_specs=[whole] * (5 + le...]
where the time goes in v4:
time: 36.4 us; the launch traced here: 36.1 us
  starting transfers between devices  20.7 us (57%)
  Pallas kernels  7.38 us (20%)
  blocking collectives  7.37 us (20%)
  waiting for transfers between devices  0.5 us (1%)
    ppermute x3, starting transfers between devices, swapped(): return lax.ppermute(block, axis, route)  20.7 us
    all_gather x1, blocking collectives, per_device(): lax.all_gather(sent_near, 'lat', axis_index_groups=pairs_of(lat_size, Fal...  5.46 us
    pallas_call x1, Pallas kernels, per_device(): pl.pallas_call(late_kernel, out_shape=jax.ShapeDtypeStruct((72, 2, D), jn...  2.81 us
    pallas_call x1, Pallas kernels, per_device(): pl.pallas_call(early_kernel, out_shape=passed, in_specs=[whole] * (5 + le...  2.61 us
    all_gather x1, blocking collectives, per_device(): lax.all_gather(own_t, 'lon', axis_index_groups=pairs_of(lon_size, False),...  1.91 us
    pallas_call x1, Pallas kernels, per_device(): pl.pallas_call(fetch_kernel, out_shape=[pltpu.VMEM((WLA, HLO, 2, D), jnp....  1.22 us
  transfers between devices with their start and end apart: 3, of which 1 were waited for; matrix products, arithmetic and copies ran while one was open for 0% of the time, Pallas kernels for 7%

profile of v4, /device:TPU:24, one launch (start us, length us, event | category | flops | bytes accessed | tf_op | source)
XLA Modules:
  0.0 36.1 jit_solution(17041430603493270589)
XLA Ops:
  0.0 1.2 %fetch.1 = (bf16[6,6,2,192]{3,2,1,0:T(2,128)(2,1)S(1)}, bf16[6,12,2,192]{3,2,1,0:T(2,128)(2,1)S(1)}, bf16[144,192]{1,0:T(8,128)(2,1)S(1)}, bf16[6,2,3312]{2,1,0:T(2,128)(2,1)S(1)}, f32[1,192]{1,0:T(1,128)S(1)}) custom-call(bf16[6,12,2,192]{3,2,1,0:T(2,128)(2,1)} %bitcast.15, bf16[6,2,3312]{2,1,0:T(2,128)(2,1)} %bitcast.14, f32[1,192]{1,0:T(1,128)} %bitcast.16, ...), custom_call_target="tpu_custom_call" | custom-call | tf_op jit(solution)/shard_map/fetch/pallas_call | solution.py:380
  1.2 12.6 %collective-permute-start = (bf16[6,6,2,192]{3,2,1,0:T(2,128)(2,1)S(1)}, bf16[6,6,2,192]{3,2,1,0:T(2,128)(2,1)S(1)}, u32[]{:S(2)}, u32[]{:S(2)}) collective-permute-start(bf16[6,6,2,192]{3,2,1,0:T(2,128)(2,1)S(1)} %get-tuple-element.27), channel_id=1, source_target_pairs={{2,4},{4,2},{6,8},{8,6},{10,12},{12,10},{14,16},{16,14},{18,20},{2... | collective-permute-start | bytes 82952 | tf_op jit(solution)/shard_map/ppermute | solution.py:367
  13.8 1.9 %all_gather.9.joint_ref = bf16[6,24,2,192]{3,2,1,0:T(2,128)(2,1)S(1)} all-gather(bf16[6,12,2,192]{3,2,1,0:T(2,128)(2,1)S(1)} %get-tuple-element.28), channel_id=1, replica_groups={{0,2},{4,6},{8,10},{12,14},{16,18},{20,22},{24,26},{28,30},{32,34},{36,..., dimensions={1}, use_global_device_ids=true | all-gather | bytes 165888 | tf_op jit(solution)/shard_map/all_gather | solution.py:410
  15.7 0.0 collective-permute-done.far_ref
  15.7 0.0 copy-start.2
  15.7 0.6 %pack.1 = (bf16[288,192]{1,0:T(8,128)(2,1)S(1)}, bf16[54,138]{1,0:T(8,128)(2,1)S(1)}, bf16[198,256]{1,0:T(8,128)(2,1)S(1)}, bf16[198,256]{1,0:T(8,128)(2,1)S(1)}) custom-call(bf16[6,6,2,192]{3,2,1,0:T(2,128)(2,1)S(1)} %collective-permute-done.far_ref, bf16[6,24,2,192]{3,2,1,0:T(2,128)(2,1)S(1)} %all_gather.9.joint_ref, ...), custom_call_target="tpu_custom_call" | custom-call | tf_op jit(solution)/shard_map/pack/pallas_call | solution.py:417
  16.3 4.7 %collective-permute-start.1 = (bf16[198,256]{1,0:T(8,128)(2,1)S(1)}, bf16[198,256]{1,0:T(8,128)(2,1)S(1)}, u32[]{:S(2)}, u32[]{:S(2)}) collective-permute-start(bf16[198,256]{1,0:T(8,128)(2,1)S(1)} %get-tuple-element.30), channel_id=1, source_target_pairs={{64,128},{128,64},{192,256},{256,192},{320,384},{384,320},{448,0},... | collective-permute-start | bytes 304136 | tf_op jit(solution)/shard_map/ppermute | solution.py:367
  21.0 0.0 copy-start.1
  21.1 5.5 %all-gather.1.both_ref = bf16[2,198,256]{2,1,0:T(8,128)(2,1)S(1)} all-gather(bf16[1,198,256]{2,1,0:T(8,128)(2,1)S(1)} %bitcast.13), channel_id=2, replica_groups={{0,64},{128,192},{256,320},{384,448},{1,65},{129,193},{257,321},{385,44..., dimensions={0}, use_global_device_ids=true | all-gather | bytes 304128 | tf_op jit(solution)/shard_map/all_gather | solution.py:435
  26.5 0.0 copy-start
  26.5 0.0 collective-permute-done.1.far_ref
  26.5 0.0 copy-start.3
  26.5 0.1 assemble.1
  26.7 3.5 %collective-permute-start.2 = (bf16[216,256]{1,0:T(8,128)(2,1)S(1)}, bf16[216,256]{1,0:T(8,128)(2,1)S(1)}, u32[]{:S(2)}, u32[]{:S(2)}) collective-permute-start(bf16[216,256]{1,0:T(8,128)(2,1)S(1)} %get-tuple-element.33), channel_id=1, source_target_pairs={{0,1},{1,0},{2,3},{3,2},{4,5},{5,4},{6,7},{7,6},{8,9},{9,8},{10,11... | collective-permute-start | bytes 331784 | tf_op jit(solution)/shard_map/ppermute | solution.py:367
  30.1 0.0 copy-done.2
  30.2 0.0 copy-done.1
  30.2 0.0 copy-done
  30.2 0.0 copy-done.3
  30.2 2.6 %early.1 = (f32[144,192]{1,0:T(8,128)S(1)}, f32[72,192]{1,0:T(8,128)S(1)}, bf16[2,216,192]{2,1,0:T(8,128)(2,1)S(1)}, bf16[2,144,192]{2,1,0:T(8,128)(2,1)S(1)}, f...) custom-call(bf16[288,192]{1,0:T(8,128)(2,1)S(1)} %get-tuple-element., ...), custom_call_target="tpu_custom_call" | custom-call | flops 4000000000 | tf_op jit(solution)/shard_map/early/pallas_call | solution.py:471
  32.8 0.5 %collective-permute-done.2.other_ref = bf16[216,256]{1,0:T(8,128)(2,1)S(1)} collective-permute-done((bf16[216,256]{1,0:T(8,128)(2,1)S(1)}, bf16[216,256]{1,0:T(8,128)(2,1)S(1)}, u32[]{:S(2)}, u32[]{:S(2)}) %collective-permute-start.2) | collective-permute-done | bytes 110624 | tf_op jit(solution)/shard_map/ppermute | solution.py:367
  33.3 2.8 %late.1 = bf16[72,2,192]{2,1,0:T(2,128)(2,1)} custom-call(bf16[216,256]{1,0:T(8,128)(2,1)S(1)} %collective-permute-done.2.other_ref, f32[144,192]{1,0:T(8,128)S(1)} %get-tuple-element.40.alone_ref, f32[72,192]{1,0:T(8,128)S(1)} %get-tuple-element.41.own_ref, bf16[2,216,192]{2,1,0:T(8,128)(2,1)S(1)} %get-tuple-element.42.asked_ref, ...), custom_call_target="tpu_custom_call" | custom-call | tf_op jit(solution)/shard_map/late/pallas_call | solution.py:480
Async XLA Ops:
  1.2 14.5 %collective-permute-start = (bf16[6,6,2,192]{3,2,1,0:T(2,128)(2,1)S(1)}, bf16[6,6,2,192]{3,2,1,0:T(2,128)(2,1)S(1)}, u32[]{:S(2)}, u32[]{:S(2)}) collective-permute-start(bf16[6,6,2,192]{3,2,1,0:T(2,128)(2,1)S(1)} %get-tuple-element.27), channel_id=1, source_target_pairs={{2,4},{4,2},{6,8},{8,6},{10,12},{12,10},{14,16},{16,14},{18,20},{2... | collective-permute-start | bytes 82952 | tf_op jit(solution)/shard_map/ppermute | solution.py:367
  15.7 14.4 %copy-start.2 = (bf16[192,576]{1,0:T(8,128)(2,1)S(1)}, bf16[192,576]{1,0:T(8,128)(2,1)}, u32[]{:S(2)}) copy-start(bf16[192,576]{1,0:T(8,128)(2,1)} %qkv_ref.3) | copy-start | bytes 663556
  16.3 10.2 %collective-permute-start.1 = (bf16[198,256]{1,0:T(8,128)(2,1)S(1)}, bf16[198,256]{1,0:T(8,128)(2,1)S(1)}, u32[]{:S(2)}, u32[]{:S(2)}) collective-permute-start(bf16[198,256]{1,0:T(8,128)(2,1)S(1)} %get-tuple-element.30), channel_id=1, source_target_pairs={{64,128},{128,64},{192,256},{256,192},{320,384},{384,320},{448,0},... | collective-permute-start | bytes 304136 | tf_op jit(solution)/shard_map/ppermute | solution.py:367
  21.0 9.1 %copy-start.1 = (bf16[768,192]{0,1:T(8,128)(2,1)S(1)}, bf16[768,192]{0,1:T(8,128)(2,1)}, u32[]{:S(2)}) copy-start(bf16[768,192]{0,1:T(8,128)(2,1)} %param.15) | copy-start | bytes 884740
  26.5 3.6 %copy-start = (bf16[192,768]{1,0:T(8,128)(2,1)S(1)}, bf16[192,768]{1,0:T(8,128)(2,1)}, u32[]{:S(2)}) copy-start(bf16[192,768]{1,0:T(8,128)(2,1)} %fc1_ref.3) | copy-start | bytes 884740
  26.5 3.6 %copy-start.3 = (bf16[192,192]{1,0:T(8,128)(2,1)S(1)}, bf16[192,192]{1,0:T(8,128)(2,1)}, u32[]{:S(2)}) copy-start(bf16[192,192]{1,0:T(8,128)(2,1)} %proj_ref.3) | copy-start | bytes 221188
  26.7 6.6 %collective-permute-start.2 = (bf16[216,256]{1,0:T(8,128)(2,1)S(1)}, bf16[216,256]{1,0:T(8,128)(2,1)S(1)}, u32[]{:S(2)}, u32[]{:S(2)}) collective-permute-start(bf16[216,256]{1,0:T(8,128)(2,1)S(1)} %get-tuple-element.33), channel_id=1, source_target_pairs={{0,1},{1,0},{2,3},{3,2},{4,5},{5,4},{6,7},{7,6},{8,9},{9,8},{10,11... | collective-permute-start | bytes 331784 | tf_op jit(solution)/shard_map/ppermute | solution.py:367

commit v5 on v4

--- a/solution.py
+++ b/solution.py
@@ -21,7 +21,8 @@
 LANES = 256
 TABLE = 54
 CELLS = 144
-FAR_COLUMNS = 6
+SENT = 112
+FAR_COLUMNS = 12
 VMEM_LIMIT = 16 * 1024 * 1024
 
 norm_eps = 1e-05
@@ -91,30 +92,6 @@
     mixed = dot(halved(normalized(first, gain)), fc1)
     hidden = halved(mixed * (1.0 + lax.erf(mixed * (0.5**0.5))) * 0.5)
     return halved(first + dot_t(hidden, fc2_t))
-
-
-def fetch_kernel(
-    cells_ref, tables_ref, gain1_ref, gain2_ref,
-    half_ref, own_ref, rows_ref, held_ref, gain2_held, raw_ref, gain1_held, sems,
-):
-    odd = lax.axis_index("lon") % 2
-    copies = [
-        pltpu.make_async_copy(gain1_ref, gain1_held, sems.at[0]),
-        pltpu.make_async_copy(cells_ref, raw_ref, sems.at[1]),
-        pltpu.make_async_copy(tables_ref, held_ref, sems.at[2]),
-        pltpu.make_async_copy(gain2_ref, gain2_held, sems.at[3]),
-    ]
-    for copy in copies:
-        copy.start()
-    copies[0].wait()
-    copies[1].wait()
-    rows = raw_ref[...].reshape(CELLS, D)
-    rows_ref[...] = rows
-    cells = rows.astype(jnp.float32)
-    own_ref[...] = halved(normalized(cells, gain1_held[...])).reshape(raw_ref.shape)
-    half_ref[...] = own_ref[:, pl.ds(HLO * odd, HLO)]
-    copies[2].wait()
-    copies[3].wait()
 
 
 def pack_kernel(
@@ -159,17 +136,20 @@
         for at in (0, HLA)
     ]
     lower_ref[...] = halved(rows[0])
-    blank = jnp.zeros((CELLS + TABLE, LANES), jnp.bfloat16)
-    sent_far_ref[...] = blank
-    sent_near_ref[...] = blank
-    sent_far_ref[:CELLS, :D] = halved(jnp.where(lat_even, head, tail))
-    sent_near_ref[:CELLS, :D] = halved(jnp.where(lat_even, tail, head))
-    sent_far_ref[CELLS:, :span] = halved(rows[1])
-    sent_near_ref[CELLS:, :span] = halved(rows[1])
+    upper = jnp.concatenate([rows[1], jnp.zeros((TABLE, LANES - span), jnp.float32)], axis=1)
+    for ref, cells in (
+        (sent_far_ref, jnp.where(lat_even, head, tail)),
+        (sent_near_ref, jnp.where(lat_even, tail, head)),
+    ):
+        second = cells[72:]
+        rest = second[:, LANES - D :]
+        ref[:72] = halved(jnp.concatenate([cells[:72], second[:, : LANES - D]], axis=1))
+        ref[72:SENT] = halved(jnp.concatenate([rest[:40], rest[32:]], axis=1))
+        ref[SENT:] = halved(upper)
 
 
 def assemble_kernel(
-    far_ref, both_ref, wide_ref, alone_ref, pair_ref, table_ref, sent_ref
+    far_ref, both_ref, wide_ref, gain_ref, gain2_ref, gain2_out, alone_ref, pair_ref, table_ref, sent_ref
 ):
     lev = lax.axis_index("lev")
     lat_odd = lax.axis_index("lat") % 2
@@ -178,18 +158,26 @@
     wide = wide_ref[...].astype(jnp.float32)
     before = jnp.where(lat_odd == 0, far, near)
     after = jnp.where(lat_odd == 0, near, far)
+
+    def unpacked(rows):
+        rest = [rows[72:SENT, : LANES // 2], rows[80:SENT, LANES // 2 :]]
+        second = [rows[:72, D:], jnp.concatenate(rest, axis=0)]
+        return rows[:72, :D], jnp.concatenate(second, axis=1)
+
+    edges = unpacked(before), unpacked(after)
     levels = [
         jnp.concatenate(
             [
-                before[l * 72 : (l + 1) * 72, :D],
+                edges[0][l],
                 wide[l * HALF : (l + 1) * HALF],
-                after[l * 72 : (l + 1) * 72, :D],
+                edges[1][l],
             ],
             axis=0,
         )
         for l in range(2)
     ]
-    pair = jnp.where(lev == 0, levels[1], levels[0])
+    gain2_out[...] = gain2_ref[...]
+    pair = normalized(jnp.where(lev == 0, levels[1], levels[0]), gain_ref[...])
     pair_ref[...] = halved(pair)
     first = pair[:HALF]
     second = pair[HALF:]
@@ -197,7 +185,7 @@
     rest = second[:, LANES - D :]
     sent_ref[HALF:] = halved(jnp.concatenate([rest[:72], rest[72:]], axis=1))
     alone_ref[...] = halved(jnp.where(lev == 0, levels[0], levels[1]))
-    table_ref[...] = halved(before[CELLS:, : WLA * SPAN])
+    table_ref[...] = halved(before[SENT:, : WLA * SPAN])
 
 
 def packed_dots(packed, weight):
@@ -213,7 +201,8 @@
 def early_kernel(
     alone_cells_ref,
     pair_cells_ref,
-    raw_ref,
+    wide_ref,
+    gain1_ref,
     upper_ref,
     lower_ref,
     qkv_ref,
@@ -245,10 +234,12 @@
     back = [halved(jnp.where(cell == source + at * WLO, 1.0, 0.0)) for at in (0, HLA)]
     for at in range(2):
         back_ref[at] = back[at]
-    raw = raw_ref[...]
-    cell = 2 * counted((72, 1), 0)
-    own_ref[...] = dot(one_hot(cell + 1 - lev, CELLS), raw)
-    alone_own = dot(one_hot(cell + lev, CELLS), raw)
+    wide = wide_ref[...]
+    place = counted((72, 1), 0)
+    lat_row = (place * 5462) >> 16
+    cell = lat_row * 24 + HLO + place - WLO * lat_row
+    own_ref[...] = dot(one_hot(cell + HALF * (1 - lev), ROWS), wide)
+    alone_own = dot(one_hot(cell + HALF * lev, ROWS), wide)
     woven_row = counted((CELLS, 72), 0) - 2 * counted((CELLS, 72), 1)
     woven_ref[...] = halved(jnp.where(woven_row == 1 - lev, 1.0, 0.0))
     entry, spot = by_18(counted((3 * GROUP, 1), 0))
@@ -298,7 +289,7 @@
         bias_ref[lat_window] = bias_of(lat_window, 2)
 
     parts = []
-    for lat_window, (asked, scores, values) in enumerate(asked_of(alone_cells_ref[...])):
+    for lat_window, (asked, scores, values) in enumerate(asked_of(halved(normalized(alone_cells_ref[...].astype(jnp.float32), gain1_ref[...])))):
         parts.append(softmax_context([scores + bias_of(lat_window, 0)], [values], owned))
     alone = finish(
         alone_own,
@@ -376,44 +367,14 @@
     cells_t = tokens.transpose(1, 2, 0, 3)
     tables_t = earth_bias[:, 0].transpose(1, 0, 2)
     params = pltpu.CompilerParams(vmem_limit_bytes=VMEM_LIMIT)
-    anywhere = pl.BlockSpec(memory_space=pltpu.HBM)
-    half_t, own_t, raw_t, tables_t, gain2 = pl.pallas_call(
-        fetch_kernel,
-        out_shape=[
-            pltpu.VMEM((WLA, HLO, 2, D), jnp.bfloat16),
-            pltpu.VMEM(cells_t.shape, jnp.bfloat16),
-            pltpu.VMEM((CELLS, D), jnp.bfloat16),
-            pltpu.VMEM(tables_t.shape, jnp.bfloat16),
-            pltpu.VMEM((1, D), jnp.float32),
-        ],
-        in_specs=[anywhere] * 4,
-        out_specs=[pl.BlockSpec(memory_space=pltpu.VMEM)] * 5,
-        scratch_shapes=[
-            pltpu.VMEM(cells_t.shape, jnp.bfloat16),
-            pltpu.VMEM((1, D), jnp.float32),
-            pltpu.SemaphoreType.DMA((4,)),
-        ],
-        compiler_params=params,
-        name="fetch",
-    )(
-        *[
-            pltpu.with_memory_space_constraint(x, pltpu.HBM)
-            for x in (
-                cells_t,
-                tables_t,
-                norm1_gain.reshape(1, D),
-                norm2_gain.reshape(1, D),
-            )
-        ]
-    )
-    far = swapped(half_t, "lon", True)
+    far = swapped(cells_t, "lon", True)
     joint = lax.all_gather(
-        own_t, "lon", axis_index_groups=pairs_of(lon_size, False), axis=1, tiled=True
+        cells_t, "lon", axis_index_groups=pairs_of(lon_size, False), axis=1, tiled=True
     )
     whole = pl.BlockSpec(memory_space=pltpu.VMEM)
     placed = pltpu.with_memory_space_constraint
     held = lambda x: placed(x, pltpu.VMEM)
-    sent = pltpu.VMEM((CELLS + TABLE, LANES), jnp.bfloat16)
+    sent = pltpu.VMEM((SENT + TABLE, LANES), jnp.bfloat16)
     wide, lower, sent_far, sent_near = pl.pallas_call(
         pack_kernel,
         out_shape=[
@@ -433,20 +394,22 @@
     )
     lat_far = swapped(sent_far, "lat", True)
     lat_both = lax.all_gather(sent_near, "lat", axis_index_groups=pairs_of(lat_size, False))
+    gain1 = held(norm1_gain.reshape(1, D))
     level = pltpu.VMEM((ROWS, D), jnp.bfloat16)
-    alone_cells, pair_cells, upper, sent = pl.pallas_call(
+    gain2, alone_cells, pair_cells, upper, sent = pl.pallas_call(
         assemble_kernel,
         out_shape=[
+            pltpu.VMEM((1, D), jnp.float32),
             level,
             level,
             pltpu.VMEM((TABLE, WLA * SPAN), jnp.bfloat16),
             pltpu.VMEM((HALF + 72, LANES), jnp.bfloat16),
         ],
-        in_specs=[whole] * 3,
-        out_specs=[whole] * 4,
+        in_specs=[whole] * 5,
+        out_specs=[whole] * 5,
         compiler_params=params,
         name="assemble",
-    )(held(lat_far), held(lat_both), wide)
+    )(held(lat_far), held(lat_both), wide, gain1, held(norm2_gain.reshape(1, D)))
     other = swapped(sent, "lev", False)
 
     shared = (
@@ -471,12 +434,12 @@
     early = pl.pallas_call(
         early_kernel,
         out_shape=passed,
-        in_specs=[whole] * (5 + len(shared)),
+        in_specs=[whole] * (6 + len(shared)),
         out_specs=[whole] * len(passed),
         cost_estimate=pl.CostEstimate(flops=4_000_000_000, transcendentals=0, bytes_accessed=0),
         compiler_params=params,
         name="early",
-    )(alone_cells, pair_cells, raw_t, upper, lower, *shared)
+    )(alone_cells, pair_cells, wide, gain1, upper, lower, *shared)
     result = pl.pallas_call(
         late_kernel,
         out_shape=jax.ShapeDtypeStruct((72, 2, D), jnp.bfloat16),

time: 36.4 us -> 36.2 us (level)
  the two profiles are of different devices: /device:TPU:24 before, /device:TPU:64 now
where the time goes in v5:
time: 36.2 us; the launch traced here: 36 us
  starting transfers between devices  19.1 us (53%)
  blocking collectives  7.41 us (20%)
  Pallas kernels  6.56 us (18%)
  waiting for transfers between devices  2.83 us (8%)
    ppermute x3, starting transfers between devices, swapped(): return lax.ppermute(block, axis, route)  19.1 us
    all_gather x1, blocking collectives, per_device(): lax.all_gather(sent_near, 'lat', axis_index_groups=pairs_of(lat_size, Fal...  5.29 us
    ppermute x3, waiting for transfers between devices, swapped(): return lax.ppermute(block, axis, route)  2.83 us
    pallas_call x1, Pallas kernels, per_device(): pl.pallas_call(late_kernel, out_shape=jax.ShapeDtypeStruct((72, 2, D), jn...  2.82 us
    pallas_call x1, Pallas kernels, per_device(): pl.pallas_call(early_kernel, out_shape=passed, in_specs=[whole] * (6 + le...  2.74 us
    all_gather x1, blocking collectives, per_device(): lax.all_gather(cells_t, 'lon', axis_index_groups=pairs_of(lon_size, False...  2.12 us
  transfers between devices with their start and end apart: 3, of which 2 were waited for; matrix products, arithmetic and copies ran while one was open for 0% of the time, Pallas kernels for 8%

profile of v5, /device:TPU:64, one launch (start us, length us, event | category | flops | bytes accessed | tf_op | source)
XLA Modules:
  0.0 36.0 jit_solution(7073851232501021002)
XLA Ops:
  0.0 0.0 copy-start.4
  0.0 11.8 %collective-permute-start = (bf16[6,12,2,192]{3,2,1,0:T(2,128)(2,1)}, bf16[6,12,2,192]{3,2,1,0:T(2,128)(2,1)S(1)}, u32[]{:S(2)}, u32[]{:S(2)}) collective-permute-start(bf16[6,12,2,192]{3,2,1,0:T(2,128)(2,1)} %bitcast.18), channel_id=1, source_target_pairs={{2,4},{4,2},{6,8},{8,6},{10,12},{12,10},{14,16},{16,14},{18,20},{2... | collective-permute-start | bytes 165896 | tf_op jit(solution)/shard_map/ppermute | solution.py:358
  11.8 2.1 %all_gather.9.joint_ref = bf16[6,24,2,192]{3,2,1,0:T(2,128)(2,1)S(1)} all-gather(bf16[6,12,2,192]{3,2,1,0:T(2,128)(2,1)} %bitcast.19), channel_id=1, replica_groups={{0,2},{4,6},{8,10},{12,14},{16,18},{20,22},{24,26},{28,30},{32,34},{36,..., dimensions={1}, use_global_device_ids=true | all-gather | bytes 165888 | tf_op jit(solution)/shard_map/all_gather | solution.py:371
  13.9 0.9 %collective-permute-done.far_ref = bf16[6,12,2,192]{3,2,1,0:T(2,128)(2,1)S(1)} collective-permute-done((bf16[6,12,2,192]{3,2,1,0:T(2,128)(2,1)}, bf16[6,12,2,192]{3,2,1,0:T(2,128)(2,1)S(1)}, u32[]{:S(2)}, u32[]{:S(2)}) %collective-permute-start) | collective-permute-done | bytes 55328 | tf_op jit(solution)/shard_map/ppermute | solution.py:358
  14.8 0.0 copy-done.4
  14.8 0.0 copy-start.5
  14.8 0.0 copy-start.6
  14.8 0.0 copy-start.2
  14.8 0.0 copy-start.3
  14.9 0.6 %pack.1 = (bf16[288,192]{1,0:T(8,128)(2,1)S(1)}, bf16[54,138]{1,0:T(8,128)(2,1)S(1)}, bf16[166,256]{1,0:T(8,128)(2,1)S(1)}, bf16[166,256]{1,0:T(8,128)(2,1)S(1)}) custom-call(bf16[6,12,2,192]{3,2,1,0:T(2,128)(2,1)S(1)} %collective-permute-done.far_ref, bf16[6,24,2,192]{3,2,1,0:T(2,128)(2,1)S(1)} %all_gather.9.joint_ref, bf16[6,2,3312]{2,1,0:T(2,128)(2,1)S(1)} %bitcast.14), custom_call_target="tpu_custom_call" | custom-call | tf_op jit(solution)/shard_map/pack/pallas_call | solution.py:378
  15.5 5.4 %collective-permute-start.1 = (bf16[166,256]{1,0:T(8,128)(2,1)S(1)}, bf16[166,256]{1,0:T(8,128)(2,1)S(1)}, u32[]{:S(2)}, u32[]{:S(2)}) collective-permute-start(bf16[166,256]{1,0:T(8,128)(2,1)S(1)} %get-tuple-element.23), channel_id=1, source_target_pairs={{64,128},{128,64},{192,256},{256,192},{320,384},{384,320},{448,0},... | collective-permute-start | bytes 254984 | tf_op jit(solution)/shard_map/ppermute | solution.py:358
  20.9 0.0 copy-start
  20.9 0.0 copy-start.1
  20.9 5.3 %all-gather.1.both_ref = bf16[2,166,256]{2,1,0:T(8,128)(2,1)S(1)} all-gather(bf16[1,166,256]{2,1,0:T(8,128)(2,1)S(1)} %bitcast.13), channel_id=2, replica_groups={{0,64},{128,192},{256,320},{384,448},{1,65},{129,193},{257,321},{385,44..., dimensions={0}, use_global_device_ids=true | all-gather | bytes 254976 | tf_op jit(solution)/shard_map/all_gather | solution.py:396
  26.2 0.0 collective-permute-done.1.far_ref
  26.2 0.0 copy-done.5
  26.2 0.0 copy-done.6
  26.2 0.4 %assemble.1 = (f32[1,192]{1,0:T(1,128)S(1)}, bf16[288,192]{1,0:T(8,128)(2,1)S(1)}, bf16[288,192]{1,0:T(8,128)(2,1)S(1)}, bf16[54,138]{1,0:T(8,128)(2,1)S(1)}, bf16[216,256]{1,0:T(8,128)(2,1)S(1)}) custom-call(bf16[166,256]{1,0:T(8,128)(2,1)S(1)} %collective-permute-done.1.far_ref, bf16[2,166,256]{2,1,0:T(8,128)(2,1)S(1)} %all-gather.1.both_ref, ...), custom_call_target="tpu_custom_call" | custom-call | tf_op jit(solution)/shard_map/assemble/pallas_call | solution.py:399
  26.6 1.9 %collective-permute-start.2 = (bf16[216,256]{1,0:T(8,128)(2,1)S(1)}, bf16[216,256]{1,0:T(8,128)(2,1)S(1)}, u32[]{:S(2)}, u32[]{:S(2)}) collective-permute-start(bf16[216,256]{1,0:T(8,128)(2,1)S(1)} %get-tuple-element.26), channel_id=1, source_target_pairs={{0,1},{1,0},{2,3},{3,2},{4,5},{5,4},{6,7},{7,6},{8,9},{9,8},{10,11... | collective-permute-start | bytes 331784 | tf_op jit(solution)/shard_map/ppermute | solution.py:358
  28.5 0.0 copy-done.2
  28.5 0.0 copy-done.3
  28.5 0.0 copy-done
  28.5 0.0 copy-done.1
  28.5 2.7 %early.1 = (f32[144,192]{1,0:T(8,128)S(1)}, f32[72,192]{1,0:T(8,128)S(1)}, bf16[2,216,192]{2,1,0:T(8,128)(2,1)S(1)}, bf16[2,144,192]{2,1,0:T(8,128)(2,1)S(1)}, f...) custom-call(bf16[288,192]{1,0:T(8,128)(2,1)S(1)} %get-tuple-element., ...), custom_call_target="tpu_custom_call" | custom-call | flops 4000000000 | tf_op jit(solution)/shard_map/early/pallas_call | solution.py:434
  31.3 1.9 %collective-permute-done.2.other_ref = bf16[216,256]{1,0:T(8,128)(2,1)S(1)} collective-permute-done((bf16[216,256]{1,0:T(8,128)(2,1)S(1)}, bf16[216,256]{1,0:T(8,128)(2,1)S(1)}, u32[]{:S(2)}, u32[]{:S(2)}) %collective-permute-start.2) | collective-permute-done | bytes 110624 | tf_op jit(solution)/shard_map/ppermute | solution.py:358
  33.2 2.8 %late.1 = bf16[72,2,192]{2,1,0:T(2,128)(2,1)} custom-call(bf16[216,256]{1,0:T(8,128)(2,1)S(1)} %collective-permute-done.2.other_ref, f32[144,192]{1,0:T(8,128)S(1)} %get-tuple-element.32.alone_ref, f32[72,192]{1,0:T(8,128)S(1)} %get-tuple-element.33.own_ref, bf16[2,216,192]{2,1,0:T(8,128)(2,1)S(1)} %get-tuple-element.34.asked_ref, ...), custom_call_target="tpu_custom_call" | custom-call | tf_op jit(solution)/shard_map/late/pallas_call | solution.py:443
Async XLA Ops:
  0.0 14.8 %copy-start.4 = (bf16[2,1,6,3312]{3,0,2,1:T(2,128)(2,1)S(1)}, bf16[2,1,6,3312]{3,0,2,1:T(2,128)(2,1)}, u32[]{:S(2)}) copy-start(bf16[2,1,6,3312]{3,0,2,1:T(2,128)(2,1)} %param.12) | copy-start | bytes 238468
  0.0 14.8 %collective-permute-start = (bf16[6,12,2,192]{3,2,1,0:T(2,128)(2,1)}, bf16[6,12,2,192]{3,2,1,0:T(2,128)(2,1)S(1)}, u32[]{:S(2)}, u32[]{:S(2)}) collective-permute-start(bf16[6,12,2,192]{3,2,1,0:T(2,128)(2,1)} %bitcast.18), channel_id=1, source_target_pairs={{2,4},{4,2},{6,8},{8,6},{10,12},{12,10},{14,16},{16,14},{18,20},{2... | collective-permute-start | bytes 165896 | tf_op jit(solution)/shard_map/ppermute | solution.py:358
  14.8 11.4 %copy-start.5 = (f32[192]{0:T(256)S(1)}, f32[192]{0:T(256)}, u32[]{:S(2)}) copy-start(f32[192]{0:T(256)} %param.13) | copy-start | bytes 2308
  14.8 11.4 %copy-start.6 = (f32[192]{0:T(256)S(1)}, f32[192]{0:T(256)}, u32[]{:S(2)}) copy-start(f32[192]{0:T(256)} %param.9) | copy-start | bytes 2308
  14.8 13.7 %copy-start.2 = (bf16[192,576]{1,0:T(8,128)(2,1)S(1)}, bf16[192,576]{1,0:T(8,128)(2,1)}, u32[]{:S(2)}) copy-start(bf16[192,576]{1,0:T(8,128)(2,1)} %qkv_ref.3) | copy-start | bytes 663556
  14.8 13.7 %copy-start.3 = (bf16[192,192]{1,0:T(8,128)(2,1)S(1)}, bf16[192,192]{1,0:T(8,128)(2,1)}, u32[]{:S(2)}) copy-start(bf16[192,192]{1,0:T(8,128)(2,1)} %proj_ref.3) | copy-start | bytes 221188
  15.5 10.7 %collective-permute-start.1 = (bf16[166,256]{1,0:T(8,128)(2,1)S(1)}, bf16[166,256]{1,0:T(8,128)(2,1)S(1)}, u32[]{:S(2)}, u32[]{:S(2)}) collective-permute-start(bf16[166,256]{1,0:T(8,128)(2,1)S(1)} %get-tuple-element.23), channel_id=1, source_target_pairs={{64,128},{128,64},{192,256},{256,192},{320,384},{384,320},{448,0},... | collective-permute-start | bytes 254984 | tf_op jit(solution)/shard_map/ppermute | solution.py:358
  20.9 7.6 %copy-start = (bf16[192,768]{1,0:T(8,128)(2,1)S(1)}, bf16[192,768]{1,0:T(8,128)(2,1)}, u32[]{:S(2)}) copy-start(bf16[192,768]{1,0:T(8,128)(2,1)} %fc1_ref.3) | copy-start | bytes 884740
  20.9 7.6 %copy-start.1 = (bf16[768,192]{0,1:T(8,128)(2,1)S(1)}, bf16[768,192]{0,1:T(8,128)(2,1)}, u32[]{:S(2)}) copy-start(bf16[768,192]{0,1:T(8,128)(2,1)} %param.15) | copy-start | bytes 884740
  26.6 6.6 %collective-permute-start.2 = (bf16[216,256]{1,0:T(8,128)(2,1)S(1)}, bf16[216,256]{1,0:T(8,128)(2,1)S(1)}, u32[]{:S(2)}, u32[]{:S(2)}) collective-permute-start(bf16[216,256]{1,0:T(8,128)(2,1)S(1)} %get-tuple-element.26), channel_id=1, source_target_pairs={{0,1},{1,0},{2,3},{3,2},{4,5},{5,4},{6,7},{7,6},{8,9},{9,8},{10,11... | collective-permute-start | bytes 331784 | tf_op jit(solution)/shard_map/ppermute | solution.py:358

commit v6 on v5

--- a/solution.py
+++ b/solution.py
@@ -22,7 +22,7 @@
 TABLE = 54
 CELLS = 144
 SENT = 112
-FAR_COLUMNS = 12
+FAR_COLUMNS = 6
 VMEM_LIMIT = 16 * 1024 * 1024
 
 norm_eps = 1e-05
@@ -92,6 +92,13 @@
     mixed = dot(halved(normalized(first, gain)), fc1)
     hidden = halved(mixed * (1.0 + lax.erf(mixed * (0.5**0.5))) * 0.5)
     return halved(first + dot_t(hidden, fc2_t))
+
+
+def half_kernel(cells_ref, half_ref, sem):
+    odd = lax.axis_index("lon") % 2
+    copy = pltpu.make_async_copy(cells_ref.at[:, pl.ds(HLO * odd, HLO)], half_ref, sem)
+    copy.start()
+    copy.wait()
 
 
 def pack_kernel(
@@ -367,7 +374,16 @@
     cells_t = tokens.transpose(1, 2, 0, 3)
     tables_t = earth_bias[:, 0].transpose(1, 0, 2)
     params = pltpu.CompilerParams(vmem_limit_bytes=VMEM_LIMIT)
-    far = swapped(cells_t, "lon", True)
+    half_t = pl.pallas_call(
+        half_kernel,
+        out_shape=pltpu.VMEM((WLA, HLO, 2, D), jnp.bfloat16),
+        in_specs=[pl.BlockSpec(memory_space=pltpu.HBM)],
+        out_specs=pl.BlockSpec(memory_space=pltpu.VMEM),
+        scratch_shapes=[pltpu.SemaphoreType.DMA],
+        compiler_params=pltpu.CompilerParams(vmem_limit_bytes=VMEM_LIMIT),
+        name="half",
+    )(pltpu.with_memory_space_constraint(cells_t, pltpu.HBM))
+    far = swapped(half_t, "lon", True)
     joint = lax.all_gather(
         cells_t, "lon", axis_index_groups=pairs_of(lon_size, False), axis=1, tiled=True
     )

time: 36.2 us -> 36.3 us (level)
  the two profiles are of different devices: /device:TPU:64 before, /device:TPU:24 now
where the time goes in v6:
time: 36.3 us; the launch traced here: 36 us
  starting transfers between devices  20.8 us (57%)
  Pallas kernels  7.38 us (20%)
  blocking collectives  7.2 us (20%)
  waiting for transfers between devices  0.41 us (1%)
    ppermute x3, starting transfers between devices, swapped(): return lax.ppermute(block, axis, route)  20.8 us
    all_gather x1, blocking collectives, per_device(): lax.all_gather(sent_near, 'lat', axis_index_groups=pairs_of(lat_size, Fal...  5.29 us
    pallas_call x1, Pallas kernels, per_device(): pl.pallas_call(late_kernel, out_shape=jax.ShapeDtypeStruct((72, 2, D), jn...  2.82 us
    pallas_call x1, Pallas kernels, per_device(): pl.pallas_call(early_kernel, out_shape=passed, in_specs=[whole] * (6 + le...  2.73 us
    all_gather x1, blocking collectives, per_device(): lax.all_gather(cells_t, 'lon', axis_index_groups=pairs_of(lon_size, False...  1.91 us
    pallas_call x1, Pallas kernels, per_device(): pl.pallas_call(half_kernel, out_shape=pltpu.VMEM((WLA, HLO, 2, D), jnp.bf...  0.85 us
  transfers between devices with their start and end apart: 3, of which 1 were waited for; matrix products, arithmetic and copies ran while one was open for 0% of the time, Pallas kernels for 8%

profile of v6, /device:TPU:24, one launch (start us, length us, event | category | flops | bytes accessed | tf_op | source)
XLA Modules:
  0.0 36.0 jit_solution(17060467845146379691)
XLA Ops:
  0.0 0.0 copy-start.7
  0.0 0.8 %half.1 = bf16[6,6,2,192]{3,2,1,0:T(2,128)(2,1)S(1)} custom-call(bf16[6,12,2,192]{3,2,1,0:T(2,128)(2,1)} %bitcast.18), custom_call_target="tpu_custom_call" | custom-call | tf_op jit(solution)/shard_map/half/pallas_call | solution.py:377
  0.9 0.0 copy-start.4
  0.9 12.7 %collective-permute-start = (bf16[6,6,2,192]{3,2,1,0:T(2,128)(2,1)S(1)}, bf16[6,6,2,192]{3,2,1,0:T(2,128)(2,1)S(1)}, u32[]{:S(2)}, u32[]{:S(2)}) collective-permute-start(bf16[6,6,2,192]{3,2,1,0:T(2,128)(2,1)S(1)} %half.1), channel_id=1, source_target_pairs={{2,4},{4,2},{6,8},{8,6},{10,12},{12,10},{14,16},{16,14},{18,20},{2... | collective-permute-start | bytes 82952 | tf_op jit(solution)/shard_map/ppermute | solution.py:365
  13.6 0.0 copy-done.7
  13.6 1.9 %all_gather.9.joint_ref = bf16[6,24,2,192]{3,2,1,0:T(2,128)(2,1)S(1)} all-gather(bf16[6,12,2,192]{3,2,1,0:T(2,128)(2,1)S(1)} %bitcast.19), channel_id=1, replica_groups={{0,2},{4,6},{8,10},{12,14},{16,18},{20,22},{24,26},{28,30},{32,34},{36,..., dimensions={1}, use_global_device_ids=true | all-gather | bytes 165888 | tf_op jit(solution)/shard_map/all_gather | solution.py:387
  15.5 0.0 collective-permute-done.far_ref
  15.5 0.0 copy-done.4
  15.5 0.0 copy-start.5
  15.5 0.0 copy-start.6
  15.5 0.0 copy-start.2
  15.5 0.0 copy-start.3
  15.6 0.6 %pack.1 = (bf16[288,192]{1,0:T(8,128)(2,1)S(1)}, bf16[54,138]{1,0:T(8,128)(2,1)S(1)}, bf16[166,256]{1,0:T(8,128)(2,1)S(1)}, bf16[166,256]{1,0:T(8,128)(2,1)S(1)}) custom-call(bf16[6,6,2,192]{3,2,1,0:T(2,128)(2,1)S(1)} %collective-permute-done.far_ref, bf16[6,24,2,192]{3,2,1,0:T(2,128)(2,1)S(1)} %all_gather.9.joint_ref, bf16[6,2,3312]{2,1,0:T(2,128)(2,1)S(1)} %bitcast.14), custom_call_target="tpu_custom_call" | custom-call | tf_op jit(solution)/shard_map/pack/pallas_call | solution.py:394
  16.2 4.7 %collective-permute-start.1 = (bf16[166,256]{1,0:T(8,128)(2,1)S(1)}, bf16[166,256]{1,0:T(8,128)(2,1)S(1)}, u32[]{:S(2)}, u32[]{:S(2)}) collective-permute-start(bf16[166,256]{1,0:T(8,128)(2,1)S(1)} %get-tuple-element.23), channel_id=1, source_target_pairs={{64,128},{128,64},{192,256},{256,192},{320,384},{384,320},{448,0},... | collective-permute-start | bytes 254984 | tf_op jit(solution)/shard_map/ppermute | solution.py:365
  20.9 0.0 copy-start
  20.9 0.0 copy-start.1
  20.9 5.3 %all-gather.1.both_ref = bf16[2,166,256]{2,1,0:T(8,128)(2,1)S(1)} all-gather(bf16[1,166,256]{2,1,0:T(8,128)(2,1)S(1)} %bitcast.13), channel_id=2, replica_groups={{0,64},{128,192},{256,320},{384,448},{1,65},{129,193},{257,321},{385,44..., dimensions={0}, use_global_device_ids=true | all-gather | bytes 254976 | tf_op jit(solution)/shard_map/all_gather | solution.py:412
  26.2 0.0 collective-permute-done.1.far_ref
  26.2 0.0 copy-done.5
  26.2 0.0 copy-done.6
  26.2 0.4 %assemble.1 = (f32[1,192]{1,0:T(1,128)S(1)}, bf16[288,192]{1,0:T(8,128)(2,1)S(1)}, bf16[288,192]{1,0:T(8,128)(2,1)S(1)}, bf16[54,138]{1,0:T(8,128)(2,1)S(1)}, bf16[216,256]{1,0:T(8,128)(2,1)S(1)}) custom-call(bf16[166,256]{1,0:T(8,128)(2,1)S(1)} %collective-permute-done.1.far_ref, bf16[2,166,256]{2,1,0:T(8,128)(2,1)S(1)} %all-gather.1.both_ref, ...), custom_call_target="tpu_custom_call" | custom-call | tf_op jit(solution)/shard_map/assemble/pallas_call | solution.py:415
  26.6 3.5 %collective-permute-start.2 = (bf16[216,256]{1,0:T(8,128)(2,1)S(1)}, bf16[216,256]{1,0:T(8,128)(2,1)S(1)}, u32[]{:S(2)}, u32[]{:S(2)}) collective-permute-start(bf16[216,256]{1,0:T(8,128)(2,1)S(1)} %get-tuple-element.26), channel_id=1, source_target_pairs={{0,1},{1,0},{2,3},{3,2},{4,5},{5,4},{6,7},{7,6},{8,9},{9,8},{10,11... | collective-permute-start | bytes 331784 | tf_op jit(solution)/shard_map/ppermute | solution.py:365
  30.0 0.0 copy-done.2
  30.0 0.0 copy-done.3
  30.1 0.0 copy-done
  30.1 0.0 copy-done.1
  30.1 2.7 %early.1 = (f32[144,192]{1,0:T(8,128)S(1)}, f32[72,192]{1,0:T(8,128)S(1)}, bf16[2,216,192]{2,1,0:T(8,128)(2,1)S(1)}, bf16[2,144,192]{2,1,0:T(8,128)(2,1)S(1)}, f...) custom-call(bf16[288,192]{1,0:T(8,128)(2,1)S(1)} %get-tuple-element., ...), custom_call_target="tpu_custom_call" | custom-call | flops 4000000000 | tf_op jit(solution)/shard_map/early/pallas_call | solution.py:450
  32.8 0.4 %collective-permute-done.2.other_ref = bf16[216,256]{1,0:T(8,128)(2,1)S(1)} collective-permute-done((bf16[216,256]{1,0:T(8,128)(2,1)S(1)}, bf16[216,256]{1,0:T(8,128)(2,1)S(1)}, u32[]{:S(2)}, u32[]{:S(2)}) %collective-permute-start.2) | collective-permute-done | bytes 110624 | tf_op jit(solution)/shard_map/ppermute | solution.py:365
  33.2 2.8 %late.1 = bf16[72,2,192]{2,1,0:T(2,128)(2,1)} custom-call(bf16[216,256]{1,0:T(8,128)(2,1)S(1)} %collective-permute-done.2.other_ref, f32[144,192]{1,0:T(8,128)S(1)} %get-tuple-element.32.alone_ref, f32[72,192]{1,0:T(8,128)S(1)} %get-tuple-element.33.own_ref, bf16[2,216,192]{2,1,0:T(8,128)(2,1)S(1)} %get-tuple-element.34.asked_ref, ...), custom_call_target="tpu_custom_call" | custom-call | tf_op jit(solution)/shard_map/late/pallas_call | solution.py:459
Async XLA Ops:
  0.0 13.6 %copy-start.7 = (bf16[2,6,12,192]{3,0,2,1:T(2,128)(2,1)S(1)}, bf16[2,6,12,192]{3,0,2,1:T(2,128)(2,1)}, u32[]{:S(2)}) copy-start(bf16[2,6,12,192]{3,0,2,1:T(2,128)(2,1)} %param.8) | copy-start | bytes 165892
  0.9 14.7 %copy-start.4 = (bf16[2,1,6,3312]{3,0,2,1:T(2,128)(2,1)S(1)}, bf16[2,1,6,3312]{3,0,2,1:T(2,128)(2,1)}, u32[]{:S(2)}) copy-start(bf16[2,1,6,3312]{3,0,2,1:T(2,128)(2,1)} %param.12) | copy-start | bytes 238468
  0.9 14.6 %collective-permute-start = (bf16[6,6,2,192]{3,2,1,0:T(2,128)(2,1)S(1)}, bf16[6,6,2,192]{3,2,1,0:T(2,128)(2,1)S(1)}, u32[]{:S(2)}, u32[]{:S(2)}) collective-permute-start(bf16[6,6,2,192]{3,2,1,0:T(2,128)(2,1)S(1)} %half.1), channel_id=1, source_target_pairs={{2,4},{4,2},{6,8},{8,6},{10,12},{12,10},{14,16},{16,14},{18,20},{2... | collective-permute-start | bytes 82952 | tf_op jit(solution)/shard_map/ppermute | solution.py:365
  15.5 10.7 %copy-start.5 = (f32[192]{0:T(256)S(1)}, f32[192]{0:T(256)}, u32[]{:S(2)}) copy-start(f32[192]{0:T(256)} %param.13) | copy-start | bytes 2308
  15.5 10.7 %copy-start.6 = (f32[192]{0:T(256)S(1)}, f32[192]{0:T(256)}, u32[]{:S(2)}) copy-start(f32[192]{0:T(256)} %param.9) | copy-start | bytes 2308
  15.5 14.5 %copy-start.2 = (bf16[192,576]{1,0:T(8,128)(2,1)S(1)}, bf16[192,576]{1,0:T(8,128)(2,1)}, u32[]{:S(2)}) copy-start(bf16[192,576]{1,0:T(8,128)(2,1)} %qkv_ref.3) | copy-start | bytes 663556
  15.5 14.5 %copy-start.3 = (bf16[192,192]{1,0:T(8,128)(2,1)S(1)}, bf16[192,192]{1,0:T(8,128)(2,1)}, u32[]{:S(2)}) copy-start(bf16[192,192]{1,0:T(8,128)(2,1)} %proj_ref.3) | copy-start | bytes 221188
  16.2 10.0 %collective-permute-start.1 = (bf16[166,256]{1,0:T(8,128)(2,1)S(1)}, bf16[166,256]{1,0:T(8,128)(2,1)S(1)}, u32[]{:S(2)}, u32[]{:S(2)}) collective-permute-start(bf16[166,256]{1,0:T(8,128)(2,1)S(1)} %get-tuple-element.23), channel_id=1, source_target_pairs={{64,128},{128,64},{192,256},{256,192},{320,384},{384,320},{448,0},... | collective-permute-start | bytes 254984 | tf_op jit(solution)/shard_map/ppermute | solution.py:365
  20.9 9.2 %copy-start = (bf16[192,768]{1,0:T(8,128)(2,1)S(1)}, bf16[192,768]{1,0:T(8,128)(2,1)}, u32[]{:S(2)}) copy-start(bf16[192,768]{1,0:T(8,128)(2,1)} %fc1_ref.3) | copy-start | bytes 884740
  20.9 9.2 %copy-start.1 = (bf16[768,192]{0,1:T(8,128)(2,1)S(1)}, bf16[768,192]{0,1:T(8,128)(2,1)}, u32[]{:S(2)}) copy-start(bf16[768,192]{0,1:T(8,128)(2,1)} %param.15) | copy-start | bytes 884740
  26.6 6.6 %collective-permute-start.2 = (bf16[216,256]{1,0:T(8,128)(2,1)S(1)}, bf16[216,256]{1,0:T(8,128)(2,1)S(1)}, u32[]{:S(2)}, u32[]{:S(2)}) collective-permute-start(bf16[216,256]{1,0:T(8,128)(2,1)S(1)} %get-tuple-element.26), channel_id=1, source_target_pairs={{0,1},{1,0},{2,3},{3,2},{4,5},{5,4},{6,7},{7,6},{8,9},{9,8},{10,11... | collective-permute-start | bytes 331784 | tf_op jit(solution)/shard_map/ppermute | solution.py:365

commit v7 on v5

--- a/solution.py
+++ b/solution.py
@@ -149,12 +149,12 @@
 
 
 def assemble_kernel(
-    far_ref, both_ref, wide_ref, gain_ref, gain2_ref, gain2_out, alone_ref, pair_ref, table_ref, sent_ref
+    near_ref, both_ref, wide_ref, gain_ref, gain2_ref, gain2_out, alone_ref, pair_ref, table_ref, sent_ref
 ):
     lev = lax.axis_index("lev")
     lat_odd = lax.axis_index("lat") % 2
-    near = both_ref[1 - lat_odd].astype(jnp.float32)
-    far = far_ref[...].astype(jnp.float32)
+    near = near_ref[...].astype(jnp.float32)
+    far = both_ref[lat_odd].astype(jnp.float32)
     wide = wide_ref[...].astype(jnp.float32)
     before = jnp.where(lat_odd == 0, far, near)
     after = jnp.where(lat_odd == 0, near, far)
@@ -392,8 +392,8 @@
         held(joint),
         held(tables_t),
     )
-    lat_far = swapped(sent_far, "lat", True)
-    lat_both = lax.all_gather(sent_near, "lat", axis_index_groups=pairs_of(lat_size, False))
+    lat_near = swapped(sent_near, "lat", False)
+    lat_both = lax.all_gather(sent_far, "lat", axis_index_groups=pairs_of(lat_size, True))
     gain1 = held(norm1_gain.reshape(1, D))
     level = pltpu.VMEM((ROWS, D), jnp.bfloat16)
     gain2, alone_cells, pair_cells, upper, sent = pl.pallas_call(
@@ -409,7 +409,7 @@
         out_specs=[whole] * 5,
         compiler_params=params,
         name="assemble",
-    )(held(lat_far), held(lat_both), wide, gain1, held(norm2_gain.reshape(1, D)))
+    )(held(lat_near), held(lat_both), wide, gain1, held(norm2_gain.reshape(1, D)))
     other = swapped(sent, "lev", False)
 
     shared = (

time: 36.2 us -> 35.8 us (0.989)
  the two profiles are of different devices: /device:TPU:64 before, /device:TPU:56 now
where the time goes in v7:
time: 35.8 us; the launch traced here: 35.6 us
  starting transfers between devices  20 us (56%)
  blocking collectives  8.62 us (24%)
  Pallas kernels  6.56 us (18%)
    ppermute x3, starting transfers between devices, swapped(): return lax.ppermute(block, axis, route)  20 us
    all_gather x1, blocking collectives, per_device(): lax.all_gather(sent_far, 'lat', axis_index_groups=pairs_of(lat_size, True))  6.5 us
    pallas_call x1, Pallas kernels, per_device(): pl.pallas_call(late_kernel, out_shape=jax.ShapeDtypeStruct((72, 2, D), jn...  2.82 us
    pallas_call x1, Pallas kernels, per_device(): pl.pallas_call(early_kernel, out_shape=passed, in_specs=[whole] * (6 + le...  2.74 us
    all_gather x1, blocking collectives, per_device(): lax.all_gather(cells_t, 'lon', axis_index_groups=pairs_of(lon_size, False...  2.12 us
  transfers between devices with their start and end apart: 3, of which 1 were waited for; matrix products, arithmetic and copies ran while one was open for 0% of the time, Pallas kernels for 8%

profile of v7, /device:TPU:56, one launch (start us, length us, event | category | flops | bytes accessed | tf_op | source)
XLA Modules:
  0.0 35.6 jit_solution(1493693221171949461)
XLA Ops:
  0.0 0.0 copy-start.4
  0.0 12.7 %collective-permute-start = (bf16[6,12,2,192]{3,2,1,0:T(2,128)(2,1)}, bf16[6,12,2,192]{3,2,1,0:T(2,128)(2,1)S(1)}, u32[]{:S(2)}, u32[]{:S(2)}) collective-permute-start(bf16[6,12,2,192]{3,2,1,0:T(2,128)(2,1)} %bitcast.18), channel_id=1, source_target_pairs={{2,4},{4,2},{6,8},{8,6},{10,12},{12,10},{14,16},{16,14},{18,20},{2... | collective-permute-start | bytes 165896 | tf_op jit(solution)/shard_map/ppermute | solution.py:358
  12.7 2.1 %all_gather.9.joint_ref = bf16[6,24,2,192]{3,2,1,0:T(2,128)(2,1)S(1)} all-gather(bf16[6,12,2,192]{3,2,1,0:T(2,128)(2,1)} %bitcast.19), channel_id=1, replica_groups={{0,2},{4,6},{8,10},{12,14},{16,18},{20,22},{24,26},{28,30},{32,34},{36,..., dimensions={1}, use_global_device_ids=true | all-gather | bytes 165888 | tf_op jit(solution)/shard_map/all_gather | solution.py:371
  14.8 0.2 collective-permute-done.far_ref
  15.0 0.0 copy-done.4
  15.0 0.0 copy-start.5
  15.0 0.0 copy-start.6
  15.0 0.0 copy-start.2
  15.0 0.0 copy-start.3
  15.0 0.6 %pack.1 = (bf16[288,192]{1,0:T(8,128)(2,1)S(1)}, bf16[54,138]{1,0:T(8,128)(2,1)S(1)}, bf16[166,256]{1,0:T(8,128)(2,1)S(1)}, bf16[166,256]{1,0:T(8,128)(2,1)S(1)}) custom-call(bf16[6,12,2,192]{3,2,1,0:T(2,128)(2,1)S(1)} %collective-permute-done.far_ref, bf16[6,24,2,192]{3,2,1,0:T(2,128)(2,1)S(1)} %all_gather.9.joint_ref, bf16[6,2,3312]{2,1,0:T(2,128)(2,1)S(1)} %bitcast.14), custom_call_target="tpu_custom_call" | custom-call | tf_op jit(solution)/shard_map/pack/pallas_call | solution.py:378
  15.7 3.3 %collective-permute-start.1 = (bf16[166,256]{1,0:T(8,128)(2,1)S(1)}, bf16[166,256]{1,0:T(8,128)(2,1)S(1)}, u32[]{:S(2)}, u32[]{:S(2)}) collective-permute-start(bf16[166,256]{1,0:T(8,128)(2,1)S(1)} %get-tuple-element.23), channel_id=1, source_target_pairs={{0,64},{64,0},{128,192},{192,128},{256,320},{320,256},{384,448},{4... | collective-permute-start | bytes 254984 | tf_op jit(solution)/shard_map/ppermute | solution.py:358
  19.0 0.0 copy-start
  19.0 0.0 copy-start.1
  19.0 6.5 %all-gather.1.both_ref = bf16[2,166,256]{2,1,0:T(8,128)(2,1)S(1)} all-gather(bf16[1,166,256]{2,1,0:T(8,128)(2,1)S(1)} %bitcast.13), channel_id=2, replica_groups={{64,128},{192,256},{320,384},{448,0},{65,129},{193,257},{321,385},{449,..., dimensions={0}, use_global_device_ids=true | all-gather | bytes 254976 | tf_op jit(solution)/shard_map/all_gather | solution.py:396
  25.5 0.0 collective-permute-done.1.near_ref
  25.5 0.0 copy-done.5
  25.5 0.0 copy-done.6
  25.5 0.4 %assemble.1 = (f32[1,192]{1,0:T(1,128)S(1)}, bf16[288,192]{1,0:T(8,128)(2,1)S(1)}, bf16[288,192]{1,0:T(8,128)(2,1)S(1)}, bf16[54,138]{1,0:T(8,128)(2,1)S(1)}, bf16[216,256]{1,0:T(8,128)(2,1)S(1)}) custom-call(bf16[166,256]{1,0:T(8,128)(2,1)S(1)} %collective-permute-done.1.near_ref, bf16[2,166,256]{2,1,0:T(8,128)(2,1)S(1)} %all-gather.1.both_ref, ...), custom_call_target="tpu_custom_call" | custom-call | tf_op jit(solution)/shard_map/assemble/pallas_call | solution.py:399
  25.9 4.1 %collective-permute-start.2 = (bf16[216,256]{1,0:T(8,128)(2,1)S(1)}, bf16[216,256]{1,0:T(8,128)(2,1)S(1)}, u32[]{:S(2)}, u32[]{:S(2)}) collective-permute-start(bf16[216,256]{1,0:T(8,128)(2,1)S(1)} %get-tuple-element.26), channel_id=1, source_target_pairs={{0,1},{1,0},{2,3},{3,2},{4,5},{5,4},{6,7},{7,6},{8,9},{9,8},{10,11... | collective-permute-start | bytes 331784 | tf_op jit(solution)/shard_map/ppermute | solution.py:358
  29.9 0.0 copy-done.2
  30.0 0.0 copy-done.3
  30.0 0.0 copy-done
  30.0 0.0 copy-done.1
  30.0 2.7 %early.1 = (f32[144,192]{1,0:T(8,128)S(1)}, f32[72,192]{1,0:T(8,128)S(1)}, bf16[2,216,192]{2,1,0:T(8,128)(2,1)S(1)}, bf16[2,144,192]{2,1,0:T(8,128)(2,1)S(1)}, f...) custom-call(bf16[288,192]{1,0:T(8,128)(2,1)S(1)} %get-tuple-element., ...), custom_call_target="tpu_custom_call" | custom-call | flops 4000000000 | tf_op jit(solution)/shard_map/early/pallas_call | solution.py:434
  32.7 0.0 collective-permute-done.2.other_ref
  32.7 2.8 %late.1 = bf16[72,2,192]{2,1,0:T(2,128)(2,1)} custom-call(bf16[216,256]{1,0:T(8,128)(2,1)S(1)} %collective-permute-done.2.other_ref, f32[144,192]{1,0:T(8,128)S(1)} %get-tuple-element.32.alone_ref, f32[72,192]{1,0:T(8,128)S(1)} %get-tuple-element.33.own_ref, bf16[2,216,192]{2,1,0:T(8,128)(2,1)S(1)} %get-tuple-element.34.asked_ref, ...), custom_call_target="tpu_custom_call" | custom-call | tf_op jit(solution)/shard_map/late/pallas_call | solution.py:443
Async XLA Ops:
  0.0 15.0 %copy-start.4 = (bf16[2,1,6,3312]{3,0,2,1:T(2,128)(2,1)S(1)}, bf16[2,1,6,3312]{3,0,2,1:T(2,128)(2,1)}, u32[]{:S(2)}) copy-start(bf16[2,1,6,3312]{3,0,2,1:T(2,128)(2,1)} %param.12) | copy-start | bytes 238468
  0.0 15.0 %collective-permute-start = (bf16[6,12,2,192]{3,2,1,0:T(2,128)(2,1)}, bf16[6,12,2,192]{3,2,1,0:T(2,128)(2,1)S(1)}, u32[]{:S(2)}, u32[]{:S(2)}) collective-permute-start(bf16[6,12,2,192]{3,2,1,0:T(2,128)(2,1)} %bitcast.18), channel_id=1, source_target_pairs={{2,4},{4,2},{6,8},{8,6},{10,12},{12,10},{14,16},{16,14},{18,20},{2... | collective-permute-start | bytes 165896 | tf_op jit(solution)/shard_map/ppermute | solution.py:358
  15.0 10.5 %copy-start.5 = (f32[192]{0:T(256)S(1)}, f32[192]{0:T(256)}, u32[]{:S(2)}) copy-start(f32[192]{0:T(256)} %param.13) | copy-start | bytes 2308
  15.0 10.5 %copy-start.6 = (f32[192]{0:T(256)S(1)}, f32[192]{0:T(256)}, u32[]{:S(2)}) copy-start(f32[192]{0:T(256)} %param.9) | copy-start | bytes 2308
  15.0 14.9 %copy-start.2 = (bf16[192,576]{1,0:T(8,128)(2,1)S(1)}, bf16[192,576]{1,0:T(8,128)(2,1)}, u32[]{:S(2)}) copy-start(bf16[192,576]{1,0:T(8,128)(2,1)} %qkv_ref.3) | copy-start | bytes 663556
  15.0 14.9 %copy-start.3 = (bf16[192,192]{1,0:T(8,128)(2,1)S(1)}, bf16[192,192]{1,0:T(8,128)(2,1)}, u32[]{:S(2)}) copy-start(bf16[192,192]{1,0:T(8,128)(2,1)} %proj_ref.3) | copy-start | bytes 221188
  15.7 9.8 %collective-permute-start.1 = (bf16[166,256]{1,0:T(8,128)(2,1)S(1)}, bf16[166,256]{1,0:T(8,128)(2,1)S(1)}, u32[]{:S(2)}, u32[]{:S(2)}) collective-permute-start(bf16[166,256]{1,0:T(8,128)(2,1)S(1)} %get-tuple-element.23), channel_id=1, source_target_pairs={{0,64},{64,0},{128,192},{192,128},{256,320},{320,256},{384,448},{4... | collective-permute-start | bytes 254984 | tf_op jit(solution)/shard_map/ppermute | solution.py:358
  19.0 11.0 %copy-start = (bf16[192,768]{1,0:T(8,128)(2,1)S(1)}, bf16[192,768]{1,0:T(8,128)(2,1)}, u32[]{:S(2)}) copy-start(bf16[192,768]{1,0:T(8,128)(2,1)} %fc1_ref.3) | copy-start | bytes 884740
  19.0 11.0 %copy-start.1 = (bf16[768,192]{0,1:T(8,128)(2,1)S(1)}, bf16[768,192]{0,1:T(8,128)(2,1)}, u32[]{:S(2)}) copy-start(bf16[768,192]{0,1:T(8,128)(2,1)} %param.15) | copy-start | bytes 884740
  25.9 6.9 %collective-permute-start.2 = (bf16[216,256]{1,0:T(8,128)(2,1)S(1)}, bf16[216,256]{1,0:T(8,128)(2,1)S(1)}, u32[]{:S(2)}, u32[]{:S(2)}) collective-permute-start(bf16[216,256]{1,0:T(8,128)(2,1)S(1)} %get-tuple-element.26), channel_id=1, source_target_pairs={{0,1},{1,0},{2,3},{3,2},{4,5},{5,4},{6,7},{7,6},{8,9},{9,8},{10,11... | collective-permute-start | bytes 331784 | tf_op jit(solution)/shard_map/ppermute | solution.py:358

commit v8 on v6

--- a/solution.py
+++ b/solution.py
@@ -156,12 +156,12 @@
 
 
 def assemble_kernel(
-    far_ref, both_ref, wide_ref, gain_ref, gain2_ref, gain2_out, alone_ref, pair_ref, table_ref, sent_ref
+    near_ref, both_ref, wide_ref, gain_ref, gain2_ref, gain2_out, alone_ref, pair_ref, table_ref, sent_ref
 ):
     lev = lax.axis_index("lev")
     lat_odd = lax.axis_index("lat") % 2
-    near = both_ref[1 - lat_odd].astype(jnp.float32)
-    far = far_ref[...].astype(jnp.float32)
+    near = near_ref[...].astype(jnp.float32)
+    far = both_ref[lat_odd].astype(jnp.float32)
     wide = wide_ref[...].astype(jnp.float32)
     before = jnp.where(lat_odd == 0, far, near)
     after = jnp.where(lat_odd == 0, near, far)
@@ -408,8 +408,8 @@
         held(joint),
         held(tables_t),
     )
-    lat_far = swapped(sent_far, "lat", True)
-    lat_both = lax.all_gather(sent_near, "lat", axis_index_groups=pairs_of(lat_size, False))
+    lat_near = swapped(sent_near, "lat", False)
+    lat_both = lax.all_gather(sent_far, "lat", axis_index_groups=pairs_of(lat_size, True))
     gain1 = held(norm1_gain.reshape(1, D))
     level = pltpu.VMEM((ROWS, D), jnp.bfloat16)
     gain2, alone_cells, pair_cells, upper, sent = pl.pallas_call(
@@ -425,7 +425,7 @@
         out_specs=[whole] * 5,
         compiler_params=params,
         name="assemble",
-    )(held(lat_far), held(lat_both), wide, gain1, held(norm2_gain.reshape(1, D)))
+    )(held(lat_near), held(lat_both), wide, gain1, held(norm2_gain.reshape(1, D)))
     other = swapped(sent, "lev", False)
 
     shared = (

time: 36.3 us -> 36.1 us (level)
  the two profiles are of different devices: /device:TPU:24 before, /device:TPU:56 now
where the time goes in v8:
time: 36.1 us; the launch traced here: 35.8 us
  starting transfers between devices  19.4 us (54%)
  blocking collectives  8.41 us (23%)
  Pallas kernels  7.39 us (20%)
  waiting for transfers between devices  0.41 us (1%)
    ppermute x3, starting transfers between devices, swapped(): return lax.ppermute(block, axis, route)  19.4 us
    all_gather x1, blocking collectives, per_device(): lax.all_gather(sent_far, 'lat', axis_index_groups=pairs_of(lat_size, True))  6.5 us
    pallas_call x1, Pallas kernels, per_device(): pl.pallas_call(late_kernel, out_shape=jax.ShapeDtypeStruct((72, 2, D), jn...  2.82 us
    pallas_call x1, Pallas kernels, per_device(): pl.pallas_call(early_kernel, out_shape=passed, in_specs=[whole] * (6 + le...  2.73 us
    all_gather x1, blocking collectives, per_device(): lax.all_gather(cells_t, 'lon', axis_index_groups=pairs_of(lon_size, False...  1.91 us
    pallas_call x1, Pallas kernels, per_device(): pl.pallas_call(half_kernel, out_shape=pltpu.VMEM((WLA, HLO, 2, D), jnp.bf...  0.85 us
  transfers between devices with their start and end apart: 3, of which 1 were waited for; matrix products, arithmetic and copies ran while one was open for 0% of the time, Pallas kernels for 8%

profile of v8, /device:TPU:56, one launch (start us, length us, event | category | flops | bytes accessed | tf_op | source)
XLA Modules:
  0.0 35.8 jit_solution(9434638833354737604)
XLA Ops:
  0.0 0.0 copy-start.7
  0.0 0.8 %half.1 = bf16[6,6,2,192]{3,2,1,0:T(2,128)(2,1)S(1)} custom-call(bf16[6,12,2,192]{3,2,1,0:T(2,128)(2,1)} %bitcast.18), custom_call_target="tpu_custom_call" | custom-call | tf_op jit(solution)/shard_map/half/pallas_call | solution.py:377
  0.9 0.0 copy-start.4
  0.9 12.7 %collective-permute-start = (bf16[6,6,2,192]{3,2,1,0:T(2,128)(2,1)S(1)}, bf16[6,6,2,192]{3,2,1,0:T(2,128)(2,1)S(1)}, u32[]{:S(2)}, u32[]{:S(2)}) collective-permute-start(bf16[6,6,2,192]{3,2,1,0:T(2,128)(2,1)S(1)} %half.1), channel_id=1, source_target_pairs={{2,4},{4,2},{6,8},{8,6},{10,12},{12,10},{14,16},{16,14},{18,20},{2... | collective-permute-start | bytes 82952 | tf_op jit(solution)/shard_map/ppermute | solution.py:365
  13.6 0.0 copy-done.7
  13.6 1.9 %all_gather.9.joint_ref = bf16[6,24,2,192]{3,2,1,0:T(2,128)(2,1)S(1)} all-gather(bf16[6,12,2,192]{3,2,1,0:T(2,128)(2,1)S(1)} %bitcast.19), channel_id=1, replica_groups={{0,2},{4,6},{8,10},{12,14},{16,18},{20,22},{24,26},{28,30},{32,34},{36,..., dimensions={1}, use_global_device_ids=true | all-gather | bytes 165888 | tf_op jit(solution)/shard_map/all_gather | solution.py:387
  15.5 0.0 collective-permute-done.far_ref
  15.5 0.0 copy-done.4
  15.5 0.0 copy-start.5
  15.5 0.0 copy-start.6
  15.5 0.0 copy-start.2
  15.5 0.0 copy-start.3
  15.6 0.6 %pack.1 = (bf16[288,192]{1,0:T(8,128)(2,1)S(1)}, bf16[54,138]{1,0:T(8,128)(2,1)S(1)}, bf16[166,256]{1,0:T(8,128)(2,1)S(1)}, bf16[166,256]{1,0:T(8,128)(2,1)S(1)}) custom-call(bf16[6,6,2,192]{3,2,1,0:T(2,128)(2,1)S(1)} %collective-permute-done.far_ref, bf16[6,24,2,192]{3,2,1,0:T(2,128)(2,1)S(1)} %all_gather.9.joint_ref, bf16[6,2,3312]{2,1,0:T(2,128)(2,1)S(1)} %bitcast.14), custom_call_target="tpu_custom_call" | custom-call | tf_op jit(solution)/shard_map/pack/pallas_call | solution.py:394
  16.2 3.3 %collective-permute-start.1 = (bf16[166,256]{1,0:T(8,128)(2,1)S(1)}, bf16[166,256]{1,0:T(8,128)(2,1)S(1)}, u32[]{:S(2)}, u32[]{:S(2)}) collective-permute-start(bf16[166,256]{1,0:T(8,128)(2,1)S(1)} %get-tuple-element.23), channel_id=1, source_target_pairs={{0,64},{64,0},{128,192},{192,128},{256,320},{320,256},{384,448},{4... | collective-permute-start | bytes 254984 | tf_op jit(solution)/shard_map/ppermute | solution.py:365
  19.4 0.0 copy-start
  19.5 0.0 copy-start.1
  19.5 6.5 %all-gather.1.both_ref = bf16[2,166,256]{2,1,0:T(8,128)(2,1)S(1)} all-gather(bf16[1,166,256]{2,1,0:T(8,128)(2,1)S(1)} %bitcast.13), channel_id=2, replica_groups={{64,128},{192,256},{320,384},{448,0},{65,129},{193,257},{321,385},{449,..., dimensions={0}, use_global_device_ids=true | all-gather | bytes 254976 | tf_op jit(solution)/shard_map/all_gather | solution.py:412
  26.0 0.0 collective-permute-done.1.near_ref
  26.0 0.0 copy-done.5
  26.0 0.0 copy-done.6
  26.0 0.4 %assemble.1 = (f32[1,192]{1,0:T(1,128)S(1)}, bf16[288,192]{1,0:T(8,128)(2,1)S(1)}, bf16[288,192]{1,0:T(8,128)(2,1)S(1)}, bf16[54,138]{1,0:T(8,128)(2,1)S(1)}, bf16[216,256]{1,0:T(8,128)(2,1)S(1)}) custom-call(bf16[166,256]{1,0:T(8,128)(2,1)S(1)} %collective-permute-done.1.near_ref, bf16[2,166,256]{2,1,0:T(8,128)(2,1)S(1)} %all-gather.1.both_ref, ...), custom_call_target="tpu_custom_call" | custom-call | tf_op jit(solution)/shard_map/assemble/pallas_call | solution.py:415
  26.3 3.5 %collective-permute-start.2 = (bf16[216,256]{1,0:T(8,128)(2,1)S(1)}, bf16[216,256]{1,0:T(8,128)(2,1)S(1)}, u32[]{:S(2)}, u32[]{:S(2)}) collective-permute-start(bf16[216,256]{1,0:T(8,128)(2,1)S(1)} %get-tuple-element.26), channel_id=1, source_target_pairs={{0,1},{1,0},{2,3},{3,2},{4,5},{5,4},{6,7},{7,6},{8,9},{9,8},{10,11... | collective-permute-start | bytes 331784 | tf_op jit(solution)/shard_map/ppermute | solution.py:365
  29.8 0.0 copy-done.2
  29.8 0.0 copy-done.3
  29.8 0.0 copy-done
  29.8 0.0 copy-done.1
  29.8 2.7 %early.1 = (f32[144,192]{1,0:T(8,128)S(1)}, f32[72,192]{1,0:T(8,128)S(1)}, bf16[2,216,192]{2,1,0:T(8,128)(2,1)S(1)}, bf16[2,144,192]{2,1,0:T(8,128)(2,1)S(1)}, f...) custom-call(bf16[288,192]{1,0:T(8,128)(2,1)S(1)} %get-tuple-element., ...), custom_call_target="tpu_custom_call" | custom-call | flops 4000000000 | tf_op jit(solution)/shard_map/early/pallas_call | solution.py:450
  32.6 0.4 %collective-permute-done.2.other_ref = bf16[216,256]{1,0:T(8,128)(2,1)S(1)} collective-permute-done((bf16[216,256]{1,0:T(8,128)(2,1)S(1)}, bf16[216,256]{1,0:T(8,128)(2,1)S(1)}, u32[]{:S(2)}, u32[]{:S(2)}) %collective-permute-start.2) | collective-permute-done | bytes 110624 | tf_op jit(solution)/shard_map/ppermute | solution.py:365
  33.0 2.8 %late.1 = bf16[72,2,192]{2,1,0:T(2,128)(2,1)} custom-call(bf16[216,256]{1,0:T(8,128)(2,1)S(1)} %collective-permute-done.2.other_ref, f32[144,192]{1,0:T(8,128)S(1)} %get-tuple-element.32.alone_ref, f32[72,192]{1,0:T(8,128)S(1)} %get-tuple-element.33.own_ref, bf16[2,216,192]{2,1,0:T(8,128)(2,1)S(1)} %get-tuple-element.34.asked_ref, ...), custom_call_target="tpu_custom_call" | custom-call | tf_op jit(solution)/shard_map/late/pallas_call | solution.py:459
Async XLA Ops:
  0.0 13.6 %copy-start.7 = (bf16[2,6,12,192]{3,0,2,1:T(2,128)(2,1)S(1)}, bf16[2,6,12,192]{3,0,2,1:T(2,128)(2,1)}, u32[]{:S(2)}) copy-start(bf16[2,6,12,192]{3,0,2,1:T(2,128)(2,1)} %param.8) | copy-start | bytes 165892
  0.9 14.7 %copy-start.4 = (bf16[2,1,6,3312]{3,0,2,1:T(2,128)(2,1)S(1)}, bf16[2,1,6,3312]{3,0,2,1:T(2,128)(2,1)}, u32[]{:S(2)}) copy-start(bf16[2,1,6,3312]{3,0,2,1:T(2,128)(2,1)} %param.12) | copy-start | bytes 238468
  0.9 14.6 %collective-permute-start = (bf16[6,6,2,192]{3,2,1,0:T(2,128)(2,1)S(1)}, bf16[6,6,2,192]{3,2,1,0:T(2,128)(2,1)S(1)}, u32[]{:S(2)}, u32[]{:S(2)}) collective-permute-start(bf16[6,6,2,192]{3,2,1,0:T(2,128)(2,1)S(1)} %half.1), channel_id=1, source_target_pairs={{2,4},{4,2},{6,8},{8,6},{10,12},{12,10},{14,16},{16,14},{18,20},{2... | collective-permute-start | bytes 82952 | tf_op jit(solution)/shard_map/ppermute | solution.py:365
  15.5 10.5 %copy-start.5 = (f32[192]{0:T(256)S(1)}, f32[192]{0:T(256)}, u32[]{:S(2)}) copy-start(f32[192]{0:T(256)} %param.13) | copy-start | bytes 2308
  15.5 10.5 %copy-start.6 = (f32[192]{0:T(256)S(1)}, f32[192]{0:T(256)}, u32[]{:S(2)}) copy-start(f32[192]{0:T(256)} %param.9) | copy-start | bytes 2308
  15.5 14.3 %copy-start.2 = (bf16[192,576]{1,0:T(8,128)(2,1)S(1)}, bf16[192,576]{1,0:T(8,128)(2,1)}, u32[]{:S(2)}) copy-start(bf16[192,576]{1,0:T(8,128)(2,1)} %qkv_ref.3) | copy-start | bytes 663556
  15.5 14.3 %copy-start.3 = (bf16[192,192]{1,0:T(8,128)(2,1)S(1)}, bf16[192,192]{1,0:T(8,128)(2,1)}, u32[]{:S(2)}) copy-start(bf16[192,192]{1,0:T(8,128)(2,1)} %proj_ref.3) | copy-start | bytes 221188
  16.2 9.8 %collective-permute-start.1 = (bf16[166,256]{1,0:T(8,128)(2,1)S(1)}, bf16[166,256]{1,0:T(8,128)(2,1)S(1)}, u32[]{:S(2)}, u32[]{:S(2)}) collective-permute-start(bf16[166,256]{1,0:T(8,128)(2,1)S(1)} %get-tuple-element.23), channel_id=1, source_target_pairs={{0,64},{64,0},{128,192},{192,128},{256,320},{320,256},{384,448},{4... | collective-permute-start | bytes 254984 | tf_op jit(solution)/shard_map/ppermute | solution.py:365
  19.4 10.4 %copy-start = (bf16[192,768]{1,0:T(8,128)(2,1)S(1)}, bf16[192,768]{1,0:T(8,128)(2,1)}, u32[]{:S(2)}) copy-start(bf16[192,768]{1,0:T(8,128)(2,1)} %fc1_ref.3) | copy-start | bytes 884740
  19.5 10.4 %copy-start.1 = (bf16[768,192]{0,1:T(8,128)(2,1)S(1)}, bf16[768,192]{0,1:T(8,128)(2,1)}, u32[]{:S(2)}) copy-start(bf16[768,192]{0,1:T(8,128)(2,1)} %param.15) | copy-start | bytes 884740
  26.3 6.6 %collective-permute-start.2 = (bf16[216,256]{1,0:T(8,128)(2,1)S(1)}, bf16[216,256]{1,0:T(8,128)(2,1)S(1)}, u32[]{:S(2)}, u32[]{:S(2)}) collective-permute-start(bf16[216,256]{1,0:T(8,128)(2,1)S(1)} %get-tuple-element.26), channel_id=1, source_target_pairs={{0,1},{1,0},{2,3},{3,2},{4,5},{5,4},{6,7},{7,6},{8,9},{9,8},{10,11... | collective-permute-start | bytes 331784 | tf_op jit(solution)/shard_map/ppermute | solution.py:365
